TPU v7x, 32 devices: a whole 2x2x4 slice. The times are simulated.
32 devices in a mesh: dp: 4 (over z), expert: 8 (over y, x, core).
Axes of the slice: x: 2, y: 2, z: 4, core: 2. Of those that a mesh axis runs over, the one named last changes fastest.
Arguments:
- block_in: float32 [25216, 768], P(('dp', 'expert')), may hold values from -6 to 6
- out_grad: float32 [25216, 768], P(('dp', 'expert')), may hold values from -6 to 6
- expert_ids: int32 [25216, 2], P(('dp', 'expert')), may hold values from 0 to 15, as said below
- slot_ids: int32 [25216, 2], P(('dp', 'expert')), may hold values from -1 to 110, as said below
- qkv_weight: bfloat16 [768, 2304], P('dp'), may hold values from -0.21875 to 0.21875
- q_bias: bfloat16 [768], P('dp'), may hold values from -3 to 3
- v_bias: bfloat16 [768], P('dp'), may hold values from -3 to 3
- out_weight: bfloat16 [768, 768], P('dp'), may hold values from -0.875 to 0.875
- out_bias: bfloat16 [768], P('dp'), may hold values from -2 to 2
- norm1_gain: bfloat16 [768], P('dp'), may hold values from 0.5 to 1.5
- norm1_bias: bfloat16 [768], P('dp'), may hold values from -2 to 2
- norm2_gain: bfloat16 [768], P('dp'), may hold values from 0.5 to 1.5
- norm2_bias: bfloat16 [768], P('dp'), may hold values from -2 to 2
- router_weight: bfloat16 [768, 16], P('dp'), may hold values from -0.4375 to 0.4375
- up_weight: bfloat16 [16, 768, 3072], P('expert'), may hold values from -0.21875 to 0.21875
- up_bias: bfloat16 [16, 3072], P('expert'), may hold values from -3 to 3
- down_weight: bfloat16 [16, 3072, 768], P('expert'), may hold values from -2.5 to 2.5
- down_bias: bfloat16 [16, 768], P('expert'), may hold values from -10 to 10
Outputs:
- block_out: float32 [25216, 768], P(('dp', 'expert'))
- input_grad: float32 [25216, 768], P(('dp', 'expert'))
- qkv_weight_grad: float32 [768, 2304], P(('dp', 'expert'))
- q_bias_grad: float32 [768], P(('dp', 'expert'))
- v_bias_grad: float32 [768], P(('dp', 'expert'))
- out_weight_grad: float32 [768, 768], P(('dp', 'expert'))
- out_bias_grad: float32 [768], P(('dp', 'expert'))
- norm1_gain_grad: float32 [768], P(('dp', 'expert'))
- norm1_bias_grad: float32 [768], P(('dp', 'expert'))
- norm2_gain_grad: float32 [768], P(('dp', 'expert'))
- norm2_bias_grad: float32 [768], P(('dp', 'expert'))
- router_weight_grad: float32 [768, 16], P(('dp', 'expert'))
- up_weight_grad: float32 [16, 768, 3072], P('expert', 'dp')
- up_bias_grad: float32 [16, 3072], P('expert', 'dp')
- down_weight_grad: float32 [16, 3072, 768], P('expert', 'dp')
- down_bias_grad: float32 [16, 768], P('expert', 'dp')
Inputs may be any that keep to these rules, and one draw needn't show every extreme that they name: `expert_ids`: the two experts of a token differ. `slot_ids`: within each block of 788 rows (the rows of one device), a choice's slot is its rank among the choices of that block naming the same expert, in a priority order where all first choices come before all second choices (the order among tokens is drawn); ranks of 111 or more are dropped and marked -1. Slots of one block and expert are distinct, and some expert fills all 111 slots in every block.
All inputs are finite; a program needn't handle non-finite values.
Results may differ from a plain program's by a relative error of at most 0.023.
Values may be sent and summed in bfloat16 or wider, within the bound.
A program may use at most 256 MiB of HBM per device.

v0:
```python
import jax
import jax.numpy as jnp
from jax import lax
from jax.sharding import PartitionSpec as P

HEADS = 12
HEAD = 64
SEQ = 197


epsilon = 1e-06
inv_root_two = 0.7071067811865476
inv_root_two_pi = 0.3989422804014327


def layer_norm(values, gain, shift):
    centred = values - jnp.mean(values, axis=-1, keepdims=True)
    variance = jnp.mean(centred * centred, axis=-1, keepdims=True)
    inv_std = lax.rsqrt(variance + epsilon)
    normed = centred * inv_std
    return (normed * gain.astype(jnp.float32) + shift.astype(jnp.float32), normed, inv_std)


def norm_backward(cotangent, normed, inv_std, gain):
    scaled = cotangent * gain.astype(jnp.float32)
    centred = (
        scaled
        - jnp.mean(scaled, axis=-1, keepdims=True)
        - normed * jnp.mean(scaled * normed, axis=-1, keepdims=True)
    )
    return (centred * inv_std, jnp.sum(cotangent * normed, axis=0), jnp.sum(cotangent, axis=0))


def gelu_value(pre_act):
    return 0.5 * pre_act * (1.0 + jax.scipy.special.erf(pre_act * inv_root_two))


def gelu_slope(pre_act):
    cumulative = 0.5 * (1.0 + jax.scipy.special.erf(pre_act * inv_root_two))
    return cumulative + pre_act * jnp.exp(-0.5 * pre_act * pre_act) * inv_root_two_pi


def place_rows(pairs, flat_index, slot_total):
    model_width = pairs.shape[-1]
    empty = jnp.zeros((slot_total, model_width), pairs.dtype)
    return empty.at[flat_index.reshape(-1)].set(pairs.reshape(-1, model_width), mode="drop")


def gate_lookup(router_probs, chosen):
    labels = jnp.arange(router_probs.shape[1], dtype=jnp.int32)
    one_hot = (chosen[:, :, None] == labels[None, None, :]).astype(jnp.float32)
    return (jnp.sum(router_probs[:, None, :] * one_hot, axis=-1), one_hot)


def expert_hidden(row_block, up_weight, up_bias):
    pre_act = jnp.einsum("nxcd,xdf->nxcf", row_block, up_weight, preferred_element_type=jnp.float32)
    pre_act = pre_act + up_bias.astype(jnp.float32)[None, :, None, :]
    return (pre_act, gelu_value(pre_act).astype(jnp.bfloat16))


def expert_output(active, down_weight, down_bias):
    produced = jnp.einsum("nxcf,xfd->nxcd", active, down_weight, preferred_element_type=jnp.float32)
    return (produced + down_bias.astype(jnp.float32)[None, :, None, :]).astype(jnp.bfloat16)


def local(
    block_in,
    out_grad,
    expert_ids,
    slot_ids,
    qkv_weight,
    q_bias,
    v_bias,
    out_weight,
    out_bias,
    norm1_gain,
    norm1_bias,
    norm2_gain,
    norm2_bias,
    router_weight,
    up_weight,
    up_bias,
    down_weight,
    down_bias,
):
    dense_full = (
        lax.all_gather(qkv_weight, "dp", axis=0, tiled=True),
        lax.all_gather(q_bias, "dp", axis=0, tiled=True),
        lax.all_gather(v_bias, "dp", axis=0, tiled=True),
        lax.all_gather(out_weight, "dp", axis=0, tiled=True),
        lax.all_gather(out_bias, "dp", axis=0, tiled=True),
        lax.all_gather(norm1_gain, "dp", axis=0, tiled=True),
        lax.all_gather(norm1_bias, "dp", axis=0, tiled=True),
        lax.all_gather(norm2_gain, "dp", axis=0, tiled=True),
        lax.all_gather(norm2_bias, "dp", axis=0, tiled=True),
        lax.all_gather(router_weight, "dp", axis=0, tiled=True),
    )
    (
        qkv_full,
        q_shift,
        v_shift,
        out_full,
        out_shift,
        gain_one,
        shift_one,
        gain_two,
        shift_two,
        router_full,
    ) = dense_full
    tok_rows = block_in.shape[0]
    model_width = block_in.shape[1]
    images = tok_rows // SEQ
    experts = router_full.shape[1]
    capacity = tok_rows * 2 * 9 // (8 * experts) + 1
    groups = lax.axis_size("expert")
    per_owner = up_weight.shape[0]
    head_scale = HEAD ** (-0.5)
    normed_in, normed_one, inv_one = layer_norm(block_in, gain_one, shift_one)
    first_in = normed_in.astype(jnp.bfloat16)
    projected = jnp.dot(first_in, qkv_full, preferred_element_type=jnp.float32)
    queries = (
        (projected[:, :model_width] + q_shift.astype(jnp.float32))
        .astype(jnp.bfloat16)
        .reshape(images, SEQ, HEADS, HEAD)
    )
    key_heads = (
        projected[:, model_width : 2 * model_width]
        .astype(jnp.bfloat16)
        .reshape(images, SEQ, HEADS, HEAD)
    )
    value_heads = (
        (projected[:, 2 * model_width :] + v_shift.astype(jnp.float32))
        .astype(jnp.bfloat16)
        .reshape(images, SEQ, HEADS, HEAD)
    )
    scores = (
        jnp.einsum("bqhd,bkhd->bhqk", queries, key_heads, preferred_element_type=jnp.float32)
        * head_scale
    )
    exp_scores = jnp.exp(scores)
    score_total = jnp.sum(exp_scores, axis=-1, keepdims=True)
    log_total = jnp.log(score_total)
    attn_weights = (exp_scores / score_total).astype(jnp.bfloat16)
    attended = (
        jnp.einsum("bhqk,bkhd->bqhd", attn_weights, value_heads, preferred_element_type=jnp.float32)
        .astype(jnp.bfloat16)
        .reshape(tok_rows, model_width)
    )
    hidden = (
        block_in
        + jnp.dot(attended, out_full, preferred_element_type=jnp.float32)
        + out_shift.astype(jnp.float32)
    )
    normed_mid, normed_two, inv_two = layer_norm(hidden, gain_two, shift_two)
    second_in = normed_mid.astype(jnp.bfloat16)
    logits = jnp.dot(second_in, router_full, preferred_element_type=jnp.float32)
    router_exp = jnp.exp(logits)
    router_probs = router_exp / jnp.sum(router_exp, axis=-1, keepdims=True)
    gate_values, one_hot = gate_lookup(router_probs, expert_ids)
    flat_index = jnp.where(slot_ids >= 0, expert_ids * capacity + slot_ids, experts * capacity)
    pairs = jnp.broadcast_to(second_in[:, None, :], (tok_rows, 2, model_width))
    send_rows = place_rows(pairs, flat_index, experts * capacity).reshape(
        groups, per_owner, capacity, model_width
    )
    pre_act, active = expert_hidden(
        lax.all_to_all(send_rows, "expert", split_axis=0, concat_axis=0, tiled=True),
        up_weight,
        up_bias,
    )
    outs_back = lax.all_to_all(
        expert_output(active, down_weight, down_bias),
        "expert",
        split_axis=0,
        concat_axis=0,
        tiled=True,
    ).reshape(experts * capacity, model_width)
    gathered_out = jnp.take(outs_back, flat_index, axis=0, mode="fill", fill_value=0).astype(
        jnp.float32
    )
    block_out = hidden + jnp.sum(gate_values[:, :, None] * gathered_out, axis=1)
    d_gates = jnp.sum(out_grad[:, None, :] * gathered_out, axis=-1)
    scaled = (gate_values[:, :, None] * out_grad[:, None, :]).astype(jnp.bfloat16)
    grad_send = place_rows(scaled, flat_index, experts * capacity).reshape(
        groups, per_owner, capacity, model_width
    )
    grad_recv, row_recv = (
        lax.all_to_all(grad_send, "expert", split_axis=0, concat_axis=0, tiled=True),
        lax.all_to_all(send_rows, "expert", split_axis=0, concat_axis=0, tiled=True),
    )
    pre_act, active = expert_hidden(row_recv, up_weight, up_bias)
    down_grad = jnp.einsum("nxcf,nxcd->xfd", active, grad_recv, preferred_element_type=jnp.float32)
    down_shift_grad = jnp.sum(grad_recv.astype(jnp.float32), axis=(0, 2))
    d_pre = jnp.einsum(
        "nxcd,xfd->nxcf", grad_recv, down_weight, preferred_element_type=jnp.float32
    ) * gelu_slope(pre_act)
    d_pre_b = d_pre.astype(jnp.bfloat16)
    up_grad = jnp.einsum("nxcd,nxcf->xdf", row_recv, d_pre_b, preferred_element_type=jnp.float32)
    up_shift_grad = jnp.sum(d_pre, axis=(0, 2))
    d_rows = jnp.einsum(
        "nxcf,xdf->nxcd", d_pre_b, up_weight, preferred_element_type=jnp.float32
    ).astype(jnp.bfloat16)
    rows_back = lax.all_to_all(d_rows, "expert", split_axis=0, concat_axis=0, tiled=True).reshape(
        experts * capacity, model_width
    )
    expert_sums = (
        lax.psum_scatter(
            up_grad.astype(jnp.bfloat16), "dp", scatter_dimension=1, tiled=True
        ).astype(jnp.float32),
        lax.psum_scatter(
            up_shift_grad.astype(jnp.bfloat16), "dp", scatter_dimension=1, tiled=True
        ).astype(jnp.float32),
        lax.psum_scatter(
            down_grad.astype(jnp.bfloat16), "dp", scatter_dimension=1, tiled=True
        ).astype(jnp.float32),
        lax.psum_scatter(
            down_shift_grad.astype(jnp.bfloat16), "dp", scatter_dimension=1, tiled=True
        ).astype(jnp.float32),
    )
    again = (
        lax.all_gather(qkv_weight, "dp", axis=0, tiled=True),
        lax.all_gather(out_weight, "dp", axis=0, tiled=True),
        lax.all_gather(norm1_gain, "dp", axis=0, tiled=True),
        lax.all_gather(norm2_gain, "dp", axis=0, tiled=True),
        lax.all_gather(router_weight, "dp", axis=0, tiled=True),
    )
    qkv_back, out_back, gain_one_back, gain_two_back, router_back = again
    d_probs = jnp.sum(d_gates[:, :, None] * one_hot, axis=1)
    d_logits = (
        router_probs * (d_probs - jnp.sum(router_probs * d_probs, axis=-1, keepdims=True))
    ).astype(jnp.bfloat16)
    router_grad = jnp.dot(second_in.T, d_logits, preferred_element_type=jnp.float32)
    row_grads = jnp.take(rows_back, flat_index, axis=0, mode="fill", fill_value=0).astype(
        jnp.float32
    )
    d_second = jnp.dot(d_logits, router_back.T, preferred_element_type=jnp.float32) + jnp.sum(
        row_grads, axis=1
    )
    d_mid, gain_two_grad, shift_two_grad = norm_backward(
        d_second, normed_two, inv_two, gain_two_back
    )
    d_hidden = out_grad + d_mid
    out_shift_grad = jnp.sum(d_hidden, axis=0)
    d_hidden_b = d_hidden.astype(jnp.bfloat16)
    out_weight_grad = jnp.dot(attended.T, d_hidden_b, preferred_element_type=jnp.float32)
    d_attended = (
        jnp.dot(d_hidden_b, out_back.T, preferred_element_type=jnp.float32)
        .astype(jnp.bfloat16)
        .reshape(images, SEQ, HEADS, HEAD)
    )
    scores_again = (
        jnp.einsum("bqhd,bkhd->bhqk", queries, key_heads, preferred_element_type=jnp.float32)
        * head_scale
    )
    attn_again = jnp.exp(scores_again - log_total)
    attn_again_b = attn_again.astype(jnp.bfloat16)
    d_values = jnp.einsum(
        "bhqk,bqhd->bkhd", attn_again_b, d_attended, preferred_element_type=jnp.float32
    )
    d_att = jnp.einsum(
        "bqhd,bkhd->bhqk", d_attended, value_heads, preferred_element_type=jnp.float32
    )
    d_scores = (
        attn_again * (d_att - jnp.sum(attn_again * d_att, axis=-1, keepdims=True)) * head_scale
    ).astype(jnp.bfloat16)
    d_queries = jnp.einsum(
        "bhqk,bkhd->bqhd", d_scores, key_heads, preferred_element_type=jnp.float32
    )
    d_keys = jnp.einsum("bhqk,bqhd->bkhd", d_scores, queries, preferred_element_type=jnp.float32)
    q_shift_grad = jnp.sum(d_queries, axis=(0, 1)).reshape(model_width)
    v_shift_grad = jnp.sum(d_values, axis=(0, 1)).reshape(model_width)
    d_projected = jnp.concatenate(
        [
            d_queries.reshape(tok_rows, model_width),
            d_keys.reshape(tok_rows, model_width),
            d_values.reshape(tok_rows, model_width),
        ],
        axis=1,
    ).astype(jnp.bfloat16)
    qkv_grad = jnp.dot(first_in.T, d_projected, preferred_element_type=jnp.float32)
    d_first = jnp.dot(d_projected, qkv_back.T, preferred_element_type=jnp.float32)
    d_input, gain_one_grad, shift_one_grad = norm_backward(
        d_first, normed_one, inv_one, gain_one_back
    )
    input_grad = d_hidden + d_input
    dense_sums = (
        lax.psum_scatter(qkv_grad, ("dp", "expert"), scatter_dimension=0, tiled=True),
        lax.psum_scatter(q_shift_grad, ("dp", "expert"), scatter_dimension=0, tiled=True),
        lax.psum_scatter(v_shift_grad, ("dp", "expert"), scatter_dimension=0, tiled=True),
        lax.psum_scatter(out_weight_grad, ("dp", "expert"), scatter_dimension=0, tiled=True),
        lax.psum_scatter(out_shift_grad, ("dp", "expert"), scatter_dimension=0, tiled=True),
        lax.psum_scatter(gain_one_grad, ("dp", "expert"), scatter_dimension=0, tiled=True),
        lax.psum_scatter(shift_one_grad, ("dp", "expert"), scatter_dimension=0, tiled=True),
        lax.psum_scatter(gain_two_grad, ("dp", "expert"), scatter_dimension=0, tiled=True),
        lax.psum_scatter(shift_two_grad, ("dp", "expert"), scatter_dimension=0, tiled=True),
        lax.psum_scatter(router_grad, ("dp", "expert"), scatter_dimension=0, tiled=True),
    )
    return (
        block_out,
        input_grad,
        dense_sums[0],
        dense_sums[1],
        dense_sums[2],
        dense_sums[3],
        dense_sums[4],
        dense_sums[5],
        dense_sums[6],
        dense_sums[7],
        dense_sums[8],
        dense_sums[9],
        expert_sums[0],
        expert_sums[1],
        expert_sums[2],
        expert_sums[3],
    )


def solution(mesh):
    in_specs = (
        P(("dp", "expert"), None),
        P(("dp", "expert"), None),
        P(("dp", "expert"), None),
        P(("dp", "expert"), None),
        P("dp", None),
        P("dp"),
        P("dp"),
        P("dp", None),
        P("dp"),
        P("dp"),
        P("dp"),
        P("dp"),
        P("dp"),
        P("dp", None),
        P("expert", None, None),
        P("expert", None),
        P("expert", None, None),
        P("expert", None),
    )
    out_specs = (
        P(("dp", "expert"), None),
        P(("dp", "expert"), None),
        P(("dp", "expert"), None),
        P(("dp", "expert")),
        P(("dp", "expert")),
        P(("dp", "expert"), None),
        P(("dp", "expert")),
        P(("dp", "expert")),
        P(("dp", "expert")),
        P(("dp", "expert")),
        P(("dp", "expert")),
        P(("dp", "expert"), None),
        P("expert", "dp", None),
        P("expert", "dp"),
        P("expert", "dp", None),
        P("expert", "dp"),
    )
    return jax.shard_map(local, mesh=mesh, in_specs=in_specs, out_specs=out_specs, check_vma=False)
```

profile of v0, /device:TPU:0, one launch (start us, length us, event | category | flops | bytes accessed | tf_op | source)
XLA Modules:
  0.0 1198.4 jit_solution(12337913423758448502)
XLA Ops:
  16.5 21.9 %all-reduce.16 = (bf16[768]{0:T(1024)(128)(2,1)S(1)}, bf16[768]{0:T(1024)(128)(2,1)S(1)}, bf16[768]{0:T(1024)(128)(2,1)S(1)}, bf16[768]{0:T(1024)(128)(2,1)S(1)}...) all-reduce(bf16[768]{0:T(1024)(128)(2,1)S(1)} %dynamic-update-slice, ...), channel_id=1, replica_groups=mesh['dp'=4,'expert'=8] {'dp'}, use_global_device_ids=true, to_apply=%add.1 | all-reduce | flops 5376 | bytes 21504
  41.4 41.3 %all-gather.4.cloned.1.call-done = bf16[768,2304]{1,0:T(8,128)(2,1)} async-done(((bf16[192,2304]{1,0:T(8,128)(2,1)}), bf16[768,2304]{1,0:T(8,128)(2,1)}) %all-gather.4.cloned.1.call-update) | async-done | bytes 3538960 | tf_op jit(solution)/shard_map/all_gather | solution.py:87
  143.9 13.0 %scatter_custom_fusion = bf16[1776,768]{1,0:T(8,128)(2,1)} fusion(s32[1576]{0:T(1024)S(1)} %fusion.67, bf16[1576,768]{1,0:T(8,128)(2,1)} %reshape.219, bf16[]{:T(256)} %constant.19.clone.1), kind=kCustom, calls=%fused_computation.90 | custom fusion | bytes 2728448 | tf_op jit(solution)/shard_map/scatter | solution.py:46
  167.7 13.1 %all-gather = bf16[4,192,16]{1,2,0:T(8,128)(2,1)S(1)} all-gather(bf16[1,192,16]{1,2,0:T(8,128)(2,1)S(1)} %bitcast.110), channel_id=1, replica_groups=mesh['dp'=4,'expert'=8] {'dp'}, dimensions={0}, use_global_device_ids=true | all-gather | bytes 30720 | tf_op jit(solution)/shard_map/all_gather | solution.py:96
  193.0 19.3 %scatter_custom_fusion.1 = bf16[1776,768]{1,0:T(8,128)(2,1)} fusion(s32[1576]{0:T(1024)S(1)} %fusion.67, f32[1576,768]{1,0:T(8,128)} %mul.228, f32[1576]{0:T(1024)S(1)} %mul.226, bf16[]{:T(256)} %constant.19.clone.1), kind=kCustom, calls=%fused_computation.77 | custom fusion | flops 2420736 | bytes 7577602 | tf_op jit(solution)/shard_map/scatter | solution.py:46
  222.4 18.1 %fusion.7 = (bf16[8,2,111,3072]{3,2,0,1:T(8,128)(2,1)}, f32[2,8,111,3072]{3,2,1,0:T(8,128)}) fusion(f32[2,3072]{1,0:T(2,128)S(1)} %convert_element_type.135, bf16[2,768,3072]{2,1,0:T(8,128)(2,1)} %param.34, bf16[8,2,111,768]{3,1,2,0:T(2,128)(2,1)} %all-to-all-done), kind=kOutput, calls=%fused_computation.14 | convolution fusion | flops 8412954624 | bytes 44924928 | tf_op jit(solution)/shard_map/nxcd,xdf->nxcf/dot_general | solution.py:56
  240.4 15.3 %all-to-all-done.2 = bf16[8,2,111,768]{3,1,2,0:T(2,128)(2,1)S(1)} async-done(((bf16[8,2,111,768]{3,1,2,0:T(2,128)(2,1)}), bf16[8,2,111,768]{3,1,2,0:T(2,128)(2,1)S(1)}, u32[]{:S(2)}, u32[]{:S(2)}) %all-to-all-start.2) | async-done | bytes 2727968 | tf_op jit(solution)/shard_map/all_to_all | solution.py:187
  255.8 21.9 %fusion.83 = (bf16[2,3072]{1,0:T(2,128)(2,1)S(1)}, bf16[8,2,111,3072]{3,2,0,1:T(8,128)(2,1)}) fusion(f32[2,8,111,3072]{3,2,1,0:T(8,128)} %get-tuple-element.55, f32[2,3072]{1,0:T(2,128)S(1)} %convert_element_type.135, bf16[2,3072,768]{2,1,0:T(8,128)(2,1)} %param.36, bf16[8,2,111,768]{3,1,2,0:T(2,128)(2,1)S(1)} %all-to-all-done.2), kind=kOutput, calls=%fused_computation.131 | convolution fusion | flops 8445683712 | bytes 44937216 | tf_op jit(solution)/shard_map/nxcd,xfd->nxcf/dot_general | solution.py:193
  277.6 14.5 %convert_bitcast_fusion = bf16[8,2,111,768]{3,2,0,1:T(8,128)(2,1)S(1)} fusion(bf16[2,768,3072]{2,1,0:T(8,128)(2,1)} %param.34, bf16[8,2,111,3072]{3,2,0,1:T(8,128)(2,1)} %get-tuple-element.65), kind=kOutput, calls=%fused_computation.56 | convolution fusion | flops 8381583360 | bytes 23076864 | tf_op jit(solution)/shard_map/nxcf,xdf->nxcd/dot_general | solution.py:199
  300.9 14.2 %fusion.38 = bf16[8,2,111,768]{3,2,0,1:T(8,128)(2,1)S(1)} fusion(f32[2,768]{1,0:T(2,128)S(1)} %convert_element_type.137, bf16[8,2,111,3072]{3,2,0,1:T(8,128)(2,1)} %get-tuple-element.54, bf16[2,3072,768]{2,1,0:T(8,128)(2,1)} %param.36), kind=kOutput, calls=%fused_computation.55 | convolution fusion | flops 8382947328 | bytes 23083008 | tf_op jit(solution)/shard_map/nxcf,xfd->nxcd/dot_general | solution.py:62
  319.5 14.8 %all-to-all-done.3 = bf16[8,2,111,768]{3,1,2,0:T(2,128)(2,1)} async-done(((bf16[8,2,111,768]{3,1,2,0:T(2,128)(2,1)}), bf16[8,2,111,768]{3,1,2,0:T(2,128)(2,1)}, u32[]{:S(2)}, u32[]{:S(2)}) %all-to-all-start.3) | async-done | bytes 2727968 | tf_op jit(solution)/shard_map/all_to_all | solution.py:202
  364.4 7.7 all-to-all-done.1
  390.2 22.7 %fusion.37 = (f32[788,2]{1,0:T(8,128)}, f32[788,768]{1,0:T(8,128)}, f32[788,768]{1,0:T(8,128)}) fusion(f32[788,768]{1,0:T(8,128)} %param.21, bf16[788,2,768]{2,1,0:T(2,128)(2,1)} %reshape.275, pred[788,2]{1,0:T(8,128)(4,1)S(1)} %copy.168, f32[788,2]{1,0:T(8,128)S(1)} %copy.167, bf16[788,2,768]{2,1,0:T(2,128)(2,1)} %reshape.279), kind=kLoop, calls=%fused_computation.46 | loop fusion | flops 9681368 | bytes 12117864 | tf_op jit(solution)/shard_map/reduce_sum | solution.py:181
  436.5 8.0 bitcast_convert_fusion.2
  444.6 18.1 %fusion.58 = bf16[4,197,12,64]{1,3,2,0:T(8,128)(2,1)} fusion(bf16[4,197,12,64]{1,3,2,0:T(8,128)(2,1)S(1)} %copy-done.14, f32[4,12,197,197]{2,3,1,0:T(8,128)} %fusion.84, f32[4,12,197]{2,1,0:T(8,128)S(1)} %log.8, f32[4,12,197,197]{2,3,1,0:T(8,128)} %copy-done), kind=kOutput, calls=%fused_computation.88 | convolution fusion | flops 255822816 | bytes 17361216 | tf_op jit(solution)/shard_map/bhqk,bqhd->bkhd/dot_general | solution.py:268
  462.7 18.1 %bitcast_convert_fusion.3 = (bf16[4,197,12,64]{1,3,2,0:T(8,128)(2,1)}, f32[4,12,64,197]{3,2,1,0:T(8,128)}) fusion(bf16[4,197,12,64]{1,3,2,0:T(8,128)(2,1)} %copy.162, f32[4,12,197,197]{2,3,1,0:T(8,128)} %fusion.84, f32[4,12,197]{2,1,0:T(8,128)S(1)} %log.8, f32[4,12,197,197]{2,3,1,0:T(8,128)} %copy-done), kind=kOutput, calls=%fused_computation.54 | convolution fusion | flops 255822816 | bytes 19781952 | tf_op jit(solution)/shard_map/bhqk,bkhd->bqhd/dot_general | solution.py:265
  509.1 16.7 %bitcast_convert_fusion = bf16[2,3072,768]{2,1,0:T(8,128)(2,1)} fusion(bf16[8,2,111,3072]{3,2,0,1:T(8,128)(2,1)} %get-tuple-element.54, bf16[8,2,111,768]{3,1,2,0:T(2,128)(2,1)} %copy-done.11), kind=kOutput, calls=%fused_computation.17 | convolution fusion | flops 8384937984 | bytes 23076864 | tf_op jit(solution)/shard_map/nxcf,nxcd->xfd/dot_general | solution.py:191
  525.9 16.3 %bitcast_convert_fusion.1 = bf16[2,768,3072]{2,1,0:T(8,128)(2,1)} fusion(bf16[8,2,111,3072]{3,2,0,1:T(8,128)(2,1)} %get-tuple-element.65, bf16[8,2,111,768]{3,1,2,0:T(2,128)(2,1)} %all-to-all-done), kind=kOutput, calls=%fused_computation.18 | convolution fusion | flops 8384937984 | bytes 23076864 | tf_op jit(solution)/shard_map/nxcd,nxcf->xdf/dot_general | solution.py:197
  547.3 8.9 fusion.76
  563.4 66.8 %all-reduce.19.cloned.1.call-done = (f32[768]{0:T(1024)}, f32[768]{0:T(1024)}, f32[768]{0:T(1024)}, f32[768]{0:T(1024)}, f32[768]{0:T(1024)}, /*index=5*/f32[768]{0:T(1024)}, f32[768]{0:T(1024)}, f32[768,16]{0,1:T(8,128)}) async-done(((f32[768]{0:T(1024)}, f32[768]{0:T(1024)}, f32[768]{0:T(1024)}, f32[768]{0:T(1024)}, f32[768]{0:T(1024)}, /*index=5*/f32[768]{0:T(1024)}, f32[768]{0:T(1024)}, ...) | async-done | bytes 70672
  640.4 155.4 %reduce-scatter.18.cloned.1.call-done = bf16[2,768,768]{2,1,0:T(8,128)(2,1)} async-done(((bf16[2,3072,768]{2,1,0:T(8,128)(2,1)}), bf16[2,768,768]{2,1,0:T(8,128)(2,1)}) %reduce-scatter.18.cloned.1.call-update) | async-done | bytes 2359312 | tf_op jit(solution)/shard_map/reduce_scatter | solution.py:212
  800.1 160.3 %reduce-scatter.16.cloned.1.call-done = bf16[2,192,3072]{2,1,0:T(8,128)(2,1)} async-done(((bf16[2,768,3072]{2,1,0:T(8,128)(2,1)}), bf16[2,192,3072]{2,1,0:T(8,128)(2,1)}) %reduce-scatter.16.cloned.1.call-update) | async-done | bytes 2359312 | tf_op jit(solution)/shard_map/reduce_scatter | solution.py:206
  964.8 102.1 %reduce-scatter.14.cloned.1.call-done = f32[24,768]{1,0:T(8,128)} async-done(((f32[768,768]{1,0:T(8,128)}), f32[24,768]{1,0:T(8,128)}) %reduce-scatter.14.cloned.1.call-update) | async-done | bytes 73744 | tf_op jit(solution)/shard_map/reduce_scatter | solution.py:289
  1066.9 124.8 %reduce-scatter.12.cloned.1.call-done = f32[24,2304]{1,0:T(8,128)} async-done(((f32[768,2304]{1,0:T(8,128)}), f32[24,2304]{1,0:T(8,128)}) %reduce-scatter.12.cloned.1.call-update) | async-done | bytes 221200 | tf_op jit(solution)/shard_map/reduce_scatter | solution.py:286
  (230 shorter events, 249.6 us)
Async XLA Ops:
  7.2 33.1 %copy-start.3 = (f32[788,768]{1,0:T(8,128)S(1)}, f32[788,768]{1,0:T(8,128)}, u32[]{:S(2)}) copy-start(f32[788,768]{1,0:T(8,128)} %param.20) | copy-start | bytes 7262212
  7.2 75.5 %all-gather.4.cloned.1.call-start = ((), (), s32[]{:S(2)}) async-start(), calls=%async_computation.10 | async-start | bytes 4423680 | tf_op jit(solution)/shard_map/all_gather | solution.py:87
  7.9 32.9 %copy-start.23 = (s32[788,2]{0,1:T(2,128)S(1)}, s32[788,2]{0,1:T(2,128)}, u32[]{:S(2)}) copy-start(s32[788,2]{0,1:T(2,128)} %param.22) | copy-start | bytes 18916
  7.9 32.9 %copy-start.32 = (s32[788,2]{0,1:T(2,128)S(1)}, s32[788,2]{0,1:T(2,128)}, u32[]{:S(2)}) copy-start(s32[788,2]{0,1:T(2,128)} %param.23) | copy-start | bytes 18916
  7.9 126.5 %all-gather.6.cloned.1.call-start = ((), (), s32[]{:S(2)}) async-start(), calls=%async_computation.11 | async-start | bytes 1474560 | tf_op jit(solution)/shard_map/all_gather | solution.py:90
  38.4 44.3 %copy-start.26 = (f32[768]{0:T(1024)}, f32[768]{0:T(1024)S(1)}, u32[]{:S(2)}) copy-start(f32[768]{0:T(1024)S(1)} %convert_element_type.121) | copy-start | bytes 9220
  38.4 44.3 %copy-start.33 = (f32[768]{0:T(1024)}, f32[768]{0:T(1024)S(1)}, u32[]{:S(2)}) copy-start(f32[768]{0:T(1024)S(1)} %convert_element_type.122) | copy-start | bytes 9220
  40.3 47.5 %copy-start.24 = (f32[788]{0:T(1024)}, f32[788]{0:T(1024)S(1)}, u32[]{:S(2)}) copy-start(f32[788]{0:T(1024)S(1)} %broadcast_multiply_fusion.5) | copy-start | bytes 9460
  40.8 47.1 %copy-start.28 = (f32[788]{0:T(1024)}, f32[788]{0:T(1024)S(1)}, u32[]{:S(2)}) copy-start(f32[788]{0:T(1024)S(1)} %add_rsqrt_fusion.1) | copy-start | bytes 9460
  163.1 55.2 %all-to-all-start = ((bf16[8,2,111,768]{3,1,2,0:T(2,128)(2,1)}), bf16[8,2,111,768]{3,1,2,0:T(2,128)(2,1)}, u32[]{:S(2)}, u32[]{:S(2)}) async-start(bf16[8,2,111,768]{3,1,2,0:T(2,128)(2,1)} %copy.170), calls=%async_computation | async-start | bytes 5455872 | tf_op jit(solution)/shard_map/all_to_all | solution.py:166
  218.3 37.5 %all-to-all-start.2 = ((bf16[8,2,111,768]{3,1,2,0:T(2,128)(2,1)}), bf16[8,2,111,768]{3,1,2,0:T(2,128)(2,1)S(1)}, u32[]{:S(2)}, u32[]{:S(2)}) async-start(bf16[8,2,111,768]{3,1,2,0:T(2,128)(2,1)} %copy.178), calls=%async_computation.2 | async-start | bytes 5455872 | tf_op jit(solution)/shard_map/all_to_all | solution.py:187
  255.8 85.2 %copy-start.11 = (bf16[8,2,111,768]{3,1,2,0:T(2,128)(2,1)}, bf16[8,2,111,768]{3,1,2,0:T(2,128)(2,1)S(1)}, u32[]{:S(2)}) copy-start(bf16[8,2,111,768]{3,1,2,0:T(2,128)(2,1)S(1)} %all-to-all-done.2) | copy-start | bytes 8183812
  296.5 37.8 %all-to-all-start.3 = ((bf16[8,2,111,768]{3,1,2,0:T(2,128)(2,1)}), bf16[8,2,111,768]{3,1,2,0:T(2,128)(2,1)}, u32[]{:S(2)}, u32[]{:S(2)}) async-start(bf16[8,2,111,768]{3,1,2,0:T(2,128)(2,1)} %copy.180), calls=%async_computation.3 | async-start | bytes 5455872 | tf_op jit(solution)/shard_map/all_to_all | solution.py:202
  334.3 37.8 %all-to-all-start.1 = ((bf16[8,2,111,768]{3,1,2,0:T(2,128)(2,1)}), bf16[8,2,111,768]{3,1,2,0:T(2,128)(2,1)}, u32[]{:S(2)}, u32[]{:S(2)}) async-start(bf16[8,2,111,768]{3,1,2,0:T(2,128)(2,1)} %copy.172), calls=%async_computation.1 | async-start | bytes 5455872 | tf_op jit(solution)/shard_map/all_to_all | solution.py:170
  338.7 217.6 %reduce-scatter.22.cloned.1.call-start = ((), (), s32[]{:S(2)}) async-start(), calls=%async_computation.17 | async-start | bytes 245760
  344.2 213.6 %reduce-scatter.20.cloned.1.call-start = ((), (), s32[]{:S(2)}) async-start(), calls=%async_computation.16 | async-start | bytes 983040
  345.8 284.4 %all-reduce.19.cloned.1.call-start = ((), (), s32[]{:S(2)}) async-start(), calls=%async_computation.18 | async-start | bytes 155648
  390.2 24.0 %copy-start.2 = (f32[788,768]{1,0:T(8,128)S(1)}, f32[788,768]{1,0:T(8,128)}, u32[]{:S(2)}) copy-start(f32[788,768]{1,0:T(8,128)} %copy-done.1) | copy-start | bytes 7262212
  462.7 18.1 %copy-start.9 = (bf16[788,768]{1,0:T(8,128)(2,1)S(1)}, bf16[788,768]{1,0:T(8,128)(2,1)}, u32[]{:S(2)}) copy-start(bf16[788,768]{1,0:T(8,128)(2,1)} %copy-done.7) | copy-start | bytes 3631108
  462.7 19.0 %copy-start.17 = (bf16[4,197,12,64]{1,3,2,0:T(8,128)(2,1)S(1)}, bf16[4,197,12,64]{1,3,2,0:T(8,128)(2,1)}, u32[]{:S(2)}) copy-start(bf16[4,197,12,64]{1,3,2,0:T(8,128)(2,1)} %get-tuple-element.61) | copy-start | bytes 3631108
  509.0 286.8 %reduce-scatter.18.cloned.1.call-start = ((), (), s32[]{:S(2)}) async-start(), calls=%async_computation.15 | async-start | bytes 11796480 | tf_op jit(solution)/shard_map/reduce_scatter | solution.py:212
  525.8 434.6 %reduce-scatter.16.cloned.1.call-start = ((), (), s32[]{:S(2)}) async-start(), calls=%async_computation.14 | async-start | bytes 11796480 | tf_op jit(solution)/shard_map/reduce_scatter | solution.py:206
  542.2 524.7 %reduce-scatter.14.cloned.1.call-start = ((), (), s32[]{:S(2)}) async-start(), calls=%async_computation.13 | async-start | bytes 2433024 | tf_op jit(solution)/shard_map/reduce_scatter | solution.py:289
  547.3 644.4 %reduce-scatter.12.cloned.1.call-start = ((), (), s32[]{:S(2)}) async-start(), calls=%async_computation.12 | async-start | bytes 7299072 | tf_op jit(solution)/shard_map/reduce_scatter | solution.py:286
  (27 other events, 125.7 us)
Sparse Core Ops, SparseCore 0:
  9.6 73.0 all-gather.3
  84.2 28.8 all-gather.5
  344.3 18.2 reduce-scatter.21
  364.8 21.3 reduce-scatter.19
  509.2 120.9 all-reduce.18
  632.4 163.4 reduce-scatter.17
  798.2 162.1 reduce-scatter.15
  966.2 100.5 reduce-scatter.13
  1073.1 118.5 reduce-scatter.11
where the time goes:
time: 1210 us; the launch traced here: 1200 us
  waiting for transfers between devices  690 us (57%)
  matrix products  192 us (16%)
  local copies, waits for them, and re-layouts  181 us (15%)
  other arithmetic  67 us (6%)
  blocking collectives  35.1 us (3%)
  starting transfers between devices  18.2 us (2%)
  between operations  15.4 us (1%)
    reduce_scatter x1, waiting for transfers between devices, local(): lax.psum_scatter(up_grad.astype(jnp.bfloat16), 'dp', scatter_dimension=1,...  160 us
    reduce_scatter x1, waiting for transfers between devices, local(): lax.psum_scatter(down_grad.astype(jnp.bfloat16), 'dp', scatter_dimension=...  155 us
    reduce_scatter x1, waiting for transfers between devices, local(): lax.psum_scatter(qkv_grad, ('dp', 'expert'), scatter_dimension=0, tiled=T...  125 us
    reduce_scatter x1, waiting for transfers between devices, local(): lax.psum_scatter(out_weight_grad, ('dp', 'expert'), scatter_dimension=0,...  102 us
    unnamed x12, waiting for transfers between devices  68.4 us
    all_gather x1, waiting for transfers between devices, local(): lax.all_gather(qkv_weight, 'dp', axis=0, tiled=True)  41.3 us
    unnamed x106, local copies, waits for them, and re-layouts  30.8 us
  transfers between devices with their start and end apart: 13, of which 9 were waited for; matrix products, arithmetic and copies ran while one was open for 30% of the time, Pallas kernels for 0%

commit v1 on v0

v1 whole, which is shorter than its diff:
```python
import jax
import jax.numpy as jnp
from jax import lax
from jax.sharding import Mesh, PartitionSpec as P

HEADS = 12
HEAD = 64
SEQ = 197

epsilon = 1e-06
inv_root_two = 0.7071067811865476
inv_root_two_pi = 0.3989422804014327

bf16 = jnp.bfloat16
f32 = jnp.float32


def layer_norm(values, gain, shift):
    centred = values - jnp.mean(values, axis=-1, keepdims=True)
    variance = jnp.mean(centred * centred, axis=-1, keepdims=True)
    inv_std = lax.rsqrt(variance + epsilon)
    normed = centred * inv_std
    return (normed * gain + shift, normed, inv_std)


def norm_backward(cotangent, normed, inv_std, gain):
    scaled = cotangent * gain
    centred = (
        scaled
        - jnp.mean(scaled, axis=-1, keepdims=True)
        - normed * jnp.mean(scaled * normed, axis=-1, keepdims=True)
    )
    return (centred * inv_std, jnp.sum(cotangent * normed, axis=0), jnp.sum(cotangent, axis=0))


def gelu_value(pre_act):
    return 0.5 * pre_act * (1.0 + lax.erf(pre_act * inv_root_two))


def gelu_slope(pre_act):
    cumulative = 0.5 * (1.0 + lax.erf(pre_act * inv_root_two))
    return cumulative + pre_act * jnp.exp(-0.5 * pre_act * pre_act) * inv_root_two_pi


def dot(a, b):
    return jnp.dot(a, b, preferred_element_type=f32)


def dot_tn(a, b):
    return lax.dot_general(a, b, (((0,), (0,)), ((), ())), preferred_element_type=f32)


def dot_nt(a, b):
    return lax.dot_general(a, b, (((1,), (1,)), ((), ())), preferred_element_type=f32)


def shift_along(value, axis, step):
    size = lax.axis_size(axis)
    return lax.ppermute(value, axis, [(i, (i + step) % size) for i in range(size)])


def pick(value, index, axis):
    return lax.dynamic_index_in_dim(value, index, axis, keepdims=False)


def expert_grad_sum(total):
    outer, fan = lax.axis_size("hi"), lax.axis_size("lo")
    high, low = lax.axis_index("hi"), lax.axis_index("lo")
    rows, columns = total.shape
    blocks = total.reshape(outer, fan, rows // (outer * fan), columns)
    mine = [None] * fan
    for step in list(range(1, fan)) + [0]:
        piece = pick(blocks, (low + step) % fan, 1)
        summed = pick(piece, high, 0)
        for hop in range(1, outer):
            sent = pick(piece, (high + hop) % outer, 0).astype(bf16)
            summed = summed + shift_along(sent, "hi", hop).astype(f32)
        if step:
            summed = shift_along(summed.astype(bf16), "lo", step).astype(f32)
        mine[step] = summed
    if fan == 2:
        first = jnp.where(low == 0, mine[0], mine[1])
        second = jnp.where(low == 0, mine[1], mine[0])
        return jnp.stack([first, second])
    stacked = jnp.stack(mine)
    return jnp.stack([pick(stacked, (low - k) % fan, 0) for k in range(fan)])


def gather_small(vector):
    names = ("hi", "lo")
    size = lax.axis_size("hi") * lax.axis_size("lo")
    me = lax.axis_index("hi") * lax.axis_size("lo") + lax.axis_index("lo")
    rows = [vector]
    for step in range(1, size):
        rows.append(lax.ppermute(vector, names, [(i, (i + step) % size) for i in range(size)]))
    return jnp.stack(rows), me


def dense_sum(matrix):
    names = ("hi", "lo")
    members = lax.axis_size("hi") * lax.axis_size("lo")
    me = lax.axis_index("hi") * lax.axis_size("lo") + lax.axis_index("lo")
    plane = lax.axis_size("expert")
    spot = lax.axis_index("expert")
    rows, columns = matrix.shape
    piece = rows // (members * plane)
    current = matrix.reshape(members, plane, piece, columns)
    left, bit = plane, 1
    while left > 1:
        halves = current.reshape(members, left // 2, 2, piece, columns)
        side = (spot // bit) % 2
        sent = pick(halves, 1 - side, 2).astype(bf16)
        came = lax.ppermute(sent, "expert", [(i, i ^ bit) for i in range(plane)])
        current = pick(halves, side, 2) + came.astype(f32)
        left //= 2
        bit *= 2
    current = current.reshape(members, piece, columns)
    summed = pick(current, me, 0)
    for step in range(1, members):
        sent = pick(current, (me + step) % members, 0).astype(bf16)
        came = lax.ppermute(sent, names, [(i, (i + step) % members) for i in range(members)])
        summed = summed + came.astype(f32)
    return summed


def local(
    block_in,
    out_grad,
    expert_ids,
    slot_ids,
    qkv_weight,
    q_bias,
    v_bias,
    out_weight,
    out_bias,
    norm1_gain,
    norm1_bias,
    norm2_gain,
    norm2_bias,
    router_weight,
    up_weight,
    up_bias,
    down_weight,
    down_bias,
):
    tok_rows, width = block_in.shape
    images = tok_rows // SEQ
    experts = router_weight.shape[1]
    capacity = tok_rows * 2 * 9 // (8 * experts) + 1
    slots = -(-capacity // 16) * 16
    outer, fan, plane = lax.axis_size("hi"), lax.axis_size("lo"), lax.axis_size("expert")
    members = outer * fan
    low, spot = lax.axis_index("lo"), lax.axis_index("expert")
    me = lax.axis_index("hi") * fan + low
    group = ("lo", "expert")
    hidden_width = up_weight.shape[2]
    head_scale = HEAD ** (-0.5)

    vectors = (q_bias, v_bias, out_bias, norm1_gain, norm1_bias, norm2_gain, norm2_bias)
    packed = jnp.concatenate([qkv_weight, out_weight, router_weight] + [v[:, None] for v in vectors], axis=1)
    part = packed.shape[0] // plane
    packed = lax.dynamic_slice_in_dim(packed, spot * part, part, 0)
    packed = lax.all_gather(packed, ("hi", "lo", "expert"), axis=0, tiled=True)
    qkv_full = packed[:, : 3 * width]
    out_full = packed[:, 3 * width : 4 * width]
    router_full = packed[:, 4 * width : 4 * width + experts]
    rows = packed[:, 4 * width + experts :].T.astype(f32)
    q_shift, v_shift, out_shift, gain_one, shift_one, gain_two, shift_two = [rows[i] for i in range(7)]

    up_one = pick(up_weight, low, 0)
    down_one = pick(down_weight, low, 0)
    up_shift = pick(up_bias, low, 0).astype(f32)
    down_shift = pick(down_bias, low, 0).astype(f32)

    owner = (expert_ids % fan) * plane + expert_ids // fan
    spots = jnp.where(slot_ids >= 0, owner * slots + slot_ids, -1)
    total = experts * slots
    labels = jnp.arange(total, dtype=jnp.int32)
    place = ((labels[:, None] == spots[:, 0][None, :]) | (labels[:, None] == spots[:, 1][None, :])).astype(bf16)

    def exchange(value):
        return lax.all_to_all(value, group, split_axis=0, concat_axis=0, tiled=True)

    cot_rows = exchange(dot(place, out_grad.astype(bf16)).astype(bf16))

    normed_in, normed_one, inv_one = layer_norm(block_in, gain_one, shift_one)
    first_in = normed_in.astype(bf16)
    projected = dot(first_in, qkv_full)
    queries = (projected[:, :width] + q_shift).astype(bf16).reshape(images, SEQ, HEADS, HEAD)
    key_heads = projected[:, width : 2 * width].astype(bf16).reshape(images, SEQ, HEADS, HEAD)
    value_heads = (projected[:, 2 * width :] + v_shift).astype(bf16).reshape(images, SEQ, HEADS, HEAD)
    scores = jnp.einsum("bqhd,bkhd->bhqk", queries, key_heads, preferred_element_type=f32) * head_scale
    exp_scores = jnp.exp(scores)
    score_total = jnp.sum(exp_scores, axis=-1, keepdims=True)
    log_total = jnp.log(score_total)
    attn_weights = (exp_scores / score_total).astype(bf16)
    attended = (
        jnp.einsum("bhqk,bkhd->bqhd", attn_weights, value_heads, preferred_element_type=f32)
        .astype(bf16)
        .reshape(tok_rows, width)
    )
    hidden = block_in + dot(attended, out_full) + out_shift
    normed_mid, normed_two, inv_two = layer_norm(hidden, gain_two, shift_two)
    second_in = normed_mid.astype(bf16)
    logits = dot(second_in, router_full)
    router_exp = jnp.exp(logits)
    router_probs = router_exp / jnp.sum(router_exp, axis=-1, keepdims=True)
    one_hot = (expert_ids[:, :, None] == jnp.arange(experts, dtype=jnp.int32)[None, None, :]).astype(f32)
    gate_values = jnp.sum(router_probs[:, None, :] * one_hot, axis=-1)

    row_recv = exchange(dot(place, second_in).astype(bf16))

    row_exp = jnp.exp(dot(row_recv, router_full))
    mine = (jnp.arange(experts, dtype=jnp.int32) == spot * fan + low).astype(f32)
    row_gate = jnp.sum(row_exp * mine, axis=-1) / jnp.sum(row_exp, axis=-1)
    grad_recv = (row_gate[:, None] * cot_rows.astype(f32)).astype(bf16)
    pre_act = dot(row_recv, up_one) + up_shift
    active = gelu_value(pre_act).astype(bf16)
    down_grad = dot_tn(active, grad_recv)
    down_part = expert_grad_sum(down_grad)
    d_pre = dot_nt(grad_recv, down_one) * gelu_slope(pre_act)
    d_pre_b = d_pre.astype(bf16)
    up_grad = dot_tn(row_recv, d_pre_b)
    up_part = expert_grad_sum(up_grad)
    outs_back = exchange((dot(active, down_one) + down_shift).astype(bf16))
    rows_back = exchange(dot_nt(d_pre_b, up_one).astype(bf16))
    small, me = gather_small(
        jnp.concatenate([jnp.sum(d_pre, axis=0), jnp.sum(grad_recv.astype(f32), axis=0)])
    )
    from_expert = (me - jnp.arange(members)) % fan
    small = jnp.stack([jnp.sum(jnp.where((from_expert == k)[:, None], small, 0.0), axis=0) for k in range(fan)])
    up_shift_part = lax.dynamic_slice_in_dim(
        small[:, :hidden_width], me * (hidden_width // members), hidden_width // members, 1
    )
    down_shift_part = lax.dynamic_slice_in_dim(small[:, hidden_width:], me * (width // members), width // members, 1)

    take0 = (spots[:, 0][:, None] == labels[None, :]).astype(bf16)
    take1 = (spots[:, 1][:, None] == labels[None, :]).astype(bf16)
    got0, got1 = dot(take0, outs_back), dot(take1, outs_back)
    block_out = hidden + gate_values[:, :1] * got0 + gate_values[:, 1:] * got1
    d_gates = jnp.stack([jnp.sum(out_grad * got0, axis=-1), jnp.sum(out_grad * got1, axis=-1)], axis=1)
    d_probs = jnp.sum(d_gates[:, :, None] * one_hot, axis=1)
    d_logits = (router_probs * (d_probs - jnp.sum(router_probs * d_probs, axis=-1, keepdims=True))).astype(bf16)
    router_grad = dot_tn(second_in, d_logits)
    d_second = dot_nt(d_logits, router_full) + dot(take0 + take1, rows_back)
    d_mid, gain_two_grad, shift_two_grad = norm_backward(d_second, normed_two, inv_two, gain_two)
    d_hidden = out_grad + d_mid
    out_shift_grad = jnp.sum(d_hidden, axis=0)
    d_hidden_b = d_hidden.astype(bf16)
    out_weight_grad = dot_tn(attended, d_hidden_b)
    d_attended = dot_nt(d_hidden_b, out_full).astype(bf16).reshape(images, SEQ, HEADS, HEAD)
    scores_again = jnp.einsum("bqhd,bkhd->bhqk", queries, key_heads, preferred_element_type=f32) * head_scale
    attn_again = jnp.exp(scores_again - log_total)
    attn_again_b = attn_again.astype(bf16)
    d_values = jnp.einsum("bhqk,bqhd->bkhd", attn_again_b, d_attended, preferred_element_type=f32)
    d_att = jnp.einsum("bqhd,bkhd->bhqk", d_attended, value_heads, preferred_element_type=f32)
    d_scores = (
        attn_again * (d_att - jnp.sum(attn_again * d_att, axis=-1, keepdims=True)) * head_scale
    ).astype(bf16)
    d_queries = jnp.einsum("bhqk,bkhd->bqhd", d_scores, key_heads, preferred_element_type=f32)
    d_keys = jnp.einsum("bhqk,bqhd->bkhd", d_scores, queries, preferred_element_type=f32)
    q_shift_grad = jnp.sum(d_queries, axis=(0, 1)).reshape(width)
    v_shift_grad = jnp.sum(d_values, axis=(0, 1)).reshape(width)
    d_projected = jnp.concatenate(
        [d.reshape(tok_rows, width) for d in (d_queries, d_keys, d_values)], axis=1
    ).astype(bf16)
    qkv_grad = dot_tn(first_in, d_projected)
    d_first = dot_nt(d_projected, qkv_full)
    d_input, gain_one_grad, shift_one_grad = norm_backward(d_first, normed_one, inv_one, gain_one)
    input_grad = d_hidden + d_input

    columns = (q_shift_grad, v_shift_grad, out_shift_grad, gain_one_grad, shift_one_grad, gain_two_grad, shift_two_grad)
    dense = dense_sum(
        jnp.concatenate([qkv_grad, out_weight_grad, router_grad, jnp.stack(columns, axis=1)], axis=1)
    )
    vec = 4 * width + experts
    return (
        block_out,
        input_grad,
        dense[:, : 3 * width],
        dense[:, vec],
        dense[:, vec + 1],
        dense[:, 3 * width : 4 * width],
        dense[:, vec + 2],
        dense[:, vec + 3],
        dense[:, vec + 4],
        dense[:, vec + 5],
        dense[:, vec + 6],
        dense[:, 4 * width : vec],
        up_part,
        up_shift_part,
        down_part,
        down_shift_part,
    )


def solution(mesh):
    def step(*arrays):
        members, plane = mesh.shape["dp"], mesh.shape["expert"]
        fan = arrays[14].shape[0] // plane
        split = Mesh(mesh.devices.reshape(members // fan, fan, plane), ("hi", "lo", "expert"))
        every, dp = ("hi", "lo", "expert"), ("hi", "lo")
        in_specs = (
            (P(every, None),) * 4
            + (P(dp, None), P(dp), P(dp), P(dp, None), P(dp), P(dp), P(dp), P(dp), P(dp), P(dp, None))
            + (P("expert", None, None), P("expert", None), P("expert", None, None), P("expert", None))
        )
        out_specs = (
            (P(every, None),) * 3
            + (P(every), P(every), P(every, None))
            + (P(every),) * 5
            + (P(every, None), P("expert", dp, None), P("expert", dp), P("expert", dp, None), P("expert", dp))
        )
        return jax.shard_map(local, mesh=split, in_specs=in_specs, out_specs=out_specs, check_vma=False)(*arrays)

    return step
```

time: 1210 us -> 639 us (0.53)
  waiting for transfers between devices: 690 us -> 201 us
  local copies, waits for them, and re-layouts: 181 us -> 136 us
  other arithmetic: 67 us -> 31.1 us
  blocking collectives: 35.1 us -> 0 us
  starting transfers between devices: 18.2 us -> 40.5 us
    reduce_scatter x4 -> x0, waiting for transfers between devices: 543 us -> none  [the longest x1 160 us: local(): lax.psum_scatter(up_grad.astype(jnp.bfloat16), 'dp', scatter_dimension=1,...]
    ppermute x0 -> x15, waiting for transfers between devices: none -> 100 us  [the longest x6 80.9 us: shift_along(): lax.ppermute(value, axis, [(i, (i + step) % size) for i in range(size)])]
    unnamed x12 -> x1, waiting for transfers between devices: 68.4 us -> 0.02 us
    concatenate x1 -> x20, local copies, waits for them, and re-layouts: 0.22 us -> 29 us  [the longest x18 25.6 us: local(): jnp.concatenate([qkv_grad, out_weight_grad, router_grad, jnp.stack(column...]
    all_gather x2 -> x1, waiting for transfers between devices: 41.3 us -> 66.4 us  [local(): packed = lax.all_gather(packed, ('hi', 'lo', 'expert'), axis=0, tiled=True)]
    gather x4 -> x0, local copies, waits for them, and re-layouts: 24.6 us -> none  [the longest x2 12.3 us: local(): jnp.take(rows_back, flat_index, axis=0, mode='fill', fill_value=0)]
    reshape x21 -> x11, local copies, waits for them, and re-layouts: 65.3 us -> 41.9 us  [the longest x2 9.62 us: local(): (projected[:, 2 * width:] + v_shift).astype(bf16)]
    reduce_sum x5 -> x4, other arithmetic: 25.6 us -> 3.68 us  [the longest x1 2.48 us: local(): jnp.sum(grad_recv.astype(f32), axis=0)]
  transfers between devices with their start and end apart: 13 -> 20, of which waited for: 9 -> 10; matrix products, arithmetic and copies ran while one was open for 30% -> 45% of each run, Pallas kernels for 0% -> 0%
where the time goes in v1:
time: 639 us; the launch traced here: 628 us
  matrix products  203 us (32%)
  waiting for transfers between devices  201 us (31%)
  local copies, waits for them, and re-layouts  136 us (21%)
  starting transfers between devices  40.5 us (6%)
  other arithmetic  31.1 us (5%)
  between operations  16.2 us (3%)
    ppermute x6, waiting for transfers between devices, shift_along(): lax.ppermute(value, axis, [(i, (i + step) % size) for i in range(size)])  80.9 us
    dot_general x11, matrix products, dot(): return jnp.dot(a, b, preferred_element_type=f32)  66.7 us
    all_gather x1, waiting for transfers between devices, local(): packed = lax.all_gather(packed, ('hi', 'lo', 'expert'), axis=0, tiled=True)  66.4 us
    dot_general x5, matrix products, dot_nt(): lax.dot_general(a, b, (((1,), (1,)), ((), ())), preferred_element_type=f32)  47 us
    all_to_all x4, waiting for transfers between devices, exchange(): return lax.all_to_all(value, group, split_axis=0, concat_axis=0, tiled=True)  34.5 us
    dot_general x5, matrix products, dot_tn(): lax.dot_general(a, b, (((0,), (0,)), ((), ())), preferred_element_type=f32)  33.9 us
    concatenate x18, local copies, waits for them, and re-layouts, local(): jnp.concatenate([qkv_grad, out_weight_grad, router_grad, jnp.stack(column...  25.6 us
    all_to_all x4, starting transfers between devices, exchange(): return lax.all_to_all(value, group, split_axis=0, concat_axis=0, tiled=True)  20.8 us
  transfers between devices with their start and end apart: 20, of which 10 were waited for; matrix products, arithmetic and copies ran while one was open for 45% of the time, Pallas kernels for 0%

profile of v1, /device:TPU:0, one launch (start us, length us, event | category | flops | bytes accessed | tf_op | source)
XLA Modules:
  0.0 627.9 jit_solution(10328169731311380159)
XLA Ops:
  19.1 66.4 %all-gather.2.cloned.1.call-done = bf16[768,3095]{1,0:T(8,128)(2,1)} async-done(((bf16[24,3095]{1,0:T(8,128)(2,1)}), bf16[768,3095]{1,0:T(8,128)(2,1)}) %all-gather.2.cloned.1.call-update) | async-done | bytes 4753936 | tf_op jit(solution)/shard_map/all_gather | solution.py:163
  88.0 5.2 fusion.63
  153.0 6.5 %fusion.54 = bf16[1792,768]{1,0:T(8,128)(2,1)} fusion(s32[788]{0:T(1024)S(1)} %get-tuple-element.113, s32[788]{0:T(1024)S(1)} %get-tuple-element.112, f32[788,768]{1,0:T(8,128)} %param.19), kind=kOutput, calls=%fused_computation.57 | convolution fusion | flops 2175197184 | bytes 5179552 | tf_op jit(solution)/shard_map/dot_general | solution.py:46
  159.5 31.8 %all-to-all-done = bf16[16,112,768]{2,1,0:T(8,128)(2,1)S(1)} async-done(((bf16[16,112,768]{2,1,0:T(8,128)(2,1)}), bf16[16,112,768]{2,1,0:T(8,128)(2,1)S(1)}, u32[]{:S(2)}, u32[]{:S(2)}) %all-to-all-start) | async-done | bytes 2752544 | tf_op jit(solution)/shard_map/all_to_all | solution.py:182
  191.3 6.6 %all-to-all-start.2 = ((bf16[16,112,768]{2,1,0:T(8,128)(2,1)}), bf16[16,112,768]{2,1,0:T(8,128)(2,1)}, u32[]{:S(2)}, u32[]{:S(2)}) async-start(bf16[16,112,768]{2,1,0:T(8,128)(2,1)} %bitcast.166), calls=%async_computation.2 | async-start | bytes 5505024 | tf_op jit(solution)/shard_map/all_to_all | solution.py:182
  202.5 15.3 %multiply_convert_fusion = (bf16[1792,3072]{1,0:T(8,128)(2,1)S(1)}, f32[1792,3072]{1,0:T(8,128)}) fusion(f32[3072]{0:T(1024)S(1)} %bitcast.176, bf16[1792,768]{1,0:T(8,128)(2,1)S(1)} %bitcast.159, bf16[2,768,3072]{2,1,0:T(8,128)(2,1)} %param.32, s32[]{:T(128)S(6)} %select_n.205), kind=kOutput, calls=%fused_computation.7 | convolution fusion | flops 8488747008 | bytes 40513540 | tf_op jit(solution)/shard_map/dot_general | solution.py:46
  221.9 12.2 %add_convert_fusion = bf16[1792,768]{1,0:T(8,128)(2,1)} fusion(bf16[1792,3072]{1,0:T(8,128)(2,1)S(1)} %get-tuple-element.138, bf16[2,3072,768]{2,1,0:T(8,128)(2,1)} %param.34, s32[]{:T(128)S(6)} %select_n.205, f32[768]{0:T(1024)S(1)} %fusion.119), kind=kOutput, calls=%fused_computation.33 | convolution fusion | flops 8458469376 | bytes 18484228 | tf_op jit(solution)/shard_map/dot_general | solution.py:46
  236.9 6.0 all-to-all-start.1
  245.4 21.3 %fusion.137 = (f32[3072]{0:T(1024)S(1)}, bf16[1792,3072]{1,0:T(8,128)(2,1)}) fusion(f32[1792,3072]{1,0:T(8,128)} %get-tuple-element.139, f32[3072]{0:T(1024)S(1)} %bitcast.177, bf16[1792,768]{1,0:T(8,128)(2,1)S(1)} %bitcast.169, bf16[2,3072,768]{2,1,0:T(8,128)(2,1)} %param.34, s32[]{:T(128)S(6)} %select_n.205), kind=kOutput, calls=%fused_computation.240 | convolution fusion | flops 8521774080 | bytes 40525828 | tf_op jit(solution)/shard_map/dot_general | solution.py:54
  271.2 14.6 %copy.192 = bf16[3072,1792]{1,0:T(8,128)(2,1)} copy(bf16[3072,1792]{0,1:T(8,128)(2,1)} %bitcast.163) | data formatting | bytes 22020096 | tf_op jit(solution)/shard_map/dot_general | solution.py:50
  285.8 14.0 %fusion.46 = bf16[1792,768]{1,0:T(8,128)(2,1)} fusion(bf16[2,768,3072]{2,1,0:T(8,128)(2,1)} %param.32, s32[]{:T(128)S(6)} %select_n.205, bf16[1792,3072]{1,0:T(8,128)(2,1)} %get-tuple-element.148), kind=kOutput, calls=%fused_computation.55 | convolution fusion | flops 8457093120 | bytes 18481156 | tf_op jit(solution)/shard_map/dot_general | solution.py:54
  304.3 14.6 %fusion.140 = f32[2,2,768,768]{3,2,1,0:T(8,128)} fusion(bf16[2,2,768,1792]{3,2,1,0:T(8,128)(2,1)} %bitcast.164, bf16[1792,768,1,1]{1,0,3,2:T(8,128)(2,1)} %bitcast.170), kind=kOutput, calls=%fused_computation.243 | convolution fusion | flops 8455716864 | bytes 23199744 | tf_op jit(solution)/shard_map/dot_general | solution.py:50
  328.7 11.8 %fusion.6 = f32[2,2,192,3072]{3,2,1,0:T(8,128)S(1)} fusion(bf16[2,2,192,1792]{3,2,1,0:T(8,128)(2,1)S(1)} %bitcast.172, bf16[1792,3072]{1,0:T(8,128)(2,1)} %get-tuple-element.148), kind=kOutput, calls=%fused_computation.9 | convolution fusion | flops 8455716864 | bytes 23199744 | tf_op jit(solution)/shard_map/dot_general | solution.py:50
  352.0 6.7 %multiply_reduce_fusion.6 = (f32[788]{0:T(1024)S(1)}, f32[788]{0:T(1024)S(1)}, f32[788,768]{1,0:T(8,128)}) fusion(f32[788,768]{1,0:T(8,128)S(1)} %copy-done.23, f32[788,768]{1,0:T(8,128)S(1)} %fusion.19, bf16[1792,768]{1,0:T(8,128)(2,1)} %bitcast.8, s32[788]{0:T(1024)S(1)} %get-tuple-element.112), kind=kOutput, calls=%fused_computation.95 | convolution fusion | flops 2172810752 | bytes 10024176 | tf_op jit(solution)/shard_map/dot_general | solution.py:46
  381.8 5.3 fusion.138
  387.1 8.0 %bitcast_convert_fusion = (bf16[4,197,12,64]{1,3,2,0:T(8,128)(2,1)}, f32[4,12,64,197]{3,2,1,0:T(8,128)}) fusion(bf16[4,197,12,64]{1,3,2,0:T(8,128)(2,1)S(1)} %copy.159, f32[4,12,197]{2,1,0:T(8,128)S(1)} %copy-done.29, f32[4,12,197,197]{2,3,1,0:T(8,128)} %copy-done), kind=kOutput, calls=%fused_computation.63 | convolution fusion | flops 244636176 | bytes 12330624 | tf_op jit(solution)/shard_map/bhqk,bqhd->bkhd/dot_general | solution.py:255
  395.1 18.1 %fusion.87 = bf16[4,197,12,64]{1,3,2,0:T(8,128)(2,1)} fusion(bf16[4,197,12,64]{1,3,2,0:T(8,128)(2,1)S(1)} %copy-done.12, f32[4,12,197,197]{2,3,1,0:T(8,128)} %fusion.138, f32[4,12,197]{2,1,0:T(8,128)S(1)} %copy-done.29, f32[4,12,197,197]{2,3,1,0:T(8,128)} %copy-done), kind=kOutput, calls=%fused_computation.126 | convolution fusion | flops 255822816 | bytes 17361216 | tf_op jit(solution)/shard_map/bhqk,bqhd->bkhd/dot_general | solution.py:261
  413.2 17.9 %bitcast_convert_fusion.1 = (bf16[4,197,12,64]{1,3,2,0:T(8,128)(2,1)}, f32[4,12,64,197]{3,2,1,0:T(8,128)}) fusion(bf16[4,197,12,64]{1,3,2,0:T(8,128)(2,1)} %copy.154, f32[4,12,197,197]{2,3,1,0:T(8,128)} %fusion.138, f32[4,12,197]{2,1,0:T(8,128)S(1)} %copy-done.29, f32[4,12,197,197]{2,3,1,0:T(8,128)} %copy-done), kind=kOutput, calls=%fused_computation.65 | convolution fusion | flops 255822816 | bytes 19781952 | tf_op jit(solution)/shard_map/bhqk,bkhd->bqhd/dot_general | solution.py:260
  452.7 6.2 multiply_reduce_fusion.2
  473.4 12.3 %concatenate.43 = f32[4,4,2,24,3095]{4,3,1,0,2:T(8,128)} concatenate(f32[4,4,2,24,2304]{4,3,1,0,2:T(8,128)} %copy.170, f32[4,4,2,24,768]{4,3,1,0,2:T(8,128)} %fusion.90, f32[4,4,2,24,16]{4,3,1,0,2:T(8,128)} %copy.172, f32[4,4,2,24,1]{4,3,1,0,2:T(8,128)} %copy.173, f32[4,4,2,24,1]{4,3,1,0,2:T(8,128)} %copy.174, f32[4,4,2,24,1]{4,3,1,0,2:T(8,128)} %copy.175, ...), dimensions={4} | concatenate | bytes 19015680 | tf_op jit(solution)/shard_map/concatenate | solution.py:274
  494.5 13.2 %collective-permute-done.7 = bf16[192,3072]{1,0:T(8,128)(2,1)} collective-permute-done((bf16[192,3072]{1,0:T(8,128)(2,1)}, bf16[192,3072]{1,0:T(8,128)(2,1)}, u32[]{:S(2)}, u32[]{:S(2)}) %collective-permute-start.7) | collective-permute-done | bytes 1179680 | tf_op jit(solution)/shard_map/ppermute | solution.py:59
  510.0 47.3 %collective-permute-done.14 = bf16[768,768]{1,0:T(8,128)(2,1)S(1)} collective-permute-done((bf16[768,768]{1,0:T(8,128)(2,1)S(1)}, bf16[768,768]{1,0:T(8,128)(2,1)S(1)}, u32[]{:S(2)}, u32[]{:S(2)}) %collective-permute-start.14) | collective-permute-done | bytes 1179680 | tf_op jit(solution)/shard_map/ppermute | solution.py:59
  562.1 20.4 %collective-permute-done.8 = bf16[192,3072]{1,0:T(8,128)(2,1)S(1)} collective-permute-done((bf16[192,3072]{1,0:T(8,128)(2,1)S(1)}, bf16[192,3072]{1,0:T(8,128)(2,1)S(1)}, u32[]{:S(2)}, u32[]{:S(2)}) %collective-permute-start.8) | collective-permute-done | bytes 1179680 | tf_op jit(solution)/shard_map/ppermute | solution.py:59
  594.0 10.8 %collective-permute-done.2 = bf16[4,1,24,3095]{3,2,1,0:T(8,128)(2,1)S(1)} collective-permute-done((bf16[4,1,24,3095]{3,2,1,0:T(8,128)(2,1)S(1)}, bf16[4,1,24,3095]{3,2,1,0:T(8,128)(2,1)S(1)}, u32[]{:S(2)}, u32[]{:S(2)}) %collective-permute-start.2) | collective-permute-done | bytes 594272 | tf_op jit(solution)/shard_map/ppermute | solution.py:113
  (291 shorter events, 219.4 us)
Async XLA Ops:
  7.2 78.3 %all-gather.2.cloned.1.call-start = ((), (), s32[]{:S(2)}) async-start(), calls=%async_computation.4 | async-start | bytes 5068800 | tf_op jit(solution)/shard_map/all_gather | solution.py:163
  18.6 69.3 %copy-start.39 = (f32[788]{0:T(1024)}, f32[788]{0:T(1024)S(1)}, u32[]{:S(2)}) copy-start(f32[788]{0:T(1024)S(1)} %broadcast_multiply_fusion.5) | copy-start | bytes 9460
  19.1 74.1 %copy-start.46 = (f32[788]{0:T(1024)}, f32[788]{0:T(1024)S(1)}, u32[]{:S(2)}) copy-start(f32[788]{0:T(1024)S(1)} %add_rsqrt_fusion.1) | copy-start | bytes 9460
  148.7 42.6 %all-to-all-start = ((bf16[16,112,768]{2,1,0:T(8,128)(2,1)}), bf16[16,112,768]{2,1,0:T(8,128)(2,1)S(1)}, u32[]{:S(2)}, u32[]{:S(2)}) async-start(bf16[16,112,768]{2,1,0:T(8,128)(2,1)} %bitcast.171), calls=%async_computation | async-start | bytes 5505024 | tf_op jit(solution)/shard_map/all_to_all | solution.py:182
  191.3 45.6 %all-to-all-start.2 = ((bf16[16,112,768]{2,1,0:T(8,128)(2,1)}), bf16[16,112,768]{2,1,0:T(8,128)(2,1)}, u32[]{:S(2)}, u32[]{:S(2)}) async-start(bf16[16,112,768]{2,1,0:T(8,128)(2,1)} %bitcast.166), calls=%async_computation.2 | async-start | bytes 5505024 | tf_op jit(solution)/shard_map/all_to_all | solution.py:182
  236.9 62.9 %all-to-all-start.1 = ((bf16[16,112,768]{2,1,0:T(8,128)(2,1)}), bf16[16,112,768]{2,1,0:T(8,128)(2,1)}, u32[]{:S(2)}, u32[]{:S(2)}) async-start(bf16[16,112,768]{2,1,0:T(8,128)(2,1)} %bitcast.168), calls=%async_computation.1 | async-start | bytes 5505024 | tf_op jit(solution)/shard_map/all_to_all | solution.py:182
  266.7 75.8 %collective-permute-start.9 = (f32[3840]{0:T(1024)S(1)}, f32[3840]{0:T(1024)S(1)}, u32[]{:S(2)}, u32[]{:S(2)}) collective-permute-start(f32[3840]{0:T(1024)S(1)} %pad_maximum_fusion.3), channel_id=1, source_target_pairs={{0,8},{8,16},{16,24},{24,0},{1,9},{9,17},{17,25},{25,1},{2,10},{10... | collective-permute-start | bytes 46088 | tf_op jit(solution)/shard_map/ppermute | solution.py:95
  268.6 76.2 %collective-permute-start.10 = (f32[3840]{0:T(1024)S(1)}, f32[3840]{0:T(1024)S(1)}, u32[]{:S(2)}, u32[]{:S(2)}) collective-permute-start(f32[3840]{0:T(1024)S(1)} %pad_maximum_fusion.3), channel_id=1, source_target_pairs={{0,16},{8,24},{16,0},{24,8},{1,17},{9,25},{17,1},{25,9},{2,18},{10... | collective-permute-start | bytes 46088 | tf_op jit(solution)/shard_map/ppermute | solution.py:95
  270.1 76.7 %collective-permute-start.11 = (f32[3840]{0:T(1024)S(1)}, f32[3840]{0:T(1024)S(1)}, u32[]{:S(2)}, u32[]{:S(2)}) collective-permute-start(f32[3840]{0:T(1024)S(1)} %pad_maximum_fusion.3), channel_id=1, source_target_pairs={{0,24},{8,0},{16,8},{24,16},{1,25},{9,1},{17,9},{25,17},{2,26},{10... | collective-permute-start | bytes 46088 | tf_op jit(solution)/shard_map/ppermute | solution.py:95
  299.8 59.1 %all-to-all-start.3 = ((bf16[16,112,768]{2,1,0:T(8,128)(2,1)}), bf16[16,112,768]{2,1,0:T(8,128)(2,1)}, u32[]{:S(2)}, u32[]{:S(2)}) async-start(bf16[16,112,768]{2,1,0:T(8,128)(2,1)} %bitcast.167), calls=%async_computation.3 | async-start | bytes 5505024 | tf_op jit(solution)/shard_map/all_to_all | solution.py:182
  325.8 163.8 %collective-permute-start.13 = (bf16[768,768]{1,0:T(8,128)(2,1)}, bf16[768,768]{1,0:T(8,128)(2,1)}, u32[]{:S(2)}, u32[]{:S(2)}) collective-permute-start(bf16[768,768]{1,0:T(8,128)(2,1)} %get-tuple-element.123), channel_id=1, source_target_pairs={{0,16},{16,0},{1,17},{17,1},{2,18},{18,2},{3,19},{19,3},{4,20},{20... | collective-permute-start | bytes 3538952 | tf_op jit(solution)/shard_map/ppermute | solution.py:59
  327.2 182.8 %collective-permute-start.12 = (bf16[768,768]{1,0:T(8,128)(2,1)}, bf16[768,768]{1,0:T(8,128)(2,1)}, u32[]{:S(2)}, u32[]{:S(2)}) collective-permute-start(bf16[768,768]{1,0:T(8,128)(2,1)} %get-tuple-element.122), channel_id=1, source_target_pairs={{0,16},{16,0},{1,17},{17,1},{2,18},{18,2},{3,19},{19,3},{4,20},{20... | collective-permute-start | bytes 3538952 | tf_op jit(solution)/shard_map/ppermute | solution.py:59
  342.5 165.1 %collective-permute-start.7 = (bf16[192,3072]{1,0:T(8,128)(2,1)}, bf16[192,3072]{1,0:T(8,128)(2,1)}, u32[]{:S(2)}, u32[]{:S(2)}) collective-permute-start(bf16[192,3072]{1,0:T(8,128)(2,1)} %get-tuple-element.125), channel_id=1, source_target_pairs={{0,16},{16,0},{1,17},{17,1},{2,18},{18,2},{3,19},{19,3},{4,20},{20... | collective-permute-start | bytes 3538952 | tf_op jit(solution)/shard_map/ppermute | solution.py:59
  344.8 217.3 %collective-permute-start.6 = (bf16[192,3072]{1,0:T(8,128)(2,1)}, bf16[192,3072]{1,0:T(8,128)(2,1)}, u32[]{:S(2)}, u32[]{:S(2)}) collective-permute-start(bf16[192,3072]{1,0:T(8,128)(2,1)} %get-tuple-element.124), channel_id=1, source_target_pairs={{0,16},{16,0},{1,17},{17,1},{2,18},{18,2},{3,19},{19,3},{4,20},{20... | collective-permute-start | bytes 3538952 | tf_op jit(solution)/shard_map/ppermute | solution.py:59
  485.7 74.1 %slice-start = ((s8[9830400]{0:T(1024)(128)(4,1)}), s8[4194304]{0:T(1024)(128)(4,1)S(1)}, s32[]{:S(2)}) async-start(s8[9830400]{0:T(1024)(128)(4,1)} %bitcast.156), calls=%async_computation.5 | async-start | bytes 8388608
  488.5 71.2 %collective-permute-start = (bf16[4,4,24,3095]{3,2,1,0:T(8,128)(2,1)S(1)}, bf16[4,4,24,3095]{3,2,1,0:T(8,128)(2,1)S(1)}, u32[]{:S(2)}, u32[]{:S(2)}) collective-permute-start(bf16[4,4,24,3095]{3,2,1,0:T(8,128)(2,1)S(1)} %fusion.73), channel_id=1, source_target_pairs={{0,1},{1,0},{2,3},{3,2},{4,5},{5,4},{6,7},{7,6},{8,9},{9,8},{10,11... | collective-permute-start | bytes 7130888 | tf_op jit(solution)/shard_map/ppermute | solution.py:113
  489.5 70.3 %slice-start.1 = ((s8[9830400]{0:T(1024)(128)(4,1)}), s8[4194304]{0:T(1024)(128)(4,1)S(1)}, s32[]{:S(2)}) async-start(s8[9830400]{0:T(1024)(128)(4,1)} %bitcast.156), calls=%async_computation.6 | async-start | bytes 8388608
  492.0 65.3 %collective-permute-start.14 = (bf16[768,768]{1,0:T(8,128)(2,1)S(1)}, bf16[768,768]{1,0:T(8,128)(2,1)S(1)}, u32[]{:S(2)}, u32[]{:S(2)}) collective-permute-start(bf16[768,768]{1,0:T(8,128)(2,1)S(1)} %fusion.80), channel_id=1, source_target_pairs={{0,8},{8,0},{1,9},{9,1},{2,10},{10,2},{3,11},{11,3},{4,12},{12,4},... | collective-permute-start | bytes 3538952 | tf_op jit(solution)/shard_map/ppermute | solution.py:59
  510.0 72.6 %collective-permute-start.8 = (bf16[192,3072]{1,0:T(8,128)(2,1)S(1)}, bf16[192,3072]{1,0:T(8,128)(2,1)S(1)}, u32[]{:S(2)}, u32[]{:S(2)}) collective-permute-start(bf16[192,3072]{1,0:T(8,128)(2,1)S(1)} %fusion.81), channel_id=1, source_target_pairs={{0,8},{8,0},{1,9},{9,1},{2,10},{10,2},{3,11},{11,3},{4,12},{12,4},... | collective-permute-start | bytes 3538952 | tf_op jit(solution)/shard_map/ppermute | solution.py:59
  560.4 29.0 %collective-permute-start.1 = (bf16[4,2,24,3095]{3,2,1,0:T(8,128)(2,1)S(1)}, bf16[4,2,24,3095]{3,2,1,0:T(8,128)(2,1)S(1)}, u32[]{:S(2)}, u32[]{:S(2)}) collective-permute-start(bf16[4,2,24,3095]{3,2,1,0:T(8,128)(2,1)S(1)} %fusion.92), channel_id=1, source_target_pairs={{0,2},{1,3},{2,0},{3,1},{4,6},{5,7},{6,4},{7,5},{8,10},{9,11},{10,... | collective-permute-start | bytes 3565448 | tf_op jit(solution)/shard_map/ppermute | solution.py:113
  589.7 15.0 %collective-permute-start.2 = (bf16[4,1,24,3095]{3,2,1,0:T(8,128)(2,1)S(1)}, bf16[4,1,24,3095]{3,2,1,0:T(8,128)(2,1)S(1)}, u32[]{:S(2)}, u32[]{:S(2)}) collective-permute-start(bf16[4,1,24,3095]{3,2,1,0:T(8,128)(2,1)S(1)} %dynamic-slice_convert_fusion.6), channel_id=1, source_target_pairs={{0,4},{1,5},{2,6},{3,7},{4,0},{5,1},{6,2},{7,3},{8,12},{9,13},{10,... | collective-permute-start | bytes 1782728 | tf_op jit(solution)/shard_map/ppermute | solution.py:113
  604.9 8.8 %collective-permute-start.3 = (bf16[24,3095]{1,0:T(8,128)(2,1)S(1)}, bf16[24,3095]{1,0:T(8,128)(2,1)S(1)}, u32[]{:S(2)}, u32[]{:S(2)}) collective-permute-start(bf16[24,3095]{1,0:T(8,128)(2,1)S(1)} %get-tuple-element.129), channel_id=1, source_target_pairs={{0,8},{8,16},{16,24},{24,0},{1,9},{9,17},{17,25},{25,1},{2,10},{10... | collective-permute-start | bytes 445688 | tf_op jit(solution)/shard_map/ppermute | solution.py:121
  605.0 12.7 %collective-permute-start.4 = (bf16[24,3095]{1,0:T(8,128)(2,1)S(1)}, bf16[24,3095]{1,0:T(8,128)(2,1)S(1)}, u32[]{:S(2)}, u32[]{:S(2)}) collective-permute-start(bf16[24,3095]{1,0:T(8,128)(2,1)S(1)} %get-tuple-element.131), channel_id=1, source_target_pairs={{0,16},{8,24},{16,0},{24,8},{1,17},{9,25},{17,1},{25,9},{2,18},{10... | collective-permute-start | bytes 445688 | tf_op jit(solution)/shard_map/ppermute | solution.py:121
  608.1 9.6 %collective-permute-start.5 = (bf16[24,3095]{1,0:T(8,128)(2,1)S(1)}, bf16[24,3095]{1,0:T(8,128)(2,1)S(1)}, u32[]{:S(2)}, u32[]{:S(2)}) collective-permute-start(bf16[24,3095]{1,0:T(8,128)(2,1)S(1)} %get-tuple-element.130), channel_id=1, source_target_pairs={{0,24},{8,0},{16,8},{24,16},{1,25},{9,1},{17,9},{25,17},{2,26},{10... | collective-permute-start | bytes 445688 | tf_op jit(solution)/shard_map/ppermute | solution.py:121
  (59 other events, 449.0 us)
Sparse Core Ops, SparseCore 0:
  18.4 66.9 all-gather.1

commit v2 on v1

v2 whole, which is shorter than its diff:
```python
import functools

import jax
import jax.numpy as jnp
from jax import lax
from jax.experimental import pallas as pl
from jax.experimental.pallas import tpu as pltpu
from jax.sharding import Mesh, PartitionSpec as P


HEAD = 64
SEQ = 197

epsilon = 1e-06
inv_root_two = 0.7071067811865476
inv_root_two_pi = 0.3989422804014327

bf16 = jnp.bfloat16
f32 = jnp.float32
LANES = 128
SEQ_PAD = -(-SEQ // 16) * 16
ROW_TILE = 64
head_scale = HEAD ** (-0.5)
VMEM_MAX = 60 * 1024 * 1024


def dot(a, b):
    return jnp.dot(a, b, preferred_element_type=f32)


def dot_tn(a, b):
    return lax.dot_general(a, b, (((0,), (0,)), ((), ())), preferred_element_type=f32)


def dot_nt(a, b):
    return lax.dot_general(a, b, (((1,), (1,)), ((), ())), preferred_element_type=f32)


def iota(shape, axis):
    return lax.broadcasted_iota(jnp.int32, shape, axis)


def row_valid(start, count):
    return (iota((count, 1), 0) + start) % SEQ_PAD < SEQ


def normed_rows(values):
    centred = values - jnp.mean(values, axis=-1, keepdims=True)
    inv_std = lax.rsqrt(jnp.mean(centred * centred, axis=-1, keepdims=True) + epsilon)
    return centred * inv_std, inv_std


def norm_row_grad(scaled, normed, inv_std):
    return (
        scaled
        - jnp.mean(scaled, axis=-1, keepdims=True)
        - normed * jnp.mean(scaled * normed, axis=-1, keepdims=True)
    ) * inv_std


def tile_of(index, size):
    return pl.ds(pl.multiple_of(index * size, size), size)


def front_kernel(
    experts, x_ref, w_ref, small_ref, bias_ref, vec_ref, spots_ref,
    qkv_ref, att_ref, hid_ref, sec_ref, probs_ref, send_ref, first_ref,
):
    rows, width = x_ref.shape
    col = 256
    gain_one, shift_one = vec_ref[3:4, :], vec_ref[4:5, :]
    gain_two, shift_two = vec_ref[5:6, :], vec_ref[6:7, :]

    @pl.loop(0, rows // ROW_TILE)
    def _(t):
        at = tile_of(t, ROW_TILE)
        normed, _ = normed_rows(x_ref[at, :])
        first_ref[at, :] = (normed * gain_one + shift_one).astype(bf16)

    valid = row_valid(0, rows)

    @pl.loop(0, 3 * width // col)
    def _(j):
        at = tile_of(j, col)
        got = dot(first_ref[...], w_ref[:, at]) + bias_ref[:, at]
        qkv_ref[:, at] = jnp.where(valid, got, 0.0).astype(bf16)

    low = iota((1, LANES), 1) < HEAD
    keys = iota((1, SEQ_PAD), 1) < SEQ
    pairs = width // LANES

    @pl.loop(0, (rows // SEQ_PAD) * pairs)
    def _(n):
        at = tile_of(n // pairs, SEQ_PAD)
        lane = (n % pairs) * LANES
        q = qkv_ref[at, pl.ds(pl.multiple_of(lane, LANES), LANES)]
        k = qkv_ref[at, pl.ds(pl.multiple_of(width + lane, LANES), LANES)]
        v = qkv_ref[at, pl.ds(pl.multiple_of(2 * width + lane, LANES), LANES)]
        parts = []
        for side in (low, ~low):
            scores = dot_nt(jnp.where(side, q, jnp.zeros_like(q)), k) * head_scale
            weights = jnp.where(keys, jnp.exp(scores), 0.0)
            weights = weights * (1.0 / jnp.sum(weights, axis=-1, keepdims=True))
            parts.append(dot(weights.astype(bf16), v))
        att_ref[at, pl.ds(pl.multiple_of(lane, LANES), LANES)] = jnp.where(low, *parts).astype(bf16)

    @pl.loop(0, width // col)
    def _(j):
        at = tile_of(j, col)
        wide = pl.ds(pl.multiple_of(3 * width + j * col, col), col)
        hid_ref[:, at] = x_ref[:, at] + dot(att_ref[...], w_ref[:, wide]) + vec_ref[2:3, at]

    lanes = iota((1, LANES), 1) < experts

    @pl.loop(0, rows // ROW_TILE)
    def _(t):
        at = tile_of(t, ROW_TILE)
        normed, _ = normed_rows(hid_ref[at, :])
        ok = row_valid(t * ROW_TILE, ROW_TILE)
        second = jnp.where(ok, normed * gain_two + shift_two, 0.0).astype(bf16)
        sec_ref[at, :] = second
        grown = jnp.where(lanes, jnp.exp(jnp.where(lanes, dot(second, small_ref[...]), 0.0)), 0.0)
        probs_ref[at, :] = grown / jnp.sum(grown, axis=-1, keepdims=True)

    place_rows(spots_ref, sec_ref, send_ref)


def place_rows(spots_ref, rows_ref, send_ref):
    total, rows = send_ref.shape[0], rows_ref.shape[0]
    block = total // 4

    @pl.loop(0, 4)
    def _(d):
        labels = iota((block, rows), 0) + d * block
        hit = (labels == spots_ref[0:1, :]) | (labels == spots_ref[1:2, :])
        send_ref[tile_of(d, block), :] = dot(jnp.where(hit, 1.0, 0.0).astype(bf16), rows_ref[...]).astype(bf16)


def place_kernel(spots_ref, rows_ref, send_ref, held_ref):
    held_ref[...] = rows_ref[...].astype(bf16)
    place_rows(spots_ref, held_ref, send_ref)


def whole(n):
    return [pl.BlockSpec(memory_space=pltpu.VMEM)] * n


def params(**more):
    return pltpu.CompilerParams(vmem_limit_bytes=VMEM_MAX, **more)


def place_call(spots, values, total):
    rows, width = values.shape
    return pl.pallas_call(
        place_kernel,
        out_shape=jax.ShapeDtypeStruct((total, width), bf16),
        in_specs=whole(2),
        out_specs=whole(1)[0],
        scratch_shapes=[pltpu.VMEM((rows, width), bf16)],
        compiler_params=params(),
        cost_estimate=pl.CostEstimate(flops=2 * total * rows * width, bytes_accessed=rows * width * 4 + total * width * 2, transcendentals=0),
        name="place",
    )(spots, values)


def front_call(experts, total, x, weights, small, bias, vec, spots):
    rows, width = x.shape
    shapes = (
        jax.ShapeDtypeStruct((rows, 3 * width), bf16),
        jax.ShapeDtypeStruct((rows, width), bf16),
        jax.ShapeDtypeStruct((rows, width), f32),
        jax.ShapeDtypeStruct((rows, width), bf16),
        jax.ShapeDtypeStruct((rows, LANES), f32),
        jax.ShapeDtypeStruct((total, width), bf16),
    )
    return pl.pallas_call(
        functools.partial(front_kernel, experts),
        out_shape=shapes,
        in_specs=whole(6),
        out_specs=tuple(whole(6)),
        scratch_shapes=[pltpu.VMEM((rows, width), bf16)],
        compiler_params=params(),
        cost_estimate=pl.CostEstimate(flops=14 * 10**9, bytes_accessed=30 * 10**6, transcendentals=2 * 10**6),
        name="front",
    )(x, weights, small, bias, vec, spots)


def gelu_parts(pre_act):
    cumulative = 0.5 * (1.0 + lax.erf(pre_act * inv_root_two))
    return pre_act * cumulative, cumulative


def gate_kernel(experts, which_ref, x_ref, cot_ref, small_ref, grad_ref, sum_ref):
    lane = iota((1, LANES), 1)
    mine = lane == which_ref[0]
    total = jnp.zeros((1, cot_ref.shape[1]), f32)
    rows = x_ref.shape[0]
    size = 128

    def step(t, total):
        at = tile_of(t, size)
        logits = jnp.where(lane < experts, dot(x_ref[at, :], small_ref[...]), 0.0)
        grown = jnp.where(lane < experts, jnp.exp(logits), 0.0)
        gate = jnp.sum(jnp.where(mine, grown, 0.0), axis=-1, keepdims=True) / jnp.sum(grown, axis=-1, keepdims=True)
        scaled = (gate * cot_ref[at, :].astype(f32)).astype(bf16)
        grad_ref[at, :] = scaled
        return total + jnp.sum(scaled.astype(f32), axis=0, keepdims=True)

    sum_ref[...] = lax.fori_loop(0, rows // size, step, total)


def gate_call(experts, which, rows_in, cot, small):
    return pl.pallas_call(
        functools.partial(gate_kernel, experts),
        out_shape=(jax.ShapeDtypeStruct(cot.shape, bf16), jax.ShapeDtypeStruct((1, cot.shape[1]), f32)),
        in_specs=[pl.BlockSpec(memory_space=pltpu.SMEM)] + whole(3),
        out_specs=tuple(whole(2)),
        compiler_params=params(),
        cost_estimate=pl.CostEstimate(flops=10**9, bytes_accessed=3 * cot.size * 2, transcendentals=10**5),
        name="gate",
    )(which, rows_in, cot, small)


def down_kernel(x_ref, grad_ref, up_ref, shift_ref, out_ref, act_ref):
    rows = x_ref.shape[0]
    size = rows // 4

    @pl.loop(0, 4)
    def _(t):
        at = tile_of(t, size)
        act_ref[at, :] = gelu_parts(dot(x_ref[at, :], up_ref[...]) + shift_ref[...])[0].astype(bf16)

    out_ref[...] = dot_tn(act_ref[...], grad_ref[...]).astype(bf16)


def down_call(x, grads, up, shift, tile, part, parts):
    rows, width = x.shape
    span = up.shape[1] // parts
    steps = span // tile
    grid = pltpu.PrefetchScalarGridSpec(
        num_scalar_prefetch=1,
        grid=(steps,),
        in_specs=[
            pl.BlockSpec((rows, width), lambda j, p: (0, 0)),
            pl.BlockSpec((rows, width), lambda j, p: (0, 0)),
            pl.BlockSpec((width, tile), lambda j, p: (0, p[0] * steps + j)),
            pl.BlockSpec((1, tile), lambda j, p: (0, p[0] * steps + j)),
        ],
        out_specs=pl.BlockSpec((tile, width), lambda j, p: (j, 0)),
        scratch_shapes=[pltpu.VMEM((rows, tile), bf16)],
    )
    return pl.pallas_call(
        lambda p_ref, *refs: down_kernel(*refs),
        out_shape=jax.ShapeDtypeStruct((span, width), bf16),
        grid_spec=grid,
        compiler_params=params(dimension_semantics=("arbitrary",)),
        cost_estimate=pl.CostEstimate(flops=4 * rows * width * span, bytes_accessed=4 * rows * width + 4 * span * width, transcendentals=rows * span),
        name="down",
    )(part, x, grads, up, shift)


def expert_kernel(
    x_ref, grad_ref, up_ref, shift_ref, down_ref, down_shift_ref,
    upg_ref, upsum_ref, out_ref, rows_ref, pre_ref, dpre_ref, out_acc, rows_acc,
):
    j = pl.program_id(0)
    rows, _ = x_ref.shape
    tile = up_ref.shape[1]
    size = rows // 4

    @pl.when(j == 0)
    def _():
        out_acc[...] = jnp.broadcast_to(down_shift_ref[...], out_acc.shape)
        rows_acc[...] = jnp.zeros_like(rows_acc)

    def step(t, total):
        at = tile_of(t, size)
        pre = dot(x_ref[at, :], up_ref[...]) + shift_ref[...]
        act, cumulative = gelu_parts(pre)
        slope = cumulative + pre * jnp.exp(-0.5 * pre * pre) * inv_root_two_pi
        d_pre = dot_nt(grad_ref[at, :], down_ref[...]) * slope
        d_pre_b = d_pre.astype(bf16)
        dpre_ref[at, :] = d_pre_b
        out_acc[at, :] += dot(act.astype(bf16), down_ref[...])
        rows_acc[at, :] += dot_nt(d_pre_b, up_ref[...])
        return total + jnp.sum(d_pre, axis=0, keepdims=True)

    upsum_ref[...] = lax.fori_loop(0, 4, step, jnp.zeros((1, tile), f32))
    upg_ref[...] = dot_tn(x_ref[...], dpre_ref[...]).astype(bf16)

    @pl.when(j == pl.num_programs(0) - 1)
    def _():
        out_ref[...] = out_acc[...].astype(bf16)
        rows_ref[...] = rows_acc[...].astype(bf16)


def expert_call(x, grads, up, shift, down, down_shift, tile):
    rows, width = x.shape
    hidden = up.shape[1]
    fixed = lambda *shape: pl.BlockSpec(shape, lambda j: (0, 0))
    return pl.pallas_call(
        expert_kernel,
        out_shape=(
            jax.ShapeDtypeStruct((width, hidden), bf16),
            jax.ShapeDtypeStruct((1, hidden), f32),
            jax.ShapeDtypeStruct((rows, width), bf16),
            jax.ShapeDtypeStruct((rows, width), bf16),
        ),
        grid=(hidden // tile,),
        in_specs=[
            fixed(rows, width),
            fixed(rows, width),
            pl.BlockSpec((width, tile), lambda j: (0, j)),
            pl.BlockSpec((1, tile), lambda j: (0, j)),
            pl.BlockSpec((tile, width), lambda j: (j, 0)),
            fixed(1, width),
        ],
        out_specs=(
            pl.BlockSpec((width, tile), lambda j: (0, j)),
            pl.BlockSpec((1, tile), lambda j: (0, j)),
            fixed(rows, width),
            fixed(rows, width),
        ),
        scratch_shapes=[
            pltpu.VMEM((8, LANES), f32),
            pltpu.VMEM((rows, tile), bf16),
            pltpu.VMEM((rows, width), f32),
            pltpu.VMEM((rows, width), f32),
        ],
        compiler_params=params(dimension_semantics=("arbitrary",)),
        cost_estimate=pl.CostEstimate(flops=10 * rows * width * hidden, bytes_accessed=8 * rows * width + 6 * hidden * width, transcendentals=2 * rows * hidden),
        name="expert",
    )(x, grads, up, shift, down, down_shift)


def combine_kernel(
    outs_ref, back_ref, cot_ref, hid_ref, sec_ref, probs_ref, spots_ref, ids_ref, w_ref, small_ref, vec_ref,
    blk_ref, dhid_ref, dhb_ref, datt_ref, dlog_ref, sums_ref,
):
    rows, width = cot_ref.shape
    total = outs_ref.shape[0]
    size = SEQ_PAD
    gain_two = vec_ref[5:6, :]
    labels = iota((1, total), 1)
    lane = iota((1, LANES), 1)

    def step(t, sums):
        at = tile_of(t, size)
        first = jnp.where(spots_ref[at, 0:1] == labels, 1.0, 0.0).astype(bf16)
        second = jnp.where(spots_ref[at, 1:2] == labels, 1.0, 0.0).astype(bf16)
        got0, got1 = dot(first, outs_ref[...]), dot(second, outs_ref[...])
        back = dot(first + second, back_ref[...])
        probs = probs_ref[at, :]
        hot0 = jnp.where(ids_ref[at, 0:1] == lane, 1.0, 0.0)
        hot1 = jnp.where(ids_ref[at, 1:2] == lane, 1.0, 0.0)
        gate0 = jnp.sum(probs * hot0, axis=-1, keepdims=True)
        gate1 = jnp.sum(probs * hot1, axis=-1, keepdims=True)
        cot = cot_ref[at, :]
        hid = hid_ref[at, :]
        blk_ref[at, :] = hid + gate0 * got0 + gate1 * got1
        d0 = jnp.sum(cot * got0, axis=-1, keepdims=True)
        d1 = jnp.sum(cot * got1, axis=-1, keepdims=True)
        d_probs = d0 * hot0 + d1 * hot1
        d_logits = (probs * (d_probs - jnp.sum(probs * d_probs, axis=-1, keepdims=True))).astype(bf16)
        dlog_ref[at, :] = d_logits
        d_second = dot_nt(d_logits, small_ref[...]) + back
        normed, inv_std = normed_rows(hid)
        d_hidden = cot + norm_row_grad(d_second * gain_two, normed, inv_std)
        dhid_ref[at, :] = d_hidden
        d_hidden_b = d_hidden.astype(bf16)
        dhb_ref[at, :] = d_hidden_b
        datt_ref[at, :] = dot_nt(d_hidden_b, w_ref[...]).astype(bf16)
        add = lambda v: jnp.sum(v, axis=0, keepdims=True)
        return tuple(s + add(v) for s, v in zip(sums, (d_hidden, d_second * normed, d_second)))

    zero = jnp.zeros((1, width), f32)
    sums = lax.fori_loop(0, rows // size, step, (zero, zero, zero))
    for i, s in enumerate(sums):
        sums_ref[i : i + 1, :] = s


def combine_call(outs, back, cot, hid, sec, probs, spots, ids, weights, small, vec):
    rows, width = cot.shape
    shapes = (
        jax.ShapeDtypeStruct((rows, width), f32),
        jax.ShapeDtypeStruct((rows, width), f32),
        jax.ShapeDtypeStruct((rows, width), bf16),
        jax.ShapeDtypeStruct((rows, width), bf16),
        jax.ShapeDtypeStruct((rows, LANES), bf16),
        jax.ShapeDtypeStruct((8, width), f32),
    )
    return pl.pallas_call(
        combine_kernel,
        out_shape=shapes,
        grid=(1,),
        in_specs=[
            *[pl.BlockSpec(a.shape, lambda i: (0, 0)) for a in (outs, back, cot, hid, sec, probs, spots, ids)],
            pl.BlockSpec((width, width), lambda i: (0, 3)),
            *[pl.BlockSpec(a.shape, lambda i: (0, 0)) for a in (small, vec)],
        ],
        out_specs=tuple(pl.BlockSpec(s.shape, lambda i: (0, 0)) for s in shapes),
        compiler_params=params(),
        cost_estimate=pl.CostEstimate(flops=8 * 10**9, bytes_accessed=25 * 10**6, transcendentals=0),
        name="combine",
    )(outs, back, cot, hid, sec, probs, spots, ids, weights, small, vec)


def back_kernel(
    experts, x_ref, qkv_ref, datt_ref, dhid_ref, dhb_ref, att_ref, sec_ref, dlog_ref, w_ref, vec_ref, sums_ref,
    in_ref, dense_ref, dqkv_ref, first_ref, dfirst_ref,
):
    rows, width = x_ref.shape
    col = 256
    gain_one, shift_one = vec_ref[3:4, :], vec_ref[4:5, :]
    low = iota((1, LANES), 1) < HEAD
    keys = iota((1, SEQ_PAD), 1) < SEQ
    pairs = width // LANES

    @pl.loop(0, (rows // SEQ_PAD) * pairs)
    def _(n):
        at = tile_of(n // pairs, SEQ_PAD)
        lane = (n % pairs) * LANES
        spans = [pl.ds(pl.multiple_of(o + lane, LANES), LANES) for o in (0, width, 2 * width)]
        q, k, v = (qkv_ref[at, s] for s in spans)
        d_out = datt_ref[at, spans[0]]
        d_q, d_k, d_v = [], [], []
        for side in (low, ~low):
            q_side = jnp.where(side, q, jnp.zeros_like(q))
            scores = dot_nt(q_side, k) * head_scale
            weights = jnp.where(keys, jnp.exp(scores), 0.0)
            weights = weights * (1.0 / jnp.sum(weights, axis=-1, keepdims=True))
            d_w = dot_nt(jnp.where(side, d_out, jnp.zeros_like(d_out)), v)
            d_s = (weights * (d_w - jnp.sum(weights * d_w, axis=-1, keepdims=True)) * head_scale).astype(bf16)
            d_v.append(dot_tn(weights.astype(bf16), d_out))
            d_q.append(dot(d_s, k))
            d_k.append(dot_tn(d_s, q))
        for s, parts in zip(spans, (d_q, d_k, d_v)):
            dqkv_ref[at, s] = jnp.where(low, *parts).astype(bf16)

    @pl.loop(0, rows // ROW_TILE)
    def _(t):
        at = tile_of(t, ROW_TILE)
        normed, _ = normed_rows(x_ref[at, :])
        first_ref[at, :] = (normed * gain_one + shift_one).astype(bf16)

    @pl.loop(0, 3 * width // col)
    def _(j):
        at = tile_of(j, col)
        dense_ref[:, at] = dot_tn(first_ref[...], dqkv_ref[:, at]).astype(bf16)

    @pl.loop(0, width // col)
    def _(j):
        at = tile_of(j, col)
        wide = pl.ds(pl.multiple_of(3 * width + j * col, col), col)
        dense_ref[:, wide] = dot_tn(att_ref[...], dhb_ref[:, at]).astype(bf16)
        dfirst_ref[:, at] = dot_nt(dqkv_ref[...], w_ref[at, :])

    def step(t, sums):
        at = tile_of(t, ROW_TILE)
        d_first = dfirst_ref[at, :]
        normed, inv_std = normed_rows(x_ref[at, :])
        in_ref[at, :] = dhid_ref[at, :] + norm_row_grad(d_first * gain_one, normed, inv_std)
        add = lambda v: jnp.sum(v, axis=0, keepdims=True)
        return sums[0] + add(d_first * normed), sums[1] + add(d_first)

    zero = jnp.zeros((1, width), f32)
    gain_sum, shift_sum = lax.fori_loop(0, rows // ROW_TILE, step, (zero, zero))

    ones = jnp.ones((8, rows), bf16)
    q_sum = dot(ones, dqkv_ref[:, :width])[0:1, :]
    v_sum = dot(ones, dqkv_ref[:, 2 * width :])[0:1, :]
    order = [q_sum, v_sum, sums_ref[0:1, :], gain_sum, shift_sum, sums_ref[1:2, :], sums_ref[2:3, :]]
    stacked = jnp.concatenate(order + [jnp.zeros((LANES - len(order), width), f32)], axis=0)
    columns = jnp.transpose(stacked, (1, 0))
    router = dot_tn(sec_ref[...], dlog_ref[...])
    lane = iota((1, LANES), 1)
    columns = pltpu.roll(columns, experts, 1)
    dense_ref[:, pl.ds(4 * width, LANES)] = jnp.where(lane < experts, router, columns).astype(bf16)


def back_call(experts, x, qkv, datt, dhid, dhb, att, sec, dlog, weights, vec, sums):
    rows, width = x.shape
    shapes = (jax.ShapeDtypeStruct((rows, width), f32), jax.ShapeDtypeStruct((width, 4 * width + LANES), bf16))
    one = lambda a: pl.BlockSpec(a.shape, lambda i: (0, 0))
    return pl.pallas_call(
        functools.partial(back_kernel, experts),
        out_shape=shapes,
        grid=(1,),
        in_specs=[
            *[one(a) for a in (x, qkv, datt, dhid, dhb, att, sec, dlog)],
            pl.BlockSpec((width, 3 * width), lambda i: (0, 0)),
            one(vec),
            one(sums),
        ],
        out_specs=tuple(one(s) for s in shapes),
        scratch_shapes=[
            pltpu.VMEM((rows, 3 * width), bf16),
            pltpu.VMEM((rows, width), bf16),
            pltpu.VMEM((rows, width), f32),
        ],
        compiler_params=params(),
        cost_estimate=pl.CostEstimate(flops=15 * 10**9, bytes_accessed=35 * 10**6, transcendentals=2 * 10**6),
        name="back",
    )(x, qkv, datt, dhid, dhb, att, sec, dlog, weights, vec, sums)


def pick(value, index, axis):
    return lax.dynamic_index_in_dim(value, index, axis, keepdims=False)


def shift_along(value, axis, step):
    size = lax.axis_size("hi") * lax.axis_size("lo") if isinstance(axis, tuple) else lax.axis_size(axis)
    return lax.ppermute(value, axis, [(i, (i + step) % size) for i in range(size)])


def send_pairs(spans):
    fan, low = lax.axis_size("lo"), lax.axis_index("lo")
    got = [None] * fan
    for step in list(range(1, fan)) + [0]:
        got[step] = [shift_along(pick(s, (low + step) % fan, 0), "hi", hop) for hop, s in enumerate(spans, 1)]
    return got


def finish(mine, got):
    fan, low = lax.axis_size("lo"), lax.axis_index("lo")
    parts = [None] * fan
    for step in list(range(1, fan)) + [0]:
        value = pick(mine, (low + step) % fan, 0).astype(f32)
        for other in got[step]:
            value = value + other.astype(f32)
        if step:
            value = shift_along(value.astype(bf16), "lo", step).astype(f32)
        parts[step] = value
    return by_expert(parts)


def by_expert(parts):
    fan, low = lax.axis_size("lo"), lax.axis_index("lo")
    if fan == 1:
        return parts[0][None]
    if fan == 2:
        return jnp.stack([jnp.where(low == 0, parts[0], parts[1]), jnp.where(low == 0, parts[1], parts[0])])
    stacked = jnp.stack(parts)
    return jnp.stack([pick(stacked, (low - k) % fan, 0) for k in range(fan)])


def dense_sum(matrix):
    members = lax.axis_size("hi") * lax.axis_size("lo")
    me = lax.axis_index("hi") * lax.axis_size("lo") + lax.axis_index("lo")
    plane, spot = lax.axis_size("expert"), lax.axis_index("expert")
    rows, columns = matrix.shape
    piece = rows // (members * plane)
    current = matrix.reshape(members, plane, piece, columns)
    left, bit = plane, 1
    while left > 1:
        halves = current.reshape(members, left // 2, 2, piece, columns)
        side = (spot // bit) % 2
        sent = pick(halves, 1 - side, 2).astype(bf16)
        came = lax.ppermute(sent, "expert", [(i, i ^ bit) for i in range(plane)])
        current = pick(halves, side, 2).astype(f32) + came.astype(f32)
        left //= 2
        bit *= 2
    current = current.reshape(members, piece, columns)
    summed = pick(current, me, 0)
    for step in range(1, members):
        sent = pick(current, (me + step) % members, 0).astype(bf16)
        summed = summed + shift_along(sent, ("hi", "lo"), step).astype(f32)
    return summed


def local(
    block_in, out_grad, expert_ids, slot_ids, qkv_weight, q_bias, v_bias, out_weight, out_bias,
    norm1_gain, norm1_bias, norm2_gain, norm2_bias, router_weight, up_weight, up_bias, down_weight, down_bias,
):
    tok_rows, width = block_in.shape
    images = tok_rows // SEQ
    experts = router_weight.shape[1]
    capacity = tok_rows * 2 * 9 // (8 * experts) + 1
    slots = -(-capacity // 16) * 16
    total = experts * slots
    outer, fan, plane = lax.axis_size("hi"), lax.axis_size("lo"), lax.axis_size("expert")
    members = outer * fan
    high, low, spot = lax.axis_index("hi"), lax.axis_index("lo"), lax.axis_index("expert")
    me = high * fan + low
    hidden = up_weight.shape[2]

    def padded(values, fill=0):
        shaped = values.reshape(images, SEQ, values.shape[1])
        shaped = jnp.pad(shaped, ((0, 0), (0, SEQ_PAD - SEQ), (0, 0)), constant_values=fill)
        return shaped.reshape(images * SEQ_PAD, values.shape[1])

    def exchange(value):
        return lax.all_to_all(value, ("lo", "expert"), split_axis=0, concat_axis=0, tiled=True)

    vectors = (q_bias, v_bias, out_bias, norm1_gain, norm1_bias, norm2_gain, norm2_bias)
    extra = jnp.stack(vectors, axis=1)
    spare = jnp.zeros((extra.shape[0], LANES - experts - len(vectors)), bf16)
    packed = jnp.concatenate([qkv_weight, out_weight, router_weight, extra, spare], axis=1)
    part = packed.shape[0] // plane
    packed = lax.dynamic_slice_in_dim(packed, spot * part, part, 0)
    weights = lax.all_gather(packed, ("hi", "lo", "expert"), axis=0, tiled=True)
    small = weights[:, 4 * width :]
    vec = jnp.pad(small[:, experts : experts + len(vectors)].T.astype(f32), ((0, 1), (0, 0)))
    bias = jnp.concatenate([vec[0:1], jnp.zeros((1, width), f32), vec[1:2]], axis=1)

    up_one = pick(up_weight, low, 0)
    down_one = pick(down_weight, low, 0)
    up_shift = pick(up_bias, low, 0).astype(f32)[None]
    down_shift = pick(down_bias, low, 0).astype(f32)[None]

    owner = (expert_ids % fan) * plane + expert_ids // fan
    spots = padded(jnp.where(slot_ids >= 0, owner * slots + slot_ids, -1), -1)
    ids = padded(expert_ids, -1)
    spots_t = spots.T
    x = padded(block_in)
    cot = padded(out_grad)

    cot_sent, x = lax.optimization_barrier((place_call(spots_t, cot, total), x))
    cot_rows = exchange(cot_sent)

    qkv, att, hid, sec, probs, send = front_call(experts, total, x, weights, small, bias, vec, spots_t)
    rows_in = exchange(send)

    which = (spot * fan + low).astype(jnp.int32).reshape(1)
    grads, down_sum = gate_call(experts, which, rows_in, cot_rows, small)
    tile = 512 if (hidden // outer) % 512 == 0 else hidden // outer

    def down_span(hop, x_rows):
        part = ((high + hop) % outer).astype(jnp.int32).reshape(1)
        return down_call(x_rows, grads, up_one, up_shift, tile, part, outer).reshape(fan, hidden // members, width)

    down_away = [down_span(hop, rows_in) for hop in range(1, outer)]
    down_sent = send_pairs(down_away)
    rows_in, *_ = lax.optimization_barrier((rows_in, *down_away))
    up_grad, up_sum, outs, d_rows = expert_call(rows_in, grads, up_one, up_shift, down_one, down_shift, tile)
    up_blocks = up_grad.reshape(outer, fan, width // members, hidden)
    up_sent = send_pairs([pick(up_blocks, (high + hop) % outer, 0) for hop in range(1, outer)])
    both = jnp.concatenate([outs.reshape(-1, slots, width), d_rows.reshape(-1, slots, width)], axis=1)
    both = exchange(both)
    outs_back, rows_back = both[:, :slots].reshape(total, width), both[:, slots:].reshape(total, width)
    rows_in, _ = lax.optimization_barrier((rows_in, up_grad))
    down_mine = down_span(0, rows_in)
    down_part = finish(down_mine, down_sent)
    up_part = finish(pick(up_blocks, high, 0), up_sent)

    summary = jnp.concatenate([up_sum, down_sum], axis=1)
    small_rows = jnp.concatenate([summary] + [shift_along(summary, ("hi", "lo"), s) for s in range(1, members)], axis=0)
    from_expert = (me - jnp.arange(members)) % fan
    biases = jnp.stack(
        [jnp.sum(jnp.where((from_expert == k)[:, None], small_rows, 0.0), axis=0) for k in range(fan)]
    )
    up_shift_part = lax.dynamic_slice_in_dim(biases[:, :hidden], me * (hidden // members), hidden // members, 1)
    down_shift_part = lax.dynamic_slice_in_dim(biases[:, hidden:], me * (width // members), width // members, 1)

    block_out, d_hid, d_hid_b, d_att, d_log, sums = combine_call(
        outs_back, rows_back, cot, hid, sec, probs, spots, ids, weights, small, vec
    )
    input_grad, dense = back_call(experts, x, qkv, d_att, d_hid, d_hid_b, att, sec, d_log, weights, vec, sums)

    def unpadded(values):
        return values.reshape(images, SEQ_PAD, width)[:, :SEQ].reshape(tok_rows, width)

    dense = dense_sum(dense)
    at = 4 * width + experts
    return (
        unpadded(block_out), unpadded(input_grad),
        dense[:, : 3 * width], dense[:, at], dense[:, at + 1], dense[:, 3 * width : 4 * width],
        dense[:, at + 2], dense[:, at + 3], dense[:, at + 4], dense[:, at + 5], dense[:, at + 6],
        dense[:, 4 * width : at],
        up_part, up_shift_part, down_part, down_shift_part,
    )


def solution(mesh):
    def step(*arrays):
        members, plane = mesh.shape["dp"], mesh.shape["expert"]
        fan = arrays[14].shape[0] // plane
        split = Mesh(mesh.devices.reshape(members // fan, fan, plane), ("hi", "lo", "expert"))
        every, dp = ("hi", "lo", "expert"), ("hi", "lo")
        in_specs = (
            (P(every, None),) * 4
            + (P(dp, None), P(dp), P(dp), P(dp, None), P(dp), P(dp), P(dp), P(dp), P(dp), P(dp, None))
            + (P("expert", None, None), P("expert", None), P("expert", None, None), P("expert", None))
        )
        out_specs = (
            (P(every, None),) * 3
            + (P(every), P(every), P(every, None))
            + (P(every),) * 5
            + (P(every, None), P("expert", dp, None), P("expert", dp), P("expert", dp, None), P("expert", dp))
        )

        return jax.shard_map(local, mesh=split, in_specs=in_specs, out_specs=out_specs, check_vma=False)(*arrays)

    return step
```

time: 639 us -> 704 us (1.10); the launches traced: 628 us -> 701 us
  Pallas kernels: 0 us -> 220 us
  matrix products: 203 us -> 0 us
  waiting for transfers between devices: 201 us -> 339 us
  local copies, waits for them, and re-layouts: 136 us -> 62.3 us
  other arithmetic: 31.1 us -> 22.1 us
    pallas_call x0 -> x8, Pallas kernels: none -> 220 us  [the longest x1 56.1 us: expert_call(): pl.pallas_call(expert_kernel, out_shape=(jax.ShapeDtypeStruct((width, hid...]
    dot_general x27 -> x0, matrix products: 203 us -> none  [the longest x11 66.7 us: dot(): return jnp.dot(a, b, preferred_element_type=f32)]
    ppermute x6 -> x12, waiting for transfers between devices: 80.9 us -> 166 us  [shift_along(): lax.ppermute(value, axis, [(i, (i + step) % size) for i in range(size)])]
    all_to_all x4 -> x3, waiting for transfers between devices: 34.5 us -> 113 us  [exchange(): lax.all_to_all(value, ('lo', 'expert'), split_axis=0, concat_axis=0, tile...]
    reshape x12 -> x8, local copies, waits for them, and re-layouts: 46.1 us -> 8.41 us  [the longest x6 5 us: padded(): shaped = values.reshape(images, SEQ, values.shape[1])]
    concatenate x20 -> x3, local copies, waits for them, and re-layouts: 29 us -> 3.42 us  [the longest x1 3.4 us: local(): jnp.concatenate([qkv_weight, out_weight, router_weight, extra, spare], ax...]
    ppermute x6 -> x12, starting transfers between devices: 7.8 us -> 26.9 us  [shift_along(): lax.ppermute(value, axis, [(i, (i + step) % size) for i in range(size)])]
    squeeze x0 -> x5, local copies, waits for them, and re-layouts: none -> 17.5 us  [pick(): return lax.dynamic_index_in_dim(value, index, axis, keepdims=False)]
  transfers between devices with their start and end apart: 20 -> 19, of which waited for: 10 -> 7; matrix products, arithmetic and copies ran while one was open for 45% -> 9% of each run, Pallas kernels for 0% -> 20%
where the time goes in v2:
time: 704 us; the launch traced here: 701 us
  waiting for transfers between devices  339 us (48%)
  Pallas kernels  220 us (31%)
  local copies, waits for them, and re-layouts  62.3 us (9%)
  starting transfers between devices  43.7 us (6%)
  other arithmetic  22.1 us (3%)
  between operations  14.6 us (2%)
    ppermute x12, waiting for transfers between devices, shift_along(): lax.ppermute(value, axis, [(i, (i + step) % size) for i in range(size)])  166 us
    all_to_all x3, waiting for transfers between devices, exchange(): lax.all_to_all(value, ('lo', 'expert'), split_axis=0, concat_axis=0, tile...  113 us
    all_gather x1, waiting for transfers between devices, local(): weights = lax.all_gather(packed, ('hi', 'lo', 'expert'), axis=0, tiled=True)  60 us
    pallas_call x1, Pallas kernels, expert_call(): pl.pallas_call(expert_kernel, out_shape=(jax.ShapeDtypeStruct((width, hid...  56.1 us
    pallas_call x1, Pallas kernels, back_call(): pl.pallas_call(functools.partial(back_kernel, experts), out_shape=shapes,...  52.2 us
    pallas_call x1, Pallas kernels, front_call(): pl.pallas_call(functools.partial(front_kernel, experts), out_shape=shapes...  42.2 us
    pallas_call x2, Pallas kernels, down_call(): pl.pallas_call(lambda p_ref, *refs: down_kernel(*refs), out_shape=jax.Sha...  32.1 us
    ppermute x12, starting transfers between devices, shift_along(): lax.ppermute(value, axis, [(i, (i + step) % size) for i in range(size)])  26.9 us
  transfers between devices with their start and end apart: 19, of which 7 were waited for; matrix products, arithmetic and copies ran while one was open for 9% of the time, Pallas kernels for 20%

profile of v2, /device:TPU:0, one launch (start us, length us, event | category | flops | bytes accessed | tf_op | source)
XLA Modules:
  0.0 700.8 jit_solution(17038529079417269328)
XLA Ops:
  30.1 7.1 %place.1 = bf16[1792,768]{1,0:T(8,128)(2,1)} custom-call(s32[2,832]{1,0:T(2,128)} %copy.85.spots_ref, f32[832,768]{1,0:T(8,128)} %bitcast.107), custom_call_target="tpu_custom_call" | custom-call | flops 2290089984 | bytes 5308416 | tf_op jit(solution)/shard_map/place/pallas_call | solution.py:154
  37.2 6.3 all-to-all-start.1
  43.5 60.0 %all-gather.2.cloned.1.call-done.w_ref = bf16[768,3200]{1,0:T(8,128)(2,1)} async-done(((bf16[24,3200]{1,0:T(8,128)(2,1)}), bf16[768,3200]{1,0:T(8,128)(2,1)}) %all-gather.2.cloned.1.call-update) | async-done | bytes 4915216 | tf_op jit(solution)/shard_map/all_gather | solution.py:601
  107.5 42.2 %front.1 = (bf16[832,2304]{1,0:T(8,128)(2,1)}, bf16[832,768]{1,0:T(8,128)(2,1)}, f32[832,768]{1,0:T(8,128)}, bf16[832,768]{1,0:T(8,128)(2,1)}, f32[832,128]{1,0:T(8,128)}, /*index=5*/bf16[1792,768]{1,0:T(8,128)(2,1)}) custom-call(f32[832,768]{1,0:T(8,128)} %bitcast.105, bf16[768,3200]{1,0:T(8,128)(2,1)} %all-gather.2.cloned.1.call-done.w_ref, ...), custom_call_target="tpu_custom_call" | custom-call | flops 14000000000 | bytes 30000000 | tf_op jit(solution)/shard_map/front/pallas_call | solution.py:176
  151.2 4.3 all-to-all-start
  156.7 4.8 dynamic-slice_bitcast_fusion.1.refs_2_.up_ref
  161.6 4.8 dynamic-slice_bitcast_fusion.down_ref
  166.4 28.1 %all-to-all-done = bf16[16,112,768]{2,1,0:T(8,128)(2,1)S(1)} async-done(((bf16[16,112,768]{2,1,0:T(8,128)(2,1)}), bf16[16,112,768]{2,1,0:T(8,128)(2,1)S(1)}, u32[]{:S(2)}, u32[]{:S(2)}) %all-to-all-start) | async-done | bytes 2752544 | tf_op jit(solution)/shard_map/all_to_all | solution.py:593
  196.1 8.9 %gate.1 = (bf16[1792,768]{1,0:T(8,128)(2,1)}, f32[1,768]{1,0:T(1,128)}) custom-call(s32[1]{0:T(128)} %bitcast.8.which_ref, bf16[1792,768]{1,0:T(8,128)(2,1)} %bitcast.89, bf16[1792,768]{1,0:T(8,128)(2,1)} %bitcast.93, bf16[768,128]{1,0:T(8,128)(2,1)} %slice.83.small_ref), custom_call_target="tpu_custom_call" | custom-call | flops 1000000000 | bytes 8257536 | tf_op jit(solution)/shard_map/gate/pallas_call | solution.py:213
  205.0 16.0 %down.2 = bf16[1536,768]{1,0:T(8,128)(2,1)} custom-call(s32[1]{0:T(128)} %bitcast.7.p_ref, bf16[1792,768]{1,0:T(8,128)(2,1)} %bitcast.90, bf16[1792,768]{1,0:T(8,128)(2,1)} %get-tuple-element.43.refs_1_.grad_ref, bf16[768,3072]{1,0:T(8,128)(2,1)} %dynamic-slice_bitcast_fusion.1.refs_2_.up_ref, f32[1,3072]{1,0:T(1,128)} %dynamic-slice_convert_fusion.5.refs_3_.shift_ref), custom_call_target="tpu_custom_call" | custom-call | flops 8455716864 | bytes 10223616 | tf_op jit(solution)/shard_map/down/pallas_call | solution.py:252
  221.1 56.1 %expert.1 = (bf16[768,3072]{1,0:T(8,128)(2,1)}, f32[1,3072]{1,0:T(1,128)}, bf16[1792,768]{1,0:T(8,128)(2,1)}, bf16[1792,768]{1,0:T(8,128)(2,1)}) custom-call(bf16[1792,768]{1,0:T(8,128)(2,1)} %bitcast.91, bf16[1792,768]{1,0:T(8,128)(2,1)} %get-tuple-element.43.refs_1_.grad_ref, bf16[768,3072]{1,0:T(8,128)(2,1)} %dynamic-slice_bitcast_fusion.1.refs_2_.up_ref, ...), custom_call_target="tpu_custom_call" | custom-call | flops 42278584320 | bytes 25165824 | tf_op jit(solution)/shard_map/expert/pallas_call | solution.py:301
  277.1 5.5 pad_maximum_fusion
  282.6 6.1 all-to-all-start.2
  290.6 3.6 collective-permute-start.11
  297.8 84.4 %all-to-all-done.2 = bf16[16,224,768]{2,1,0:T(8,128)(2,1)} async-done(((bf16[16,224,768]{2,1,0:T(8,128)(2,1)}), bf16[16,224,768]{2,1,0:T(8,128)(2,1)}, u32[]{:S(2)}, u32[]{:S(2)}) %all-to-all-start.2) | async-done | bytes 5505056 | tf_op jit(solution)/shard_map/all_to_all | solution.py:593
  382.2 5.4 fusion.19
  387.6 21.2 %combine.1 = (f32[832,768]{1,0:T(8,128)}, f32[832,768]{1,0:T(8,128)}, bf16[832,768]{1,0:T(8,128)(2,1)}, bf16[832,768]{1,0:T(8,128)(2,1)}, bf16[832,128]{1,0:T(8,128)(2,1)}, /*index=5*/f32[8,768]{1,0:T(8,128)}) custom-call(bf16[1792,768]{1,0:T(8,128)(2,1)} %bitcast.102, bf16[1792,768]{1,0:T(8,128)(2,1)} %bitcast.101, f32[832,768]{1,0:T(8,128)} %bitcast.108, ...), custom_call_target="tpu_custom_call" | custom-call | flops 8000000000 | bytes 25000000 | tf_op jit(solution)/shard_map/combine/pallas_call | solution.py:392
  408.8 52.2 %back.1 = (f32[832,768]{1,0:T(8,128)}, bf16[768,3200]{1,0:T(8,128)(2,1)}) custom-call(f32[832,768]{1,0:T(8,128)} %bitcast.106, bf16[832,2304]{1,0:T(8,128)(2,1)} %get-tuple-element.51.qkv_ref, bf16[832,768]{1,0:T(8,128)(2,1)} %get-tuple-element.52.datt_ref, f32[832,768]{1,0:T(8,128)} %get-tuple-element.53.dhid_ref, ...), custom_call_target="tpu_custom_call" | custom-call | flops 15000000512 | bytes 35000000 | tf_op jit(solution)/shard_map/back/pallas_call | solution.py:485
  464.3 16.0 %down.3 = bf16[1536,768]{1,0:T(8,128)(2,1)} custom-call(s32[1]{0:T(128)} %bitcast.38.p_ref, bf16[1792,768]{1,0:T(8,128)(2,1)} %bitcast.92, bf16[1792,768]{1,0:T(8,128)(2,1)} %get-tuple-element.43.refs_1_.grad_ref, bf16[768,3072]{1,0:T(8,128)(2,1)} %dynamic-slice_bitcast_fusion.1.refs_2_.up_ref, f32[1,3072]{1,0:T(1,128)} %dynamic-slice_convert_fusion.5.refs_3_.shift_ref), custom_call_target="tpu_custom_call" | custom-call | flops 8455716864 | bytes 10223616 | tf_op jit(solution)/shard_map/down/pallas_call | solution.py:252
  482.1 12.1 %collective-permute-start.13 = (bf16[768,768]{1,0:T(8,128)(2,1)S(1)}, bf16[768,768]{1,0:T(8,128)(2,1)S(1)}, u32[]{:S(2)}, u32[]{:S(2)}) collective-permute-start(bf16[768,768]{1,0:T(8,128)(2,1)S(1)} %get-tuple-element.162), channel_id=1, source_target_pairs={{0,16},{16,0},{1,17},{17,1},{2,18},{18,2},{3,19},{19,3},{4,20},{20... | collective-permute-start | bytes 3538952 | tf_op jit(solution)/shard_map/ppermute | solution.py:513
  504.7 92.2 %collective-permute-done.13 = bf16[768,768]{1,0:T(8,128)(2,1)S(1)} collective-permute-done((bf16[768,768]{1,0:T(8,128)(2,1)S(1)}, bf16[768,768]{1,0:T(8,128)(2,1)S(1)}, u32[]{:S(2)}, u32[]{:S(2)}) %collective-permute-start.13) | collective-permute-done | bytes 1179680 | tf_op jit(solution)/shard_map/ppermute | solution.py:513
  597.8 49.6 %collective-permute-done.6 = bf16[192,3072]{1,0:T(8,128)(2,1)S(1)} collective-permute-done((bf16[192,3072]{1,0:T(8,128)(2,1)S(1)}, bf16[192,3072]{1,0:T(8,128)(2,1)S(1)}, u32[]{:S(2)}, u32[]{:S(2)}) %collective-permute-start.6) | collective-permute-done | bytes 1179680 | tf_op jit(solution)/shard_map/ppermute | solution.py:513
  649.8 22.8 %collective-permute-done.14 = bf16[768,768]{1,0:T(8,128)(2,1)S(1)} collective-permute-done((bf16[768,768]{1,0:T(8,128)(2,1)S(1)}, bf16[768,768]{1,0:T(8,128)(2,1)S(1)}, u32[]{:S(2)}, u32[]{:S(2)}) %collective-permute-start.14) | collective-permute-done | bytes 1179680 | tf_op jit(solution)/shard_map/ppermute | solution.py:513
  675.8 4.1 collective-permute-start.4
  (122 shorter events, 72.5 us)
Async XLA Ops:
  7.2 11.2 %copy-start.7 = (s32[788,2]{0,1:T(2,128)S(1)}, s32[788,2]{0,1:T(2,128)}, u32[]{:S(2)}) copy-start(s32[788,2]{0,1:T(2,128)} %param.20) | copy-start | bytes 18916
  7.2 11.2 %copy-start.10 = (s32[788,2]{0,1:T(2,128)S(1)}, s32[788,2]{0,1:T(2,128)}, u32[]{:S(2)}) copy-start(s32[788,2]{0,1:T(2,128)} %param.21) | copy-start | bytes 18916
  7.2 96.3 %all-gather.2.cloned.1.call-start = ((), (), s32[]{:S(2)}) async-start(), calls=%async_computation.3 | async-start | bytes 5068800 | tf_op jit(solution)/shard_map/all_gather | solution.py:601
  13.3 8.0 %copy-start.3 = (f32[788,768]{1,0:T(8,128)S(1)}, f32[788,768]{1,0:T(8,128)}, u32[]{:S(2)}) copy-start(f32[788,768]{1,0:T(8,128)} %param.19) | copy-start | bytes 7262212
  37.2 112.5 %all-to-all-start.1 = ((bf16[16,112,768]{2,1,0:T(8,128)(2,1)}), bf16[16,112,768]{2,1,0:T(8,128)(2,1)S(1)}, u32[]{:S(2)}, u32[]{:S(2)}) async-start(bf16[16,112,768]{2,1,0:T(8,128)(2,1)} %bitcast.100), calls=%async_computation.1 | async-start | bytes 5505024 | tf_op jit(solution)/shard_map/all_to_all | solution.py:593
  151.2 43.3 %all-to-all-start = ((bf16[16,112,768]{2,1,0:T(8,128)(2,1)}), bf16[16,112,768]{2,1,0:T(8,128)(2,1)S(1)}, u32[]{:S(2)}, u32[]{:S(2)}) async-start(bf16[16,112,768]{2,1,0:T(8,128)(2,1)} %bitcast.99), calls=%async_computation | async-start | bytes 5505024 | tf_op jit(solution)/shard_map/all_to_all | solution.py:593
  282.6 7.3 %copy-start.11 = (f32[1,768]{1,0:T(1,128)S(1)}, f32[1,768]{1,0:T(1,128)}, u32[]{:S(2)}) copy-start(f32[1,768]{1,0:T(1,128)} %get-tuple-element.62) | copy-start | bytes 9220
  282.6 99.6 %all-to-all-start.2 = ((bf16[16,224,768]{2,1,0:T(8,128)(2,1)}), bf16[16,224,768]{2,1,0:T(8,128)(2,1)}, u32[]{:S(2)}, u32[]{:S(2)}) async-start(bf16[16,224,768]{2,1,0:T(8,128)(2,1)} %pad_maximum_fusion), calls=%async_computation.2 | async-start | bytes 11010048 | tf_op jit(solution)/shard_map/all_to_all | solution.py:593
  290.0 192.1 %collective-permute-start.10 = (f32[1,3840]{1,0:T(1,128)S(1)}, f32[1,3840]{1,0:T(1,128)S(1)}, u32[]{:S(2)}, u32[]{:S(2)}) collective-permute-start(f32[1,3840]{1,0:T(1,128)S(1)} %constant_dynamic-update-slice_fusion), channel_id=1, source_target_pairs={{0,16},{8,24},{16,0},{24,8},{1,17},{9,25},{17,1},{25,9},{2,18},{10... | collective-permute-start | bytes 46088 | tf_op jit(solution)/shard_map/ppermute | solution.py:513
  290.6 203.6 %collective-permute-start.11 = (f32[1,3840]{1,0:T(1,128)S(1)}, f32[1,3840]{1,0:T(1,128)S(1)}, u32[]{:S(2)}, u32[]{:S(2)}) collective-permute-start(f32[1,3840]{1,0:T(1,128)S(1)} %constant_dynamic-update-slice_fusion), channel_id=1, source_target_pairs={{0,24},{8,0},{16,8},{24,16},{1,25},{9,1},{17,9},{25,17},{2,26},{10... | collective-permute-start | bytes 46088 | tf_op jit(solution)/shard_map/ppermute | solution.py:513
  294.2 200.1 %collective-permute-start.9 = (f32[1,3840]{1,0:T(1,128)S(1)}, f32[1,3840]{1,0:T(1,128)S(1)}, u32[]{:S(2)}, u32[]{:S(2)}) collective-permute-start(f32[1,3840]{1,0:T(1,128)S(1)} %constant_dynamic-update-slice_fusion), channel_id=1, source_target_pairs={{0,8},{8,16},{16,24},{24,0},{1,9},{9,17},{17,25},{25,1},{2,10},{10... | collective-permute-start | bytes 46088 | tf_op jit(solution)/shard_map/ppermute | solution.py:513
  297.0 201.0 %collective-permute-start.7 = (bf16[192,3072]{1,0:T(8,128)(2,1)}, bf16[192,3072]{1,0:T(8,128)(2,1)}, u32[]{:S(2)}, u32[]{:S(2)}) collective-permute-start(bf16[192,3072]{1,0:T(8,128)(2,1)} %get-tuple-element.160), channel_id=1, source_target_pairs={{0,16},{16,0},{1,17},{17,1},{2,18},{18,2},{3,19},{19,3},{4,20},{20... | collective-permute-start | bytes 3538952 | tf_op jit(solution)/shard_map/ppermute | solution.py:513
  464.2 37.4 %collective-permute-start = (bf16[4,4,24,3200]{3,2,1,0:T(8,128)(2,1)}, bf16[4,4,24,3200]{3,2,1,0:T(8,128)(2,1)S(1)}, u32[]{:S(2)}, u32[]{:S(2)}) collective-permute-start(bf16[4,4,24,3200]{3,2,1,0:T(8,128)(2,1)} %dynamic-slice_bitcast_fusion.2), channel_id=1, source_target_pairs={{0,1},{1,0},{2,3},{3,2},{4,5},{5,4},{6,7},{7,6},{8,9},{9,8},{10,11... | collective-permute-start | bytes 7372808 | tf_op jit(solution)/shard_map/ppermute | solution.py:559
  482.1 114.8 %collective-permute-start.13 = (bf16[768,768]{1,0:T(8,128)(2,1)S(1)}, bf16[768,768]{1,0:T(8,128)(2,1)S(1)}, u32[]{:S(2)}, u32[]{:S(2)}) collective-permute-start(bf16[768,768]{1,0:T(8,128)(2,1)S(1)} %get-tuple-element.162), channel_id=1, source_target_pairs={{0,16},{16,0},{1,17},{17,1},{2,18},{18,2},{3,19},{19,3},{4,20},{20... | collective-permute-start | bytes 3538952 | tf_op jit(solution)/shard_map/ppermute | solution.py:513
  494.2 155.5 %collective-permute-start.12 = (bf16[768,768]{1,0:T(8,128)(2,1)S(1)}, bf16[768,768]{1,0:T(8,128)(2,1)S(1)}, u32[]{:S(2)}, u32[]{:S(2)}) collective-permute-start(bf16[768,768]{1,0:T(8,128)(2,1)S(1)} %get-tuple-element.161), channel_id=1, source_target_pairs={{0,16},{16,0},{1,17},{17,1},{2,18},{18,2},{3,19},{19,3},{4,20},{20... | collective-permute-start | bytes 3538952 | tf_op jit(solution)/shard_map/ppermute | solution.py:513
  494.3 153.0 %collective-permute-start.6 = (bf16[192,3072]{1,0:T(8,128)(2,1)S(1)}, bf16[192,3072]{1,0:T(8,128)(2,1)S(1)}, u32[]{:S(2)}, u32[]{:S(2)}) collective-permute-start(bf16[192,3072]{1,0:T(8,128)(2,1)S(1)} %get-tuple-element.159), channel_id=1, source_target_pairs={{0,16},{16,0},{1,17},{17,1},{2,18},{18,2},{3,19},{19,3},{4,20},{20... | collective-permute-start | bytes 3538952 | tf_op jit(solution)/shard_map/ppermute | solution.py:513
  500.0 147.3 %collective-permute-start.8 = (bf16[192,3072]{1,0:T(8,128)(2,1)S(1)}, bf16[192,3072]{1,0:T(8,128)(2,1)S(1)}, u32[]{:S(2)}, u32[]{:S(2)}) collective-permute-start(bf16[192,3072]{1,0:T(8,128)(2,1)S(1)} %fusion.5), channel_id=1, source_target_pairs={{0,8},{8,0},{1,9},{9,1},{2,10},{10,2},{3,11},{11,3},{4,12},{12,4},... | collective-permute-start | bytes 3538952 | tf_op jit(solution)/shard_map/ppermute | solution.py:513
  503.8 93.1 %copy-start.5 = (bf16[1536,768]{1,0:T(8,128)(2,1)S(1)}, bf16[1536,768]{1,0:T(8,128)(2,1)}, u32[]{:S(2)}) copy-start(bf16[1536,768]{1,0:T(8,128)(2,1)} %down.3) | copy-start | bytes 7077892
  504.0 145.4 %collective-permute-start.1 = (bf16[4,2,24,3200]{3,2,1,0:T(8,128)(2,1)S(1)}, bf16[4,2,24,3200]{3,2,1,0:T(8,128)(2,1)S(1)}, u32[]{:S(2)}, u32[]{:S(2)}) collective-permute-start(bf16[4,2,24,3200]{3,2,1,0:T(8,128)(2,1)S(1)} %fusion.6), channel_id=1, source_target_pairs={{0,2},{1,3},{2,0},{3,1},{4,6},{5,7},{6,4},{7,5},{8,10},{9,11},{10,... | collective-permute-start | bytes 3686408 | tf_op jit(solution)/shard_map/ppermute | solution.py:559
  597.2 75.3 %collective-permute-start.14 = (bf16[768,768]{1,0:T(8,128)(2,1)S(1)}, bf16[768,768]{1,0:T(8,128)(2,1)S(1)}, u32[]{:S(2)}, u32[]{:S(2)}) collective-permute-start(bf16[768,768]{1,0:T(8,128)(2,1)S(1)} %fusion.4), channel_id=1, source_target_pairs={{0,8},{8,0},{1,9},{9,1},{2,10},{10,2},{3,11},{11,3},{4,12},{12,4},... | collective-permute-start | bytes 3538952 | tf_op jit(solution)/shard_map/ppermute | solution.py:513
  649.7 25.8 %collective-permute-start.2 = (bf16[4,1,24,3200]{3,2,1,0:T(8,128)(2,1)S(1)}, bf16[4,1,24,3200]{3,2,1,0:T(8,128)(2,1)S(1)}, u32[]{:S(2)}, u32[]{:S(2)}) collective-permute-start(bf16[4,1,24,3200]{3,2,1,0:T(8,128)(2,1)S(1)} %dynamic-slice_convert_fusion.1), channel_id=1, source_target_pairs={{0,4},{1,5},{2,6},{3,7},{4,0},{5,1},{6,2},{7,3},{8,12},{9,13},{10,... | collective-permute-start | bytes 1843208 | tf_op jit(solution)/shard_map/ppermute | solution.py:559
  675.7 12.9 %collective-permute-start.3 = (bf16[24,3200]{1,0:T(8,128)(2,1)S(1)}, bf16[24,3200]{1,0:T(8,128)(2,1)S(1)}, u32[]{:S(2)}, u32[]{:S(2)}) collective-permute-start(bf16[24,3200]{1,0:T(8,128)(2,1)S(1)} %get-tuple-element.163), channel_id=1, source_target_pairs={{0,8},{8,16},{16,24},{24,0},{1,9},{9,17},{17,25},{25,1},{2,10},{10... | collective-permute-start | bytes 460808 | tf_op jit(solution)/shard_map/ppermute | solution.py:513
  675.8 14.4 %collective-permute-start.4 = (bf16[24,3200]{1,0:T(8,128)(2,1)S(1)}, bf16[24,3200]{1,0:T(8,128)(2,1)S(1)}, u32[]{:S(2)}, u32[]{:S(2)}) collective-permute-start(bf16[24,3200]{1,0:T(8,128)(2,1)S(1)} %get-tuple-element.165), channel_id=1, source_target_pairs={{0,16},{8,24},{16,0},{24,8},{1,17},{9,25},{17,1},{25,9},{2,18},{10... | collective-permute-start | bytes 460808 | tf_op jit(solution)/shard_map/ppermute | solution.py:513
  679.8 10.3 %collective-permute-start.5 = (bf16[24,3200]{1,0:T(8,128)(2,1)S(1)}, bf16[24,3200]{1,0:T(8,128)(2,1)S(1)}, u32[]{:S(2)}, u32[]{:S(2)}) collective-permute-start(bf16[24,3200]{1,0:T(8,128)(2,1)S(1)} %get-tuple-element.164), channel_id=1, source_target_pairs={{0,24},{8,0},{16,8},{24,16},{1,25},{9,1},{17,9},{25,17},{2,26},{10... | collective-permute-start | bytes 460808 | tf_op jit(solution)/shard_map/ppermute | solution.py:513
  (8 other events, 35.2 us)
Sparse Core Ops, SparseCore 0:
  18.5 84.9 all-gather.1

commit v3 on v2

--- a/solution.py
+++ b/solution.py
@@ -62,12 +62,30 @@
     return pl.ds(pl.multiple_of(index * size, size), size)
 
 
+def pad_rows(source_ref, padded_ref):
+    width = source_ref.shape[1]
+    for i in range(source_ref.shape[0] // SEQ):
+        padded_ref[i * SEQ_PAD : i * SEQ_PAD + SEQ, :] = source_ref[i * SEQ : (i + 1) * SEQ, :]
+        padded_ref[i * SEQ_PAD + SEQ : (i + 1) * SEQ_PAD, :] = jnp.zeros((SEQ_PAD - SEQ, width), f32)
+
+
+def unpad_rows(padded_ref, out_ref):
+    for i in range(out_ref.shape[0] // SEQ):
+        out_ref[i * SEQ : (i + 1) * SEQ, :] = padded_ref[i * SEQ_PAD : i * SEQ_PAD + SEQ, :]
+
+
 def front_kernel(
-    experts, x_ref, w_ref, small_ref, bias_ref, vec_ref, spots_ref,
-    qkv_ref, att_ref, hid_ref, sec_ref, probs_ref, send_ref, first_ref,
+    experts, source_ref, w_ref, small_ref, spots_ref,
+    qkv_ref, att_ref, hid_ref, sec_ref, probs_ref, send_ref, vec_ref, x_ref, first_ref, bias_ref,
 ):
     rows, width = x_ref.shape
     col = 256
+    pad_rows(source_ref, x_ref)
+    turned = jnp.transpose(small_ref[...].astype(f32), (1, 0))
+    vec_ref[...] = pltpu.roll(turned, LANES - experts, 0)[0:8, :]
+    bias_ref[:, :width] = vec_ref[0:1, :]
+    bias_ref[:, width : 2 * width] = jnp.zeros((1, width), f32)
+    bias_ref[:, 2 * width :] = vec_ref[1:2, :]
     gain_one, shift_one = vec_ref[3:4, :], vec_ref[4:5, :]
     gain_two, shift_two = vec_ref[5:6, :], vec_ref[6:7, :]
 
@@ -83,10 +101,13 @@
     def _(j):
         at = tile_of(j, col)
         got = dot(first_ref[...], w_ref[:, at]) + bias_ref[:, at]
+        got = got * jnp.where(j < width // col, head_scale, 1.0)
         qkv_ref[:, at] = jnp.where(valid, got, 0.0).astype(bf16)
 
     low = iota((1, LANES), 1) < HEAD
-    keys = iota((1, SEQ_PAD), 1) < SEQ
+    keys = jnp.where(iota((SEQ_PAD, 1), 0) < SEQ, 1.0, 0.0).astype(bf16)
+    ones_low = jnp.where(low, keys, jnp.zeros_like(keys))
+    ones_high = jnp.where(low, jnp.zeros_like(keys), keys)
     pairs = width // LANES
 
     @pl.loop(0, (rows // SEQ_PAD) * pairs)
@@ -96,13 +117,13 @@
         q = qkv_ref[at, pl.ds(pl.multiple_of(lane, LANES), LANES)]
         k = qkv_ref[at, pl.ds(pl.multiple_of(width + lane, LANES), LANES)]
         v = qkv_ref[at, pl.ds(pl.multiple_of(2 * width + lane, LANES), LANES)]
-        parts = []
-        for side in (low, ~low):
-            scores = dot_nt(jnp.where(side, q, jnp.zeros_like(q)), k) * head_scale
-            weights = jnp.where(keys, jnp.exp(scores), 0.0)
-            weights = weights * (1.0 / jnp.sum(weights, axis=-1, keepdims=True))
-            parts.append(dot(weights.astype(bf16), v))
-        att_ref[at, pl.ds(pl.multiple_of(lane, LANES), LANES)] = jnp.where(low, *parts).astype(bf16)
+        zero = jnp.zeros_like(q)
+        grown = jnp.exp(dot_nt(jnp.where(low, q, zero), k)).astype(bf16)
+        first = dot(grown, jnp.where(low, v, ones_high))
+        grown = jnp.exp(dot_nt(jnp.where(low, zero, q), k)).astype(bf16)
+        second = dot(grown, jnp.where(low, ones_low, v))
+        sums = pltpu.roll(jnp.where(low, second, first), HEAD, 1)
+        att_ref[at, pl.ds(pl.multiple_of(lane, LANES), LANES)] = (jnp.where(low, first, second) / sums).astype(bf16)
 
     @pl.loop(0, width // col)
     def _(j):
@@ -136,9 +157,145 @@
         send_ref[tile_of(d, block), :] = dot(jnp.where(hit, 1.0, 0.0).astype(bf16), rows_ref[...]).astype(bf16)
 
 
-def place_kernel(spots_ref, rows_ref, send_ref, held_ref):
-    held_ref[...] = rows_ref[...].astype(bf16)
-    place_rows(spots_ref, held_ref, send_ref)
+def flipped(index, mask):
+    return index + mask - 2 * mask * ((index // mask) % 2)
+
+
+def gather_kernel(
+    outer, fan, qkv_ref, out_ref, small_ref, cot_ref, spots_ref,
+    w_ref, all_small_ref, send_ref, held_ref, held_small_ref, cot_pad_ref, cot_low_ref, send_sem, recv_sem, local_sem,
+):
+    members = outer * fan
+    high, low, spot = lax.axis_index("hi"), lax.axis_index("lo"), lax.axis_index("expert")
+    me = high * fan + low
+    rows, cols = held_ref.shape
+    mine = spot % 8
+    in_qkv = qkv_ref.shape[1] // cols
+    mesh_id = pl.DeviceIdType.MESH
+
+    def member(step):
+        to = (me + step) % members
+        return (to // fan, to % fan, spot)
+
+    def near(mask):
+        return (high, low, flipped(spot, mask))
+
+    barrier = pltpu.get_barrier_semaphore()
+    peers = [member(s) for s in range(1, members)] + [near(b) for b in (4, 2, 1)]
+    for peer in peers:
+        pl.semaphore_signal(barrier, inc=1, device_id=peer, device_id_type=mesh_id)
+
+    @pl.when(mine < in_qkv)
+    def _():
+        span = pl.ds(pl.multiple_of(mine * cols, cols), cols)
+        copy = pltpu.make_async_copy(qkv_ref.at[:, span], held_ref, local_sem.at[0])
+        copy.start()
+        copy.wait()
+
+    @pl.when(mine >= in_qkv)
+    def _():
+        span = pl.ds(pl.multiple_of((mine - in_qkv) * cols, cols), cols)
+        copy = pltpu.make_async_copy(out_ref.at[:, span], held_ref, local_sem.at[0])
+        copy.start()
+        copy.wait()
+
+    copy = pltpu.make_async_copy(small_ref, held_small_ref, local_sem.at[1])
+    copy.start()
+    copy.wait()
+    pl.semaphore_wait(barrier, len(peers))
+
+    def block(step, masks):
+        source = (me - step + members) % members
+        span = mine
+        for mask in masks:
+            span = flipped(span, mask)
+        return w_ref.at[
+            pl.ds(pl.multiple_of(source * rows, rows), rows), pl.ds(pl.multiple_of(span * cols, cols), cols)
+        ]
+
+    copies = []
+
+    def send(source, target, device):
+        k = len(copies)
+        copies.append(
+            pltpu.make_async_remote_copy(
+                src_ref=source, dst_ref=target, send_sem=send_sem.at[k], recv_sem=recv_sem.at[k],
+                device_id=device, device_id_type=mesh_id,
+            )
+        )
+        copies[-1].start()
+        return copies[-1]
+
+    stay = [
+        pltpu.make_async_copy(held_ref, block(0, ()), local_sem.at[0]),
+        pltpu.make_async_copy(
+            held_small_ref, all_small_ref.at[pl.ds(pl.multiple_of(me * rows, rows), rows), :], local_sem.at[1]
+        ),
+    ]
+    own = all_small_ref.at[pl.ds(pl.multiple_of(me * rows, rows), rows), :]
+    over = [None] + [send(held_ref, block(0, ()), member(s)) for s in range(1, members)]
+    near_by = [{b: send(held_ref, block(0, ()), near(b)) for b in (4, 2, 1)}]
+    late = [send(held_small_ref, own, member(s)) for s in range(1, members)]
+    for copy in stay:
+        copy.start()
+    for s in range(1, members):
+        over[s].wait_recv()
+        near_by.append({b: send(block(s, ()), block(s, ()), near(b)) for b in (4, 2, 1)})
+
+    pad_rows(cot_ref, cot_pad_ref)
+    cot_low_ref[...] = cot_pad_ref[...].astype(bf16)
+    place_rows(spots_ref, cot_low_ref, send_ref)
+
+    relays = []
+    for s in range(members):
+        first, second = (4, 2) if s % 2 == 0 else (2, 4)
+        near_by[s][first].wait_recv()
+        relays.append(send(block(s, (first,)), block(s, (first,)), near(second)))
+        late.append(send(block(s, (first,)), block(s, (first,)), near(1)))
+        near_by[s][second].wait_recv()
+        late.append(send(block(s, (second,)), block(s, (second,)), near(1)))
+    for s in range(members):
+        relays[s].wait_recv()
+        late.append(send(block(s, (4, 2)), block(s, (4, 2)), near(1)))
+    for s in range(members):
+        near_by[s][1].wait_recv()
+    for copy in late:
+        copy.wait_recv()
+    for copy in copies:
+        copy.wait_send()
+    for copy in stay:
+        copy.wait()
+
+
+def gather_call(outer, fan, total, qkv, out, small, cot, spots):
+    rows, width = out.shape
+    members = outer * fan
+    cols = 4 * width // 8
+    count = 2 * (members - 1) + 3 * members + 4 * members
+    anywhere = pl.BlockSpec(memory_space=pl.ANY)
+    padded = cot.shape[0] // SEQ * SEQ_PAD
+    return pl.pallas_call(
+        functools.partial(gather_kernel, outer, fan),
+        out_shape=(
+            jax.ShapeDtypeStruct((members * rows, 4 * width), bf16),
+            jax.ShapeDtypeStruct((members * rows, LANES), bf16),
+            jax.ShapeDtypeStruct((total, width), bf16),
+        ),
+        in_specs=[anywhere] * 3 + whole(2),
+        out_specs=(anywhere, anywhere, whole(1)[0]),
+        scratch_shapes=[
+            pltpu.VMEM((rows, cols), bf16),
+            pltpu.VMEM((rows, LANES), bf16),
+            pltpu.VMEM((padded, width), f32),
+            pltpu.VMEM((padded, width), bf16),
+            pltpu.SemaphoreType.DMA((count,)),
+            pltpu.SemaphoreType.DMA((count,)),
+            pltpu.SemaphoreType.DMA((2,)),
+        ],
+        compiler_params=params(collective_id=0, has_side_effects=True),
+        cost_estimate=pl.CostEstimate(flops=25 * 10**8, bytes_accessed=40 * 10**6, transcendentals=0),
+        name="gather",
+    )(qkv, out, small, cot, spots)
 
 
 def whole(n):
@@ -149,22 +306,9 @@
     return pltpu.CompilerParams(vmem_limit_bytes=VMEM_MAX, **more)
 
 
-def place_call(spots, values, total):
-    rows, width = values.shape
-    return pl.pallas_call(
-        place_kernel,
-        out_shape=jax.ShapeDtypeStruct((total, width), bf16),
-        in_specs=whole(2),
-        out_specs=whole(1)[0],
-        scratch_shapes=[pltpu.VMEM((rows, width), bf16)],
-        compiler_params=params(),
-        cost_estimate=pl.CostEstimate(flops=2 * total * rows * width, bytes_accessed=rows * width * 4 + total * width * 2, transcendentals=0),
-        name="place",
-    )(spots, values)
-
-
-def front_call(experts, total, x, weights, small, bias, vec, spots):
-    rows, width = x.shape
+def front_call(experts, total, x, weights, small, spots):
+    width = x.shape[1]
+    rows = x.shape[0] // SEQ * SEQ_PAD
     shapes = (
         jax.ShapeDtypeStruct((rows, 3 * width), bf16),
         jax.ShapeDtypeStruct((rows, width), bf16),
@@ -172,17 +316,22 @@
         jax.ShapeDtypeStruct((rows, width), bf16),
         jax.ShapeDtypeStruct((rows, LANES), f32),
         jax.ShapeDtypeStruct((total, width), bf16),
+        jax.ShapeDtypeStruct((8, width), f32),
     )
     return pl.pallas_call(
         functools.partial(front_kernel, experts),
         out_shape=shapes,
-        in_specs=whole(6),
-        out_specs=tuple(whole(6)),
-        scratch_shapes=[pltpu.VMEM((rows, width), bf16)],
+        in_specs=whole(4),
+        out_specs=tuple(whole(7)),
+        scratch_shapes=[
+            pltpu.VMEM((rows, width), f32),
+            pltpu.VMEM((rows, width), bf16),
+            pltpu.VMEM((1, 3 * width), f32),
+        ],
         compiler_params=params(),
         cost_estimate=pl.CostEstimate(flops=14 * 10**9, bytes_accessed=30 * 10**6, transcendentals=2 * 10**6),
         name="front",
-    )(x, weights, small, bias, vec, spots)
+    )(x, weights, small, spots)
 
 
 def gelu_parts(pre_act):
@@ -195,7 +344,7 @@
     mine = lane == which_ref[0]
     total = jnp.zeros((1, cot_ref.shape[1]), f32)
     rows = x_ref.shape[0]
-    size = 128
+    size = rows // 4
 
     def step(t, total):
         at = tile_of(t, size)
@@ -221,7 +370,8 @@
     )(which, rows_in, cot, small)
 
 
-def down_kernel(x_ref, grad_ref, up_ref, shift_ref, out_ref, act_ref):
+def down_kernel(steps, x_ref, grad_ref, up_ref, shift_ref, *refs):
+    *out_refs, act_ref = refs
     rows = x_ref.shape[0]
     size = rows // 4
 
@@ -230,43 +380,52 @@
         at = tile_of(t, size)
         act_ref[at, :] = gelu_parts(dot(x_ref[at, :], up_ref[...]) + shift_ref[...])[0].astype(bf16)
 
-    out_ref[...] = dot_tn(act_ref[...], grad_ref[...]).astype(bf16)
-
-
-def down_call(x, grads, up, shift, tile, part, parts):
+    got = dot_tn(act_ref[...], grad_ref[...]).astype(bf16)
+    for i, out_ref in enumerate(out_refs):
+
+        @pl.when(pl.program_id(0) // steps == i)
+        def _(out_ref=out_ref):
+            out_ref[...] = got
+
+
+def down_call(x, grads, up, shift, where, members):
     rows, width = x.shape
-    span = up.shape[1] // parts
+    span = up.shape[1] // members
+    tile = 384 if span % 384 == 0 else span
     steps = span // tile
+    count = where.shape[0]
     grid = pltpu.PrefetchScalarGridSpec(
         num_scalar_prefetch=1,
-        grid=(steps,),
+        grid=(count * steps,),
         in_specs=[
             pl.BlockSpec((rows, width), lambda j, p: (0, 0)),
             pl.BlockSpec((rows, width), lambda j, p: (0, 0)),
-            pl.BlockSpec((width, tile), lambda j, p: (0, p[0] * steps + j)),
-            pl.BlockSpec((1, tile), lambda j, p: (0, p[0] * steps + j)),
-        ],
-        out_specs=pl.BlockSpec((tile, width), lambda j, p: (j, 0)),
+            pl.BlockSpec((width, tile), lambda j, p: (0, p[j // steps] * steps + j % steps)),
+            pl.BlockSpec((1, tile), lambda j, p: (0, p[j // steps] * steps + j % steps)),
+        ],
+        out_specs=[
+            pl.BlockSpec((tile, width), lambda j, p, i=i: (jnp.clip(j - i * steps, 0, steps - 1), 0))
+            for i in range(count)
+        ],
         scratch_shapes=[pltpu.VMEM((rows, tile), bf16)],
     )
     return pl.pallas_call(
-        lambda p_ref, *refs: down_kernel(*refs),
-        out_shape=jax.ShapeDtypeStruct((span, width), bf16),
+        lambda p_ref, *refs: down_kernel(steps, *refs),
+        out_shape=[jax.ShapeDtypeStruct((span, width), bf16)] * count,
         grid_spec=grid,
         compiler_params=params(dimension_semantics=("arbitrary",)),
-        cost_estimate=pl.CostEstimate(flops=4 * rows * width * span, bytes_accessed=4 * rows * width + 4 * span * width, transcendentals=rows * span),
+        cost_estimate=pl.CostEstimate(flops=4 * rows * width * span * count, bytes_accessed=4 * rows * width + 4 * span * width * count, transcendentals=rows * span),
         name="down",
-    )(part, x, grads, up, shift)
-
-
-def expert_kernel(
-    x_ref, grad_ref, up_ref, shift_ref, down_ref, down_shift_ref,
-    upg_ref, upsum_ref, out_ref, rows_ref, pre_ref, dpre_ref, out_acc, rows_acc,
-):
+    )(where, x, grads, up, shift)
+
+
+def expert_kernel(where_ref, x_ref, grad_ref, up_ref, shift_ref, down_ref, down_shift_ref, *refs):
+    *upg_refs, upsum_ref, both_ref, dpre_ref, upg_ref, out_acc, rows_acc = refs
     j = pl.program_id(0)
-    rows, _ = x_ref.shape
+    rows, width = x_ref.shape
     tile = up_ref.shape[1]
     size = rows // 4
+    span = width // len(upg_refs)
 
     @pl.when(j == 0)
     def _():
@@ -287,58 +446,73 @@
 
     upsum_ref[...] = lax.fori_loop(0, 4, step, jnp.zeros((1, tile), f32))
     upg_ref[...] = dot_tn(x_ref[...], dpre_ref[...]).astype(bf16)
+    for i, ref in enumerate(upg_refs):
+        ref[...] = upg_ref[pl.ds(pl.multiple_of(where_ref[i] * span, span), span), :]
 
     @pl.when(j == pl.num_programs(0) - 1)
     def _():
-        out_ref[...] = out_acc[...].astype(bf16)
-        rows_ref[...] = rows_acc[...].astype(bf16)
-
-
-def expert_call(x, grads, up, shift, down, down_shift, tile):
+        experts, _, slots, _ = both_ref.shape
+
+        @pl.loop(0, experts)
+        def _(e):
+            at = tile_of(e, slots)
+            both_ref[e, 0] = out_acc[at, :].astype(bf16)
+            both_ref[e, 1] = rows_acc[at, :].astype(bf16)
+
+
+def expert_call(x, grads, up, shift, down, down_shift, where, experts, tile):
     rows, width = x.shape
     hidden = up.shape[1]
-    fixed = lambda *shape: pl.BlockSpec(shape, lambda j: (0, 0))
-    return pl.pallas_call(
-        expert_kernel,
-        out_shape=(
-            jax.ShapeDtypeStruct((width, hidden), bf16),
-            jax.ShapeDtypeStruct((1, hidden), f32),
-            jax.ShapeDtypeStruct((rows, width), bf16),
-            jax.ShapeDtypeStruct((rows, width), bf16),
-        ),
+    count = where.shape[0]
+    fixed = lambda *shape: pl.BlockSpec(shape, lambda j, p: (0,) * len(shape))
+    both = (experts, 2, rows // experts, width)
+    grid = pltpu.PrefetchScalarGridSpec(
+        num_scalar_prefetch=1,
         grid=(hidden // tile,),
         in_specs=[
             fixed(rows, width),
             fixed(rows, width),
-            pl.BlockSpec((width, tile), lambda j: (0, j)),
-            pl.BlockSpec((1, tile), lambda j: (0, j)),
-            pl.BlockSpec((tile, width), lambda j: (j, 0)),
+            pl.BlockSpec((width, tile), lambda j, p: (0, j)),
+            pl.BlockSpec((1, tile), lambda j, p: (0, j)),
+            pl.BlockSpec((tile, width), lambda j, p: (j, 0)),
             fixed(1, width),
         ],
-        out_specs=(
-            pl.BlockSpec((width, tile), lambda j: (0, j)),
-            pl.BlockSpec((1, tile), lambda j: (0, j)),
-            fixed(rows, width),
-            fixed(rows, width),
-        ),
+        out_specs=[pl.BlockSpec((width // count, tile), lambda j, p: (0, j))] * count
+        + [pl.BlockSpec((1, tile), lambda j, p: (0, j)), fixed(*both)],
         scratch_shapes=[
-            pltpu.VMEM((8, LANES), f32),
             pltpu.VMEM((rows, tile), bf16),
+            pltpu.VMEM((width, tile), bf16),
             pltpu.VMEM((rows, width), f32),
             pltpu.VMEM((rows, width), f32),
         ],
+    )
+    got = pl.pallas_call(
+        expert_kernel,
+        out_shape=[jax.ShapeDtypeStruct((width // count, hidden), bf16)] * count
+        + [jax.ShapeDtypeStruct((1, hidden), f32), jax.ShapeDtypeStruct(both, bf16)],
+        grid_spec=grid,
         compiler_params=params(dimension_semantics=("arbitrary",)),
         cost_estimate=pl.CostEstimate(flops=10 * rows * width * hidden, bytes_accessed=8 * rows * width + 6 * hidden * width, transcendentals=2 * rows * hidden),
         name="expert",
-    )(x, grads, up, shift, down, down_shift)
+    )(where, x, grads, up, shift, down, down_shift)
+    return got[:count], got[count], got[count + 1]
 
 
 def combine_kernel(
-    outs_ref, back_ref, cot_ref, hid_ref, sec_ref, probs_ref, spots_ref, ids_ref, w_ref, small_ref, vec_ref,
-    blk_ref, dhid_ref, dhb_ref, datt_ref, dlog_ref, sums_ref,
+    both_ref, source_ref, hid_ref, probs_ref, spots_ref, ids_ref, w_ref, small_ref, vec_ref,
+    block_ref, dhid_ref, dhb_ref, datt_ref, dlog_ref, sums_ref, outs_ref, back_ref, cot_ref, blk_ref,
 ):
     rows, width = cot_ref.shape
     total = outs_ref.shape[0]
+    experts, _, slots, _ = both_ref.shape
+    pad_rows(source_ref, cot_ref)
+
+    @pl.loop(0, experts)
+    def _(e):
+        at = tile_of(e, slots)
+        outs_ref[at, :] = both_ref[e, 0]
+        back_ref[at, :] = both_ref[e, 1]
+
     size = SEQ_PAD
     gain_two = vec_ref[5:6, :]
     labels = iota((1, total), 1)
@@ -377,43 +551,55 @@
     sums = lax.fori_loop(0, rows // size, step, (zero, zero, zero))
     for i, s in enumerate(sums):
         sums_ref[i : i + 1, :] = s
-
-
-def combine_call(outs, back, cot, hid, sec, probs, spots, ids, weights, small, vec):
-    rows, width = cot.shape
+    unpad_rows(blk_ref, block_ref)
+
+
+def combine_call(both, cot, hid, probs, spots, ids, weights, small, vec):
+    rows, width = hid.shape
+    total = both.shape[0] * both.shape[2]
     shapes = (
-        jax.ShapeDtypeStruct((rows, width), f32),
+        jax.ShapeDtypeStruct(cot.shape, f32),
         jax.ShapeDtypeStruct((rows, width), f32),
         jax.ShapeDtypeStruct((rows, width), bf16),
         jax.ShapeDtypeStruct((rows, width), bf16),
         jax.ShapeDtypeStruct((rows, LANES), bf16),
         jax.ShapeDtypeStruct((8, width), f32),
     )
+    full = lambda a: pl.BlockSpec(a.shape, lambda i: (0,) * len(a.shape))
     return pl.pallas_call(
         combine_kernel,
         out_shape=shapes,
         grid=(1,),
         in_specs=[
-            *[pl.BlockSpec(a.shape, lambda i: (0, 0)) for a in (outs, back, cot, hid, sec, probs, spots, ids)],
+            *[full(a) for a in (both, cot, hid, probs, spots, ids)],
             pl.BlockSpec((width, width), lambda i: (0, 3)),
-            *[pl.BlockSpec(a.shape, lambda i: (0, 0)) for a in (small, vec)],
-        ],
-        out_specs=tuple(pl.BlockSpec(s.shape, lambda i: (0, 0)) for s in shapes),
+            full(small),
+            full(vec),
+        ],
+        out_specs=tuple(full(a) for a in shapes),
+        scratch_shapes=[
+            pltpu.VMEM((total, width), bf16),
+            pltpu.VMEM((total, width), bf16),
+            pltpu.VMEM((rows, width), f32),
+            pltpu.VMEM((rows, width), f32),
+        ],
         compiler_params=params(),
         cost_estimate=pl.CostEstimate(flops=8 * 10**9, bytes_accessed=25 * 10**6, transcendentals=0),
         name="combine",
-    )(outs, back, cot, hid, sec, probs, spots, ids, weights, small, vec)
+    )(both, cot, hid, probs, spots, ids, weights, small, vec)
 
 
 def back_kernel(
-    experts, x_ref, qkv_ref, datt_ref, dhid_ref, dhb_ref, att_ref, sec_ref, dlog_ref, w_ref, vec_ref, sums_ref,
-    in_ref, dense_ref, dqkv_ref, first_ref, dfirst_ref,
+    experts, source_ref, qkv_ref, datt_ref, dhid_ref, dhb_ref, att_ref, sec_ref, dlog_ref, w_ref, vec_ref, sums_ref,
+    input_ref, dense_ref, dqkv_ref, first_ref, dfirst_ref, x_ref,
 ):
     rows, width = x_ref.shape
+    pad_rows(source_ref, x_ref)
     col = 256
     gain_one, shift_one = vec_ref[3:4, :], vec_ref[4:5, :]
     low = iota((1, LANES), 1) < HEAD
-    keys = iota((1, SEQ_PAD), 1) < SEQ
+    keys = iota((SEQ_PAD, 1), 0) < SEQ
+    lower = iota((LANES, 1), 0) < HEAD
     pairs = width // LANES
 
     @pl.loop(0, (rows // SEQ_PAD) * pairs)
@@ -423,19 +609,21 @@
         spans = [pl.ds(pl.multiple_of(o + lane, LANES), LANES) for o in (0, width, 2 * width)]
         q, k, v = (qkv_ref[at, s] for s in spans)
         d_out = datt_ref[at, spans[0]]
+        k_turned = jnp.transpose(k, (1, 0))
+        zero = jnp.zeros_like(q)
         d_q, d_k, d_v = [], [], []
         for side in (low, ~low):
-            q_side = jnp.where(side, q, jnp.zeros_like(q))
-            scores = dot_nt(q_side, k) * head_scale
-            weights = jnp.where(keys, jnp.exp(scores), 0.0)
-            weights = weights * (1.0 / jnp.sum(weights, axis=-1, keepdims=True))
-            d_w = dot_nt(jnp.where(side, d_out, jnp.zeros_like(d_out)), v)
-            d_s = (weights * (d_w - jnp.sum(weights * d_w, axis=-1, keepdims=True)) * head_scale).astype(bf16)
-            d_v.append(dot_tn(weights.astype(bf16), d_out))
-            d_q.append(dot(d_s, k))
-            d_k.append(dot_tn(d_s, q))
-        for s, parts in zip(spans, (d_q, d_k, d_v)):
-            dqkv_ref[at, s] = jnp.where(low, *parts).astype(bf16)
+            grown = jnp.where(keys, jnp.exp(dot_nt(k, jnp.where(side, q, zero))), 0.0)
+            weights = grown * (1.0 / jnp.sum(grown, axis=0, keepdims=True))
+            d_w = dot_nt(v, jnp.where(side, d_out, zero))
+            d_s = (weights * (d_w - jnp.sum(weights * d_w, axis=0, keepdims=True))).astype(bf16)
+            d_v.append(dot(weights.astype(bf16), d_out))
+            d_k.append(dot(d_s, q))
+            d_q.append(dot(k_turned, d_s))
+        d_query = jnp.transpose(jnp.where(lower, *d_q) * head_scale, (1, 0))
+        dqkv_ref[at, spans[0]] = d_query.astype(bf16)
+        dqkv_ref[at, spans[1]] = jnp.where(low, *d_k).astype(bf16)
+        dqkv_ref[at, spans[2]] = jnp.where(low, *d_v).astype(bf16)
 
     @pl.loop(0, rows // ROW_TILE)
     def _(t):
@@ -459,12 +647,13 @@
         at = tile_of(t, ROW_TILE)
         d_first = dfirst_ref[at, :]
         normed, inv_std = normed_rows(x_ref[at, :])
-        in_ref[at, :] = dhid_ref[at, :] + norm_row_grad(d_first * gain_one, normed, inv_std)
+        dfirst_ref[at, :] = dhid_ref[at, :] + norm_row_grad(d_first * gain_one, normed, inv_std)
         add = lambda v: jnp.sum(v, axis=0, keepdims=True)
         return sums[0] + add(d_first * normed), sums[1] + add(d_first)
 
     zero = jnp.zeros((1, width), f32)
     gain_sum, shift_sum = lax.fori_loop(0, rows // ROW_TILE, step, (zero, zero))
+    unpad_rows(dfirst_ref, input_ref)
 
     ones = jnp.ones((8, rows), bf16)
     q_sum = dot(ones, dqkv_ref[:, :width])[0:1, :]
@@ -479,8 +668,8 @@
 
 
 def back_call(experts, x, qkv, datt, dhid, dhb, att, sec, dlog, weights, vec, sums):
-    rows, width = x.shape
-    shapes = (jax.ShapeDtypeStruct((rows, width), f32), jax.ShapeDtypeStruct((width, 4 * width + LANES), bf16))
+    rows, width = dhid.shape
+    shapes = (jax.ShapeDtypeStruct(x.shape, f32), jax.ShapeDtypeStruct((width, 4 * width + LANES), bf16))
     one = lambda a: pl.BlockSpec(a.shape, lambda i: (0, 0))
     return pl.pallas_call(
         functools.partial(back_kernel, experts),
@@ -497,6 +686,7 @@
             pltpu.VMEM((rows, 3 * width), bf16),
             pltpu.VMEM((rows, width), bf16),
             pltpu.VMEM((rows, width), f32),
+            pltpu.VMEM((rows, width), f32),
         ],
         compiler_params=params(),
         cost_estimate=pl.CostEstimate(flops=15 * 10**9, bytes_accessed=35 * 10**6, transcendentals=2 * 10**6),
@@ -514,18 +704,17 @@
 
 
 def send_pairs(spans):
-    fan, low = lax.axis_size("lo"), lax.axis_index("lo")
-    got = [None] * fan
-    for step in list(range(1, fan)) + [0]:
-        got[step] = [shift_along(pick(s, (low + step) % fan, 0), "hi", hop) for hop, s in enumerate(spans, 1)]
+    got = []
+    for step in range(lax.axis_size("lo")):
+        got.append([shift_along(s[step], "hi", hop) for hop, s in enumerate(spans, 1)])
     return got
 
 
 def finish(mine, got):
-    fan, low = lax.axis_size("lo"), lax.axis_index("lo")
+    fan = lax.axis_size("lo")
     parts = [None] * fan
     for step in list(range(1, fan)) + [0]:
-        value = pick(mine, (low + step) % fan, 0).astype(f32)
+        value = mine[step].astype(f32)
         for other in got[step]:
             value = value + other.astype(f32)
         if step:
@@ -584,9 +773,9 @@
     me = high * fan + low
     hidden = up_weight.shape[2]
 
-    def padded(values, fill=0):
+    def padded(values):
         shaped = values.reshape(images, SEQ, values.shape[1])
-        shaped = jnp.pad(shaped, ((0, 0), (0, SEQ_PAD - SEQ), (0, 0)), constant_values=fill)
+        shaped = jnp.pad(shaped, ((0, 0), (0, SEQ_PAD - SEQ), (0, 0)), constant_values=-1)
         return shaped.reshape(images * SEQ_PAD, values.shape[1])
 
     def exchange(value):
@@ -595,53 +784,46 @@
     vectors = (q_bias, v_bias, out_bias, norm1_gain, norm1_bias, norm2_gain, norm2_bias)
     extra = jnp.stack(vectors, axis=1)
     spare = jnp.zeros((extra.shape[0], LANES - experts - len(vectors)), bf16)
-    packed = jnp.concatenate([qkv_weight, out_weight, router_weight, extra, spare], axis=1)
-    part = packed.shape[0] // plane
-    packed = lax.dynamic_slice_in_dim(packed, spot * part, part, 0)
-    weights = lax.all_gather(packed, ("hi", "lo", "expert"), axis=0, tiled=True)
-    small = weights[:, 4 * width :]
-    vec = jnp.pad(small[:, experts : experts + len(vectors)].T.astype(f32), ((0, 1), (0, 0)))
-    bias = jnp.concatenate([vec[0:1], jnp.zeros((1, width), f32), vec[1:2]], axis=1)
+    extra = jnp.concatenate([router_weight, extra, spare], axis=1)
+    owner = (expert_ids % fan) * plane + expert_ids // fan
+    spots = padded(jnp.where(slot_ids >= 0, owner * slots + slot_ids, -1))
+    ids = padded(expert_ids)
+    spots_t = spots.T
+
+    weights, small, cot_sent = gather_call(outer, fan, total, qkv_weight, out_weight, extra, out_grad, spots_t)
+    cot_rows = exchange(cot_sent)
+    qkv, att, hid, sec, probs, send, vec = front_call(experts, total, block_in, weights, small, spots_t)
+    rows_in = exchange(send)
 
     up_one = pick(up_weight, low, 0)
     down_one = pick(down_weight, low, 0)
     up_shift = pick(up_bias, low, 0).astype(f32)[None]
     down_shift = pick(down_bias, low, 0).astype(f32)[None]
 
-    owner = (expert_ids % fan) * plane + expert_ids // fan
-    spots = padded(jnp.where(slot_ids >= 0, owner * slots + slot_ids, -1), -1)
-    ids = padded(expert_ids, -1)
-    spots_t = spots.T
-    x = padded(block_in)
-    cot = padded(out_grad)
-
-    cot_sent, x = lax.optimization_barrier((place_call(spots_t, cot, total), x))
-    cot_rows = exchange(cot_sent)
-
-    qkv, att, hid, sec, probs, send = front_call(experts, total, x, weights, small, bias, vec, spots_t)
-    rows_in = exchange(send)
-
     which = (spot * fan + low).astype(jnp.int32).reshape(1)
     grads, down_sum = gate_call(experts, which, rows_in, cot_rows, small)
     tile = 512 if (hidden // outer) % 512 == 0 else hidden // outer
+    names = [[(high + hop) % outer * fan + (low + step) % fan for step in range(fan)] for hop in range(outer)]
 
     def down_span(hop, x_rows):
-        part = ((high + hop) % outer).astype(jnp.int32).reshape(1)
-        return down_call(x_rows, grads, up_one, up_shift, tile, part, outer).reshape(fan, hidden // members, width)
+        order = list(range(1, fan)) + [0]
+        got = down_call(x_rows, grads, up_one, up_shift, jnp.stack([names[hop][s] for s in order]), members)
+        return [got[order.index(s)] for s in range(fan)]
 
     down_away = [down_span(hop, rows_in) for hop in range(1, outer)]
     down_sent = send_pairs(down_away)
     rows_in, *_ = lax.optimization_barrier((rows_in, *down_away))
-    up_grad, up_sum, outs, d_rows = expert_call(rows_in, grads, up_one, up_shift, down_one, down_shift, tile)
-    up_blocks = up_grad.reshape(outer, fan, width // members, hidden)
-    up_sent = send_pairs([pick(up_blocks, (high + hop) % outer, 0) for hop in range(1, outer)])
-    both = jnp.concatenate([outs.reshape(-1, slots, width), d_rows.reshape(-1, slots, width)], axis=1)
+    flat = jnp.stack([m for row in names for m in row])
+    ups, up_sum, both = expert_call(
+        rows_in, grads, up_one, up_shift, down_one, down_shift, flat, experts, tile
+    )
+    ups = [ups[hop * fan : (hop + 1) * fan] for hop in range(outer)]
+    up_sent = send_pairs(ups[1:])
     both = exchange(both)
-    outs_back, rows_back = both[:, :slots].reshape(total, width), both[:, slots:].reshape(total, width)
-    rows_in, _ = lax.optimization_barrier((rows_in, up_grad))
+    rows_in, _ = lax.optimization_barrier((rows_in, up_sum))
     down_mine = down_span(0, rows_in)
     down_part = finish(down_mine, down_sent)
-    up_part = finish(pick(up_blocks, high, 0), up_sent)
+    up_part = finish(ups[0], up_sent)
 
     summary = jnp.concatenate([up_sum, down_sum], axis=1)
     small_rows = jnp.concatenate([summary] + [shift_along(summary, ("hi", "lo"), s) for s in range(1, members)], axis=0)
@@ -653,17 +835,14 @@
     down_shift_part = lax.dynamic_slice_in_dim(biases[:, hidden:], me * (width // members), width // members, 1)
 
     block_out, d_hid, d_hid_b, d_att, d_log, sums = combine_call(
-        outs_back, rows_back, cot, hid, sec, probs, spots, ids, weights, small, vec
+        both, out_grad, hid, probs, spots, ids, weights, small, vec
     )
-    input_grad, dense = back_call(experts, x, qkv, d_att, d_hid, d_hid_b, att, sec, d_log, weights, vec, sums)
-
-    def unpadded(values):
-        return values.reshape(images, SEQ_PAD, width)[:, :SEQ].reshape(tok_rows, width)
+    input_grad, dense = back_call(experts, block_in, qkv, d_att, d_hid, d_hid_b, att, sec, d_log, weights, vec, sums)
 
     dense = dense_sum(dense)
     at = 4 * width + experts
     return (
-        unpadded(block_out), unpadded(input_grad),
+        block_out, input_grad,
         dense[:, : 3 * width], dense[:, at], dense[:, at + 1], dense[:, 3 * width : 4 * width],
         dense[:, at + 2], dense[:, at + 3], dense[:, at + 4], dense[:, at + 5], dense[:, at + 6],
         dense[:, 4 * width : at],

time: 704 us -> 661 us (0.939)
  waiting for transfers between devices: 339 us -> 286 us
  blocking collectives: 0 us -> 39.6 us
  local copies, waits for them, and re-layouts: 62.3 us -> 26.7 us
  Pallas kernels: 220 us -> 249 us
  between operations: 14.6 us -> 1.15 us
    all_gather x1 -> x0, waiting for transfers between devices: 60 us -> none  [local(): weights = lax.all_gather(packed, ('hi', 'lo', 'expert'), axis=0, tiled=True)]
    all_to_all x0 -> x1, blocking collectives: none -> 39.6 us  [exchange(): lax.all_to_all(value, ('lo', 'expert'), split_axis=0, concat_axis=0, tile...]
    pallas_call x5, Pallas kernels: 116 us -> 154 us  [the longest x1 57.1 us: expert_call(): pl.pallas_call(expert_kernel, out_shape=[jax.ShapeDtypeStruct((width // c...]
    ppermute x12, waiting for transfers between devices: 166 us -> 176 us  [shift_along(): lax.ppermute(value, axis, [(i, (i + step) % size) for i in range(size)])]
    slice x6 -> x0, local copies, waits for them, and re-layouts: 10.1 us -> none  [the longest x1 5.42 us: local(): both[:, slots:].reshape(total, width)]
    all_to_all x3 -> x2, starting transfers between devices: 16.6 us -> 10.7 us  [exchange(): lax.all_to_all(value, ('lo', 'expert'), split_axis=0, concat_axis=0, tile...]
    squeeze x5 -> x3, local copies, waits for them, and re-layouts: 17.5 us -> 13 us  [pick(): return lax.dynamic_index_in_dim(value, index, axis, keepdims=False)]
    all_to_all x3 -> x2, waiting for transfers between devices: 113 us -> 110 us  [exchange(): lax.all_to_all(value, ('lo', 'expert'), split_axis=0, concat_axis=0, tile...]
  transfers between devices with their start and end apart: 19 -> 17, of which waited for: 7 -> 7; matrix products, arithmetic and copies ran while one was open for 9% -> 4% of each run, Pallas kernels for 20% -> 14%
where the time goes in v3:
time: 661 us; the launch traced here: 660 us
  waiting for transfers between devices  286 us (43%)
  Pallas kernels  249 us (38%)
  starting transfers between devices  40.9 us (6%)
  blocking collectives  39.6 us (6%)
  local copies, waits for them, and re-layouts  26.7 us (4%)
  other arithmetic  15.9 us (2%)
    ppermute x12, waiting for transfers between devices, shift_along(): lax.ppermute(value, axis, [(i, (i + step) % size) for i in range(size)])  176 us
    all_to_all x2, waiting for transfers between devices, exchange(): lax.all_to_all(value, ('lo', 'expert'), split_axis=0, concat_axis=0, tile...  110 us
    pallas_call x1, Pallas kernels, expert_call(): pl.pallas_call(expert_kernel, out_shape=[jax.ShapeDtypeStruct((width // c...  57.1 us
    pallas_call x1, Pallas kernels, back_call(): pl.pallas_call(functools.partial(back_kernel, experts), out_shape=shapes,...  48.7 us
    pallas_call x1, Pallas kernels, front_call(): pl.pallas_call(functools.partial(front_kernel, experts), out_shape=shapes...  40 us
    all_to_all x1, blocking collectives, exchange(): lax.all_to_all(value, ('lo', 'expert'), split_axis=0, concat_axis=0, tile...  39.6 us
    pallas_call x2, Pallas kernels, down_call(): pl.pallas_call(lambda p_ref, *refs: down_kernel(steps, *refs), out_shape=...  38.4 us
    pallas_call x1, Pallas kernels, gather_call(): pl.pallas_call(functools.partial(gather_kernel, outer, fan), out_shape=(j...  36.8 us
  transfers between devices with their start and end apart: 17, of which 7 were waited for; matrix products, arithmetic and copies ran while one was open for 4% of the time, Pallas kernels for 14%

profile of v3, /device:TPU:0, one launch (start us, length us, event | category | flops | bytes accessed | tf_op | source)
XLA Modules:
  0.0 660.0 jit_solution(11125703727739097772)
XLA Ops:
  9.4 36.8 %gather.1 = (bf16[768,3072]{1,0:T(8,128)(2,1)}, bf16[768,128]{1,0:T(8,128)(2,1)}, bf16[1792,768]{1,0:T(8,128)(2,1)}) custom-call(bf16[192,2304]{1,0:T(8,128)(2,1)} %qkv_ref.1, bf16[192,768]{1,0:T(8,128)(2,1)} %out_ref.1, bf16[192,128]{1,0:T(8,128)(2,1)} %concatenate.9.small_ref, f32[788,768]{1,0:T(8,128)} %source_ref.4, s32[2,832]{1,0:T(2,128)} %copy.64.spots_ref), custom_call_target="tpu_custom_call" | custom-call | flops 2500000000 | bytes 40000000 | tf_op jit(solution)/shard_map/gather/pallas_call | solution.py:277
  46.3 40.0 %front.1 = (bf16[832,2304]{1,0:T(8,128)(2,1)}, bf16[832,768]{1,0:T(8,128)(2,1)}, f32[832,768]{1,0:T(8,128)}, bf16[832,768]{1,0:T(8,128)(2,1)}, f32[832,128]{1,0:...) custom-call(f32[788,768]{1,0:T(8,128)} %source_ref.5, bf16[768,3072]{1,0:T(8,128)(2,1)} %get-tuple-element.48.w_ref, ...), custom_call_target="tpu_custom_call" | custom-call | flops 14000000000 | bytes 30000000 | tf_op jit(solution)/shard_map/front/pallas_call | solution.py:321
  86.3 39.6 %all_to_all.27 = bf16[16,112,768]{2,1,0:T(8,128)(2,1)} all-to-all(bf16[16,112,768]{2,1,0:T(8,128)(2,1)} %bitcast.64), channel_id=1, replica_groups=mesh['hi'=2,'lo'=2,'expert'=8] {'lo','expert'}, dimensions={0} | all-to-all | bytes 5505024 | tf_op jit(solution)/shard_map/all_to_all | solution.py:782
  125.9 3.9 all-to-all-start.1
  132.2 4.8 dynamic-slice_bitcast_fusion.1.refs_2_.up_ref
  137.0 4.8 dynamic-slice_bitcast_fusion.down_ref
  141.8 26.0 %all-to-all-done.1 = bf16[16,112,768]{2,1,0:T(8,128)(2,1)S(1)} async-done(((bf16[16,112,768]{2,1,0:T(8,128)(2,1)}), bf16[16,112,768]{2,1,0:T(8,128)(2,1)S(1)}, u32[]{:S(2)}, u32[]{:S(2)}) %all-to-all-start.1) | async-done | bytes 2752544 | tf_op jit(solution)/shard_map/all_to_all | solution.py:782
  169.4 6.5 gate.1
  175.8 19.1 %down.2 = (bf16[768,768]{1,0:T(8,128)(2,1)}, bf16[768,768]{1,0:T(8,128)(2,1)}) custom-call(s32[2]{0:T(128)} %pad_add_fusion.1.p_ref, bf16[1792,768]{1,0:T(8,128)(2,1)} %bitcast.57, bf16[1792,768]{1,0:T(8,128)(2,1)} %get-tuple-element.52.refs_1_.grad_ref, bf16[768,3072]{1,0:T(8,128)(2,1)} %dynamic-slice_bitcast_fusion.1.refs_2_.up_ref, ...), custom_call_target="tpu_custom_call" | custom-call | flops 8455716864 | bytes 10223616 | tf_op jit(solution)/shard_map/down/pallas_call | solution.py:412
  195.0 57.1 %expert.1 = (bf16[192,3072]{1,0:T(8,128)(2,1)}, bf16[192,3072]{1,0:T(8,128)(2,1)}, bf16[192,3072]{1,0:T(8,128)(2,1)}, bf16[192,3072]{1,0:T(8,128)(2,1)}, f32[1,3...) custom-call(s32[4]{0:T(128)} %pad_add_fusion.where_ref, bf16[1792,768]{1,0:T(8,128)(2,1)} %bitcast.58, ...), custom_call_target="tpu_custom_call" | custom-call | flops 42278584320 | bytes 25165824 | tf_op jit(solution)/shard_map/expert/pallas_call | solution.py:489
  252.1 6.8 %all-to-all-start.2 = ((bf16[16,2,112,768]{3,2,1,0:T(8,128)(2,1)}), bf16[16,2,112,768]{3,2,1,0:T(8,128)(2,1)}, u32[]{:S(2)}, u32[]{:S(2)}) async-start(bf16[16,2,112,768]{3,2,1,0:T(8,128)(2,1)} %get-tuple-element.56), calls=%async_computation.2 | async-start | bytes 11010048 | tf_op jit(solution)/shard_map/all_to_all | solution.py:782
  260.8 4.0 collective-permute-start.10
  268.1 84.3 %all-to-all-done.2.both_ref = bf16[16,2,112,768]{3,2,1,0:T(8,128)(2,1)} async-done(((bf16[16,2,112,768]{3,2,1,0:T(8,128)(2,1)}), bf16[16,2,112,768]{3,2,1,0:T(8,128)(2,1)}, u32[]{:S(2)}, u32[]{:S(2)}) %all-to-all-start.2) | async-done | bytes 5505056 | tf_op jit(solution)/shard_map/all_to_all | solution.py:782
  352.4 21.6 %combine.1 = (f32[788,768]{1,0:T(8,128)}, f32[832,768]{1,0:T(8,128)}, bf16[832,768]{1,0:T(8,128)(2,1)}, bf16[832,768]{1,0:T(8,128)(2,1)}, bf16[832,128]{1,0:T(8,128)(2,1)}, /*index=5*/f32[8,768]{1,0:T(8,128)}) custom-call(bf16[16,2,112,768]{3,2,1,0:T(8,128)(2,1)} %all-to-all-done.2.both_ref, f32[788,768]{1,0:T(8,128)} %source_ref.4, ...), custom_call_target="tpu_custom_call" | custom-call | flops 8000000000 | bytes 25000000 | tf_op jit(solution)/shard_map/combine/pallas_call | solution.py:569
  374.0 48.7 %back.1 = (f32[788,768]{1,0:T(8,128)}, bf16[768,3200]{1,0:T(8,128)(2,1)}) custom-call(f32[788,768]{1,0:T(8,128)} %source_ref.5, bf16[832,2304]{1,0:T(8,128)(2,1)} %get-tuple-element.61.qkv_ref, bf16[832,768]{1,0:T(8,128)(2,1)} %get-tuple-element.62.datt_ref, f32[832,768]{1,0:T(8,128)} %get-tuple-element.63.dhid_ref, ...), custom_call_target="tpu_custom_call" | custom-call | flops 15000000512 | bytes 35000000 | tf_op jit(solution)/shard_map/back/pallas_call | solution.py:674
  422.8 3.3 dynamic-slice_bitcast_fusion.2
  426.1 19.3 %down.3 = (bf16[768,768]{1,0:T(8,128)(2,1)}, bf16[768,768]{1,0:T(8,128)(2,1)}) custom-call(s32[2]{0:T(128)} %pad_add_fusion.2.p_ref, bf16[1792,768]{1,0:T(8,128)(2,1)} %bitcast.59, bf16[1792,768]{1,0:T(8,128)(2,1)} %get-tuple-element.52.refs_1_.grad_ref, bf16[768,3072]{1,0:T(8,128)(2,1)} %dynamic-slice_bitcast_fusion.1.refs_2_.up_ref, ...), custom_call_target="tpu_custom_call" | custom-call | flops 8455716864 | bytes 10223616 | tf_op jit(solution)/shard_map/down/pallas_call | solution.py:412
  445.4 15.7 %collective-permute-start.13 = (bf16[768,768]{1,0:T(8,128)(2,1)}, bf16[768,768]{1,0:T(8,128)(2,1)S(1)}, u32[]{:S(2)}, u32[]{:S(2)}) collective-permute-start(bf16[768,768]{1,0:T(8,128)(2,1)} %get-tuple-element.54), channel_id=1, source_target_pairs={{0,16},{16,0},{1,17},{17,1},{2,18},{18,2},{3,19},{19,3},{4,20},{20... | collective-permute-start | bytes 3538952 | tf_op jit(solution)/shard_map/ppermute | solution.py:703
  461.2 2.8 collective-permute-start.6
  469.8 93.8 %collective-permute-done.13 = bf16[768,768]{1,0:T(8,128)(2,1)S(1)} collective-permute-done((bf16[768,768]{1,0:T(8,128)(2,1)}, bf16[768,768]{1,0:T(8,128)(2,1)S(1)}, u32[]{:S(2)}, u32[]{:S(2)}) %collective-permute-start.13) | collective-permute-done | bytes 1179680 | tf_op jit(solution)/shard_map/ppermute | solution.py:703
  564.0 50.2 %collective-permute-done.6 = bf16[192,3072]{1,0:T(8,128)(2,1)S(1)} collective-permute-done((bf16[192,3072]{1,0:T(8,128)(2,1)}, bf16[192,3072]{1,0:T(8,128)(2,1)S(1)}, u32[]{:S(2)}, u32[]{:S(2)}) %collective-permute-start.6) | collective-permute-done | bytes 1179680 | tf_op jit(solution)/shard_map/ppermute | solution.py:703
  615.4 24.0 %collective-permute-done.14 = bf16[768,768]{1,0:T(8,128)(2,1)S(1)} collective-permute-done((bf16[768,768]{1,0:T(8,128)(2,1)S(1)}, bf16[768,768]{1,0:T(8,128)(2,1)S(1)}, u32[]{:S(2)}, u32[]{:S(2)}) %collective-permute-start.14) | collective-permute-done | bytes 1179680 | tf_op jit(solution)/shard_map/ppermute | solution.py:703
  643.5 3.0 collective-permute-start.5
  651.4 5.6 collective-permute-done.4
  (95 shorter events, 36.8 us)
Async XLA Ops:
  1.7 44.6 %copy-start.1 = (s32[4,208,2]{2,1,0:T(8,128)}, s32[4,208,2]{2,1,0:T(8,128)S(1)}, u32[]{:S(2)}) copy-start(s32[4,208,2]{2,1,0:T(8,128)S(1)} %pad.7) | copy-start | bytes 19972
  125.9 41.9 %all-to-all-start.1 = ((bf16[16,112,768]{2,1,0:T(8,128)(2,1)}), bf16[16,112,768]{2,1,0:T(8,128)(2,1)S(1)}, u32[]{:S(2)}, u32[]{:S(2)}) async-start(bf16[16,112,768]{2,1,0:T(8,128)(2,1)} %bitcast.63), calls=%async_computation.1 | async-start | bytes 5505024 | tf_op jit(solution)/shard_map/all_to_all | solution.py:782
  252.1 8.6 %copy-start.8 = (f32[1,3072]{1,0:T(1,128)S(1)}, f32[1,3072]{1,0:T(1,128)}, u32[]{:S(2)}) copy-start(f32[1,3072]{1,0:T(1,128)} %get-tuple-element.75) | copy-start | bytes 36868
  252.1 8.6 %copy-start.9 = (f32[1,768]{1,0:T(1,128)S(1)}, f32[1,768]{1,0:T(1,128)}, u32[]{:S(2)}) copy-start(f32[1,768]{1,0:T(1,128)} %get-tuple-element.76) | copy-start | bytes 9220
  252.1 100.3 %all-to-all-start.2 = ((bf16[16,2,112,768]{3,2,1,0:T(8,128)(2,1)}), bf16[16,2,112,768]{3,2,1,0:T(8,128)(2,1)}, u32[]{:S(2)}, u32[]{:S(2)}) async-start(bf16[16,2,112,768]{3,2,1,0:T(8,128)(2,1)} %get-tuple-element.56), calls=%async_computation.2 | async-start | bytes 11010048 | tf_op jit(solution)/shard_map/all_to_all | solution.py:782
  260.8 184.6 %collective-permute-start.10 = (f32[1,3840]{1,0:T(1,128)S(1)}, f32[1,3840]{1,0:T(1,128)S(1)}, u32[]{:S(2)}, u32[]{:S(2)}) collective-permute-start(f32[1,3840]{1,0:T(1,128)S(1)} %constant_dynamic-update-slice_fusion), channel_id=1, source_target_pairs={{0,16},{8,24},{16,0},{24,8},{1,17},{9,25},{17,1},{25,9},{2,18},{10... | collective-permute-start | bytes 46088 | tf_op jit(solution)/shard_map/ppermute | solution.py:703
  264.8 196.4 %collective-permute-start.11 = (f32[1,3840]{1,0:T(1,128)S(1)}, f32[1,3840]{1,0:T(1,128)S(1)}, u32[]{:S(2)}, u32[]{:S(2)}) collective-permute-start(f32[1,3840]{1,0:T(1,128)S(1)} %constant_dynamic-update-slice_fusion), channel_id=1, source_target_pairs={{0,24},{8,0},{16,8},{24,16},{1,25},{9,1},{17,9},{25,17},{2,26},{10... | collective-permute-start | bytes 46088 | tf_op jit(solution)/shard_map/ppermute | solution.py:703
  266.1 195.1 %collective-permute-start.9 = (f32[1,3840]{1,0:T(1,128)S(1)}, f32[1,3840]{1,0:T(1,128)S(1)}, u32[]{:S(2)}, u32[]{:S(2)}) collective-permute-start(f32[1,3840]{1,0:T(1,128)S(1)} %constant_dynamic-update-slice_fusion), channel_id=1, source_target_pairs={{0,8},{8,16},{16,24},{24,0},{1,9},{9,17},{17,25},{25,1},{2,10},{10... | collective-permute-start | bytes 46088 | tf_op jit(solution)/shard_map/ppermute | solution.py:703
  266.8 198.1 %collective-permute-start.7 = (bf16[192,3072]{1,0:T(8,128)(2,1)}, bf16[192,3072]{1,0:T(8,128)(2,1)}, u32[]{:S(2)}, u32[]{:S(2)}) collective-permute-start(bf16[192,3072]{1,0:T(8,128)(2,1)} %get-tuple-element.74), channel_id=1, source_target_pairs={{0,16},{16,0},{1,17},{17,1},{2,18},{18,2},{3,19},{19,3},{4,20},{20... | collective-permute-start | bytes 3538952 | tf_op jit(solution)/shard_map/ppermute | solution.py:703
  426.1 38.8 %copy-start.2 = (bf16[192,3072]{1,0:T(8,128)(2,1)S(1)}, bf16[192,3072]{1,0:T(8,128)(2,1)}, u32[]{:S(2)}) copy-start(bf16[192,3072]{1,0:T(8,128)(2,1)} %get-tuple-element.73) | copy-start | bytes 3538948
  426.1 40.6 %collective-permute-start = (bf16[4,4,24,3200]{3,2,1,0:T(8,128)(2,1)}, bf16[4,4,24,3200]{3,2,1,0:T(8,128)(2,1)S(1)}, u32[]{:S(2)}, u32[]{:S(2)}) collective-permute-start(bf16[4,4,24,3200]{3,2,1,0:T(8,128)(2,1)} %dynamic-slice_bitcast_fusion.2), channel_id=1, source_target_pairs={{0,1},{1,0},{2,3},{3,2},{4,5},{5,4},{6,7},{7,6},{8,9},{9,8},{10,11... | collective-permute-start | bytes 7372808 | tf_op jit(solution)/shard_map/ppermute | solution.py:748
  445.4 118.2 %collective-permute-start.13 = (bf16[768,768]{1,0:T(8,128)(2,1)}, bf16[768,768]{1,0:T(8,128)(2,1)S(1)}, u32[]{:S(2)}, u32[]{:S(2)}) collective-permute-start(bf16[768,768]{1,0:T(8,128)(2,1)} %get-tuple-element.54), channel_id=1, source_target_pairs={{0,16},{16,0},{1,17},{17,1},{2,18},{18,2},{3,19},{19,3},{4,20},{20... | collective-permute-start | bytes 3538952 | tf_op jit(solution)/shard_map/ppermute | solution.py:703
  461.1 154.3 %collective-permute-start.12 = (bf16[768,768]{1,0:T(8,128)(2,1)}, bf16[768,768]{1,0:T(8,128)(2,1)S(1)}, u32[]{:S(2)}, u32[]{:S(2)}) collective-permute-start(bf16[768,768]{1,0:T(8,128)(2,1)} %get-tuple-element.53), channel_id=1, source_target_pairs={{0,16},{16,0},{1,17},{17,1},{2,18},{18,2},{3,19},{19,3},{4,20},{20... | collective-permute-start | bytes 3538952 | tf_op jit(solution)/shard_map/ppermute | solution.py:703
  461.2 153.0 %collective-permute-start.6 = (bf16[192,3072]{1,0:T(8,128)(2,1)}, bf16[192,3072]{1,0:T(8,128)(2,1)S(1)}, u32[]{:S(2)}, u32[]{:S(2)}) collective-permute-start(bf16[192,3072]{1,0:T(8,128)(2,1)} %get-tuple-element.72), channel_id=1, source_target_pairs={{0,16},{16,0},{1,17},{17,1},{2,18},{18,2},{3,19},{19,3},{4,20},{20... | collective-permute-start | bytes 3538952 | tf_op jit(solution)/shard_map/ppermute | solution.py:703
  466.6 147.7 %collective-permute-start.8 = (bf16[192,3072]{1,0:T(8,128)(2,1)S(1)}, bf16[192,3072]{1,0:T(8,128)(2,1)S(1)}, u32[]{:S(2)}, u32[]{:S(2)}) collective-permute-start(bf16[192,3072]{1,0:T(8,128)(2,1)S(1)} %add_convert_fusion.1), channel_id=1, source_target_pairs={{0,8},{8,0},{1,9},{9,1},{2,10},{10,2},{3,11},{11,3},{4,12},{12,4},... | collective-permute-start | bytes 3538952 | tf_op jit(solution)/shard_map/ppermute | solution.py:703
  468.9 94.8 %copy-start.3 = (bf16[768,768]{1,0:T(8,128)(2,1)S(1)}, bf16[768,768]{1,0:T(8,128)(2,1)}, u32[]{:S(2)}) copy-start(bf16[768,768]{1,0:T(8,128)(2,1)} %get-tuple-element.79) | copy-start | bytes 3538948
  469.0 145.2 %copy-start.4 = (bf16[192,3072]{1,0:T(8,128)(2,1)S(1)}, bf16[192,3072]{1,0:T(8,128)(2,1)}, u32[]{:S(2)}) copy-start(bf16[192,3072]{1,0:T(8,128)(2,1)} %get-tuple-element.71) | copy-start | bytes 3538948
  469.0 146.0 %collective-permute-start.1 = (bf16[4,2,24,3200]{3,2,1,0:T(8,128)(2,1)S(1)}, bf16[4,2,24,3200]{3,2,1,0:T(8,128)(2,1)S(1)}, u32[]{:S(2)}, u32[]{:S(2)}) collective-permute-start(bf16[4,2,24,3200]{3,2,1,0:T(8,128)(2,1)S(1)} %fusion.4), channel_id=1, source_target_pairs={{0,2},{1,3},{2,0},{3,1},{4,6},{5,7},{6,4},{7,5},{8,10},{9,11},{10,... | collective-permute-start | bytes 3686408 | tf_op jit(solution)/shard_map/ppermute | solution.py:748
  564.0 75.5 %collective-permute-start.14 = (bf16[768,768]{1,0:T(8,128)(2,1)S(1)}, bf16[768,768]{1,0:T(8,128)(2,1)S(1)}, u32[]{:S(2)}, u32[]{:S(2)}) collective-permute-start(bf16[768,768]{1,0:T(8,128)(2,1)S(1)} %add_convert_fusion), channel_id=1, source_target_pairs={{0,8},{8,0},{1,9},{9,1},{2,10},{10,2},{3,11},{11,3},{4,12},{12,4},... | collective-permute-start | bytes 3538952 | tf_op jit(solution)/shard_map/ppermute | solution.py:703
  615.0 24.4 %copy-start.5 = (bf16[768,768]{1,0:T(8,128)(2,1)S(1)}, bf16[768,768]{1,0:T(8,128)(2,1)}, u32[]{:S(2)}) copy-start(bf16[768,768]{1,0:T(8,128)(2,1)} %get-tuple-element.78) | copy-start | bytes 3538948
  615.3 27.0 %collective-permute-start.2 = (bf16[4,1,24,3200]{3,2,1,0:T(8,128)(2,1)S(1)}, bf16[4,1,24,3200]{3,2,1,0:T(8,128)(2,1)S(1)}, u32[]{:S(2)}, u32[]{:S(2)}) collective-permute-start(bf16[4,1,24,3200]{3,2,1,0:T(8,128)(2,1)S(1)} %dynamic-slice_convert_fusion.1), channel_id=1, source_target_pairs={{0,4},{1,5},{2,6},{3,7},{4,0},{5,1},{6,2},{7,3},{8,12},{9,13},{10,... | collective-permute-start | bytes 1843208 | tf_op jit(solution)/shard_map/ppermute | solution.py:748
  642.6 8.8 %collective-permute-start.3 = (bf16[24,3200]{1,0:T(8,128)(2,1)S(1)}, bf16[24,3200]{1,0:T(8,128)(2,1)S(1)}, u32[]{:S(2)}, u32[]{:S(2)}) collective-permute-start(bf16[24,3200]{1,0:T(8,128)(2,1)S(1)} %get-tuple-element.141), channel_id=1, source_target_pairs={{0,8},{8,16},{16,24},{24,0},{1,9},{9,17},{17,25},{25,1},{2,10},{10... | collective-permute-start | bytes 460808 | tf_op jit(solution)/shard_map/ppermute | solution.py:703
  642.6 14.4 %collective-permute-start.4 = (bf16[24,3200]{1,0:T(8,128)(2,1)S(1)}, bf16[24,3200]{1,0:T(8,128)(2,1)S(1)}, u32[]{:S(2)}, u32[]{:S(2)}) collective-permute-start(bf16[24,3200]{1,0:T(8,128)(2,1)S(1)} %get-tuple-element.143), channel_id=1, source_target_pairs={{0,16},{8,24},{16,0},{24,8},{1,17},{9,25},{17,1},{25,9},{2,18},{10... | collective-permute-start | bytes 460808 | tf_op jit(solution)/shard_map/ppermute | solution.py:703
  643.5 13.6 %collective-permute-start.5 = (bf16[24,3200]{1,0:T(8,128)(2,1)S(1)}, bf16[24,3200]{1,0:T(8,128)(2,1)S(1)}, u32[]{:S(2)}, u32[]{:S(2)}) collective-permute-start(bf16[24,3200]{1,0:T(8,128)(2,1)S(1)} %get-tuple-element.142), channel_id=1, source_target_pairs={{0,24},{8,0},{16,8},{24,16},{1,25},{9,1},{17,9},{25,17},{2,26},{10... | collective-permute-start | bytes 460808 | tf_op jit(solution)/shard_map/ppermute | solution.py:703
  (4 other events, 19.2 us)
